TPU v7x, 16 devices: a 4x2x1 block of a 4x4x8 slice. The times are simulated.
16 devices in a mesh: dp: 2 (over y, z), sp: 8 (over x, core).
Axes of the slice: x: 4, y: 2, z: 1, core: 2. Of those that a mesh axis runs over, the one named last changes fastest.
The devices are a block of a 4x4x8 slice.
Arguments:
- signal: bfloat16 [131072, 1024], P(('dp', 'sp')), parts along dimension 0
- w_first: bfloat16 [11, 2048, 2, 32, 32], P(None, 'sp')
- w_second: bfloat16 [11, 2048, 2, 32, 32], P(None, 'sp')
Outputs:
- output: bfloat16 [131072, 1024], P(('dp', 'sp')), parts along dimension 0
There are 2 independent parts. A program takes and returns all parts, laid end to end along the dimension named above; an argument that names none is the same for every part.
All inputs are finite; a program needn't handle non-finite values.
Results may differ from a plain program's by a relative error of at most 0.02.
Values are sent between devices in bfloat16 or wider.
A program may use at most 768 MiB of HBM per device.

v0:
```python
import functools

import jax
import jax.numpy as jnp
from jax import lax
from jax.experimental import pallas as pl
from jax.experimental.pallas import tpu as pltpu
from jax.sharding import PartitionSpec as P


CORES = 2
CHIPS = 4
LANES = 128
BF16 = jnp.bfloat16
F32 = jnp.float32


def mxu(lhs, rhs):
    return jnp.dot(lhs, rhs, preferred_element_type=F32)


def cost(us):
    return pl.CostEstimate(flops=int(us * 1e8), bytes_accessed=int(us * 1e5), transcendentals=0)


def params():
    return pltpu.CompilerParams(dimension_semantics=("arbitrary",), vmem_limit_bytes=60 * 2**20)


def turned(refs, i, sel):
    wide = jnp.concatenate([ref[0, slot, i] for ref in refs for slot in range(2)], axis=0)
    return lax.dot_general(wide, sel, (((0,), (0,)), ((), ())), preferred_element_type=F32)


def pack_kernel(a_ref, b_ref, out_ref, tmp):
    blk, blocks = a_ref.shape[2], a_ref.shape[4]
    row = lax.broadcasted_iota(jnp.int32, (LANES, LANES), 0)
    col = lax.broadcasted_iota(jnp.int32, (LANES, LANES), 1)
    sel = (row == col).astype(F32).astype(BF16)

    @pl.loop(0, blk // 4)
    def _(it):
        for u in range(4):
            i = it * 4 + u
            tmp[pl.ds(i, blocks, stride=blk), :] = turned((a_ref, b_ref), i, sel)

    out_ref[...] = tmp[...].astype(BF16)


def pack_pair(turned_w, hi, lo):
    _, two, blk, _, blocks = turned_w.shape
    spec = lambda stage: pl.BlockSpec((1, two, blk, blk, blocks), lambda i: (stage, 0, 0, 0, 0))
    return pl.pallas_call(
        pack_kernel,
        grid=(1,),
        in_specs=[spec(hi), spec(lo)],
        out_specs=pl.BlockSpec((blocks * blk, LANES), lambda i: (0, 0)),
        out_shape=jax.ShapeDtypeStruct((blocks * blk, LANES), BF16),
        scratch_shapes=[pltpu.VMEM((blocks * blk, LANES), F32)],
        compiler_params=params(),
        cost_estimate=cost(5),
        name="pack_pair",
    )(turned_w, turned_w)


def expand_kernel(d0, d1, d2, d3, sel_hi, sel_lo, out_hi, out_lo):
    for rel, src in enumerate((d0, d1, d2, d3)):
        val = src[...]
        out_hi[rel] = mxu(val, sel_hi[rel]).astype(BF16)
        out_lo[rel] = mxu(val, sel_lo[rel]).astype(BF16)


def expand_pair(packed, odd, blk):
    rows = packed[0].shape[0]
    tile = rows // 8
    shape = (CHIPS, LANES, LANES)
    rel, k, n = (lax.broadcasted_iota(jnp.int32, shape, axis) for axis in range(3))
    same = k % blk == n % blk
    kg, ng = k // blk, n // blk
    mate_lo = jnp.where(odd == 1, 3 - rel, rel ^ 1)
    sel_hi = (same & (((kg == 0) & (ng == rel)) | ((kg == 1) & (ng == (rel ^ 2))))).astype(BF16)
    sel_lo = (same & (((kg == 2) & (ng == rel)) | ((kg == 3) & (ng == mate_lo)))).astype(BF16)
    out = jax.ShapeDtypeStruct((CHIPS, rows, LANES), BF16)
    sel_spec = pl.BlockSpec(shape, lambda i: (0, 0, 0))
    out_spec = pl.BlockSpec((CHIPS, tile, LANES), lambda i: (0, i, 0))
    return pl.pallas_call(
        expand_kernel,
        grid=(rows // tile,),
        in_specs=[pl.BlockSpec((tile, LANES), lambda i: (i, 0))] * 4 + [sel_spec] * 2,
        out_specs=[out_spec] * 2,
        out_shape=[out] * 2,
        compiler_params=params(),
        cost_estimate=cost(5),
        name="expand_pair",
    )(*packed, sel_hi, sel_lo)


def spread_kernel(first_map, a_ref, b_ref, out_ref, tmp_a, tmp_b):
    step = pl.program_id(0)
    blk, blocks = a_ref.shape[2], a_ref.shape[4]
    lone = step == 4
    lo = jnp.where(lone, 0, 6 - 2 * step if first_map else 2 * step)
    row = lax.broadcasted_iota(jnp.int32, (LANES, 4 * LANES), 0)
    col = lax.broadcasted_iota(jnp.int32, (LANES, 4 * LANES), 1)
    fits = row % blk == col % blk
    sel = (fits & (row // blk == col // LANES)).astype(F32).astype(BF16)
    block = lax.broadcasted_iota(jnp.int32, (blocks, LANES), 0)
    group = lax.broadcasted_iota(jnp.int32, (blocks, LANES), 1) // blk
    own = jnp.where(lone, 2 * (block & 1), (block >> lo) & 3)
    first, second = (2, 1) if first_map else (1, 2)
    mates = [jnp.where(lone, own + 1, own ^ first), jnp.where(lone, own + 1, own ^ second)]

    @pl.loop(0, blk // 8)
    def _(it):
        wides = [turned((a_ref, b_ref), it * 8 + u, sel) for u in range(8)]
        for u, wide in enumerate(wides):
            for half, (mate, tmp) in enumerate(zip(mates, (tmp_a, tmp_b))):
                both = wide[:, 2 * half * LANES : 2 * (half + 1) * LANES]
                val = jnp.where(group == own, both[:, :LANES], jnp.where(group == mate, both[:, LANES:], 0.0))
                tmp[pl.ds(it * 8 + u, blocks, stride=blk), :] = val

    out_ref[0] = tmp_a[...].astype(BF16)
    out_ref[1] = tmp_b[...].astype(BF16)


def spread(turned_w, first_map):
    stages, two, blk, _, blocks = turned_w.shape
    if first_map:
        a_at = lambda i: jnp.where(i < 4, 3 + 2 * i, 2)
        b_at = lambda i: jnp.where(i < 4, 4 + 2 * i, 2)
    else:
        a_at = lambda i: 2 * i
        b_at = lambda i: jnp.minimum(2 * i + 1, stages - 3)
    spec = lambda at: pl.BlockSpec((1, two, blk, blk, blocks), lambda i: (at(i), 0, 0, 0, 0))
    rows = blocks * blk
    return pl.pallas_call(
        functools.partial(spread_kernel, first_map),
        grid=(5,),
        in_specs=[spec(a_at), spec(b_at)],
        out_specs=pl.BlockSpec((2, rows, LANES), lambda i: (i, 0, 0)),
        out_shape=jax.ShapeDtypeStruct((10, rows, LANES), BF16),
        scratch_shapes=[pltpu.VMEM((rows, LANES), F32)] * 2,
        compiler_params=params(),
        cost_estimate=cost(25),
        name="spread",
    )(turned_w, turned_w)


def two_stages(quads):
    mids = [mxu(lhs_a, rows).astype(BF16) for lhs_a, _, rows in quads]
    return [mxu(lhs_b, mid).astype(BF16) for (_, lhs_b, _), mid in zip(quads, mids)]


def chip_kernel(blk, x0, x1, x2, x3, ea, eb, o0, o1, o2, o3):
    spans = [slice(b * blk, (b + 1) * blk) for b in range(x0.shape[0] // blk)]
    quads = []
    for rows in spans:
        z = jnp.concatenate([x[rows, :] for x in (x0, x1, x2, x3)], axis=0)
        a_mat = jnp.concatenate([ea[r, rows, :] for r in range(CHIPS)], axis=0)
        b_mat = jnp.concatenate([eb[r, rows, :] for r in range(CHIPS)], axis=0)
        quads.append((a_mat, b_mat, z))
    for rows, y in zip(spans, two_stages(quads)):
        for r, o in enumerate((o0, o1, o2, o3)):
            o[rows, :] = y[r * blk : (r + 1) * blk]


def chip_stages(parts, ea, eb, blk):
    rows, width = parts[0].shape
    tile = rows // 8
    spec = pl.BlockSpec((tile, width), lambda i: (i, 0))
    wspec = pl.BlockSpec((CHIPS, tile, LANES), lambda i: (0, i, 0))
    return pl.pallas_call(
        functools.partial(chip_kernel, blk),
        grid=(rows // tile,),
        in_specs=[spec] * 4 + [wspec] * 2,
        out_specs=[spec] * 4,
        out_shape=[jax.ShapeDtypeStruct((rows, width), BF16)] * 4,
        compiler_params=params(),
        cost_estimate=cost(8),
        name="chip_stages",
    )(*parts, ea, eb)


def gelu(x):
    x = x.astype(F32)
    return (0.5 * x * (1.0 + lax.erf(x * 0.7071067811865476))).astype(BF16)


def middle_kernel(blk, chip_ref, x0, x1, x2, x3, p0, p1, p2, p3, core_w, first_w, second_w, buf):
    step = pl.program_id(0)
    group_rows = x0.shape[0]
    unroll = 8

    @pl.when(step == 0)
    def _():
        for rel, (own, mate) in enumerate(zip((x0, x1, x2, x3), (p0, p1, p2, p3))):
            base = ((chip_ref[0] + rel) % CHIPS) * group_rows

            @pl.loop(0, group_rows // (2 * blk * unroll))
            def _(it):
                outs = []
                for u in range(unroll):
                    off = pl.multiple_of((it * unroll + u) * 2 * blk, 2 * blk)
                    nxt = pl.multiple_of(off + blk, blk)
                    dst = pl.multiple_of(base + off, 2 * blk)
                    z = jnp.concatenate(
                        [own[pl.ds(off, blk), :], mate[pl.ds(off, blk), :], own[pl.ds(nxt, blk), :], mate[pl.ds(nxt, blk), :]], axis=0
                    )
                    outs.append((dst, mxu(core_w[0, pl.ds(dst, 2 * blk), :], z).astype(BF16)))
                for dst, val in outs:
                    buf[pl.ds(dst, 2 * blk), :] = val

    def quad_step(wts, lo):
        @pl.loop(0, buf.shape[0] // (4 * blk * unroll))
        def _(it):
            places, quads = [], []
            for u in range(unroll):
                quad = it * unroll + u
                first = ((quad >> lo) << (lo + 2)) | (quad & ((1 << lo) - 1))
                offs = [pl.multiple_of((first + (pos << lo)) * blk, blk) for pos in range(4)]
                z = jnp.concatenate([buf[pl.ds(o, blk), :] for o in offs], axis=0)
                a_mat = jnp.concatenate([wts[0, pl.ds(o, blk), :] for o in offs], axis=0)
                b_mat = jnp.concatenate([wts[1, pl.ds(o, blk), :] for o in offs], axis=0)
                places.append(offs)
                quads.append((a_mat, b_mat, z))
            for offs, y in zip(places, two_stages(quads)):
                for pos, o in enumerate(offs):
                    buf[pl.ds(o, blk), :] = y[pos * blk : (pos + 1) * blk]

    @pl.when((step > 0) & (step <= 4))
    def _():
        quad_step(first_w, 8 - 2 * step)

    @pl.when(step == 4)
    def _():
        rows = 64

        @pl.loop(0, buf.shape[0] // rows)
        def _(it):
            at = pl.ds(pl.multiple_of(it * rows, rows), rows)
            buf[at, :] = gelu(buf[at, :])

    @pl.when(step > 4)
    def _():
        quad_step(second_w, 2 * step - 10)


def middle(chip, parts, mates, first_w, second_w, blk):
    rows, width = parts[0].shape
    total = rows * CHIPS
    once = pl.Buffered(1)
    full = pl.BlockSpec((rows, width), lambda i, c: (0, 0), pipeline_mode=once)
    return pl.pallas_call(
        functools.partial(middle_kernel, blk),
        grid_spec=pltpu.PrefetchScalarGridSpec(
            num_scalar_prefetch=1,
            grid=(9,),
            in_specs=[full] * 8
            + [
                pl.BlockSpec((1, total, LANES), lambda i, c: (8, 0, 0), pipeline_mode=once),
                pl.BlockSpec((2, total, LANES), lambda i, c: (jnp.clip(i - 1, 0, 3), 0, 0)),
                pl.BlockSpec((2, total, LANES), lambda i, c: (jnp.clip(i - 5, 0, 3), 0, 0)),
            ],
            out_specs=pl.BlockSpec((total, width), lambda i, c: (0, 0), pipeline_mode=once),
        ),
        out_shape=jax.ShapeDtypeStruct((total, width), BF16),
        compiler_params=params(),
        cost_estimate=cost(35),
        name="middle",
    )(chip, *parts, *mates, first_w, first_w, second_w)


def core_kernel(blk, chip_ref, *refs):
    own, mate, wts, outs = refs[0:4], refs[4:8], refs[8:12], refs[12:16]
    for rel in range(CHIPS):
        for pair in range(own[rel].shape[0] // (2 * blk)):
            at, nxt = pair * 2 * blk, pair * 2 * blk + blk
            z = jnp.concatenate(
                [own[rel][at:nxt, :], mate[rel][at:nxt, :], own[rel][nxt : nxt + blk, :], mate[rel][nxt : nxt + blk, :]], axis=0
            )
            outs[rel][at : at + 2 * blk, :] = mxu(wts[rel][0, at : at + 2 * blk, :], z).astype(BF16)


def core_stage(chip, own, mate, core_w, blk):
    total, width = own.shape
    rows = total // CHIPS
    tile = rows // 8

    def rel_spec(rel):
        return pl.BlockSpec((tile, width), lambda i, c: (((c[0] + rel) % CHIPS) * 8 + i, 0))

    def w_spec(rel):
        return pl.BlockSpec((1, tile, LANES), lambda i, c: (8, ((c[0] + rel) % CHIPS) * 8 + i, 0))

    data = [rel_spec(r) for r in range(CHIPS)]
    return pl.pallas_call(
        functools.partial(core_kernel, blk),
        grid_spec=pltpu.PrefetchScalarGridSpec(
            num_scalar_prefetch=1,
            grid=(8,),
            in_specs=data + data + [w_spec(r) for r in range(CHIPS)],
            out_specs=[pl.BlockSpec((tile, width), lambda i, c: (i, 0))] * 4,
        ),
        out_shape=[jax.ShapeDtypeStruct((rows, width), BF16)] * 4,
        compiler_params=params(),
        cost_estimate=cost(8),
        name="core_stage",
    )(chip, *[own] * 4, *[mate] * 4, *[core_w] * 4)


def solution(mesh):
    members = mesh.shape["sp"]

    def to_chip(value, shift):
        pairs = [(d, (d + shift * CORES) % members) for d in range(members)]
        return lax.ppermute(value, "sp", pairs)

    def to_core(value):
        return lax.ppermute(value, "sp", [(d, d ^ 1) for d in range(members)])

    def swap(parts):
        got = [parts[0]] + [None] * (CHIPS - 1)
        for shift in (2, 1, 3):
            got[-shift % CHIPS] = to_chip(parts[shift], shift)
        return got

    def device_program(signal, w_first, w_second):
        stages, _, _, blk, _ = w_first.shape
        rows, channels = signal.shape
        group = rows // CHIPS
        width = 256
        chunks = channels // width
        chip = lax.axis_index("sp") // CORES
        odd = chip % 2
        chip_arr = jnp.full((1,), chip, jnp.int32)

        def quarter(array, rel, col, wide):
            return lax.dynamic_slice(array, (((chip + rel) % CHIPS) * group, col), (group, wide))

        def chip_weights(weights, hi, lo):
            packed = pack_pair(weights, hi, lo)
            got = swap([quarter(packed, r, 0, LANES) for r in range(CHIPS)])
            return expand_pair(got, odd, blk)

        w_first, w_second = (jnp.transpose(w, (0, 2, 3, 4, 1)) for w in (w_first, w_second))
        hi_first, lo_first = chip_weights(w_first, 0, 1)
        mid_first = spread(w_first, True)
        mid_second = spread(w_second, False)
        hi_second, lo_second = chip_weights(w_second, stages - 1, stages - 2)

        result = jnp.zeros((rows, channels), BF16)
        for c in range(chunks):
            parts = [quarter(signal, r, c * width, width) for r in range(CHIPS)]
            signal, parts = lax.optimization_barrier((signal, parts))
            parts = swap(parts)
            parts = chip_stages(parts, hi_first, lo_first, blk)
            parts = swap(parts)
            mates = [to_core(p) for p in parts]
            act = middle(chip_arr, parts, mates, mid_first, mid_second, blk)
            twin = to_core(act)
            parts = core_stage(chip_arr, act, twin, mid_second, blk)
            parts = swap(parts)
            parts = chip_stages(parts, lo_second, hi_second, blk)
            parts = swap(parts)
            for r in range(CHIPS):
                at = (((chip + r) % CHIPS) * group, c * width)
                result = lax.dynamic_update_slice(result, parts[r], at)
        return result

    row_spec = P(("dp", "sp"), None)
    weight_spec = P(None, "sp", None, None, None)
    return jax.shard_map(device_program, mesh=mesh, in_specs=(row_spec, weight_spec, weight_spec), out_specs=row_spec, check_vma=False)
```

profile of v0, /device:TPU:112, one launch (start us, length us, event | category | flops | bytes accessed | tf_op | source)
XLA Modules:
  0.0 1149.2 jit_solution(18370605863422618211)
XLA Ops:
  19.2 7.4 pack_pair.2
  33.5 52.9 %collective-permute-done.3.d1 = bf16[2048,128]{1,0:T(8,128)(2,1)S(1)} collective-permute-done((bf16[2048,128]{1,0:T(8,128)(2,1)S(1)}, bf16[2048,128]{1,0:T(8,128)(2,1)S(1)}, u32[]{:S(2)}, u32[]{:S(2)}) %collective-permute-start.3) | collective-permute-done | bytes 524320 | tf_op jit(solution)/shard_map/ppermute | solution.py:316
  94.8 40.4 %collective-permute-done.59.x3 = bf16[2048,256]{1,0:T(8,128)(2,1)S(1)} collective-permute-done((bf16[2048,256]{1,0:T(8,128)(2,1)}, bf16[2048,256]{1,0:T(8,128)(2,1)S(1)}, u32[]{:S(2)}, u32[]{:S(2)}) %collective-permute-start.59) | collective-permute-done | bytes 1048608 | tf_op jit(solution)/shard_map/ppermute | solution.py:316
  140.1 40.0 %collective-permute-done.42.x3 = bf16[2048,256]{1,0:T(8,128)(2,1)S(1)} collective-permute-done((bf16[2048,256]{1,0:T(8,128)(2,1)}, bf16[2048,256]{1,0:T(8,128)(2,1)S(1)}, u32[]{:S(2)}, u32[]{:S(2)}) %collective-permute-start.42) | collective-permute-done | bytes 1048608 | tf_op jit(solution)/shard_map/ppermute | solution.py:316
  183.5 7.2 expand_pair.2
  190.6 9.3 chip_stages.14
  203.5 21.6 %collective-permute-done.25.x3 = bf16[2048,256]{1,0:T(8,128)(2,1)} collective-permute-done((bf16[2048,256]{1,0:T(8,128)(2,1)S(1)}, bf16[2048,256]{1,0:T(8,128)(2,1)}, u32[]{:S(2)}, u32[]{:S(2)}) %collective-permute-start.25) | collective-permute-done | bytes 1048608 | tf_op jit(solution)/shard_map/ppermute | solution.py:316
  228.3 9.3 chip_stages.12
  237.6 32.4 %collective-permute-done.2.x3 = bf16[2048,256]{1,0:T(8,128)(2,1)} collective-permute-done((bf16[2048,256]{1,0:T(8,128)(2,1)}, bf16[2048,256]{1,0:T(8,128)(2,1)}, u32[]{:S(2)}, u32[]{:S(2)}) %collective-permute-start.2) | collective-permute-done | bytes 1048608 | tf_op jit(solution)/shard_map/ppermute | solution.py:316
  275.5 39.3 %collective-permute-done.62.x3 = bf16[2048,256]{1,0:T(8,128)(2,1)S(1)} collective-permute-done((bf16[2048,256]{1,0:T(8,128)(2,1)}, bf16[2048,256]{1,0:T(8,128)(2,1)S(1)}, u32[]{:S(2)}, u32[]{:S(2)}) %collective-permute-start.62) | collective-permute-done | bytes 1048608 | tf_op jit(solution)/shard_map/ppermute | solution.py:316
  314.8 9.7 chip_stages.10
  324.7 9.2 chip_stages.8
  341.3 9.6 collective-permute-done.26.x1
  350.9 12.4 %collective-permute-done.27.x2 = bf16[2048,256]{1,0:T(8,128)(2,1)} collective-permute-done((bf16[2048,256]{1,0:T(8,128)(2,1)}, bf16[2048,256]{1,0:T(8,128)(2,1)}, u32[]{:S(2)}, u32[]{:S(2)}) %collective-permute-start.27) | collective-permute-done | bytes 1048608 | tf_op jit(solution)/shard_map/ppermute | solution.py:316
  363.2 9.7 collective-permute-start.8
  372.9 12.2 %collective-permute-done.28.x3 = bf16[2048,256]{1,0:T(8,128)(2,1)S(1)} collective-permute-done((bf16[2048,256]{1,0:T(8,128)(2,1)}, bf16[2048,256]{1,0:T(8,128)(2,1)S(1)}, u32[]{:S(2)}, u32[]{:S(2)}) %collective-permute-start.28) | collective-permute-done | bytes 1048608 | tf_op jit(solution)/shard_map/ppermute | solution.py:316
  385.7 10.2 collective-permute-done.6.x1
  395.9 12.4 %collective-permute-done.7.x2 = bf16[2048,256]{1,0:T(8,128)(2,1)} collective-permute-done((bf16[2048,256]{1,0:T(8,128)(2,1)}, bf16[2048,256]{1,0:T(8,128)(2,1)}, u32[]{:S(2)}, u32[]{:S(2)}) %collective-permute-start.7) | collective-permute-done | bytes 1048608 | tf_op jit(solution)/shard_map/ppermute | solution.py:316
  408.2 19.7 %collective-permute-done.8.x3 = bf16[2048,256]{1,0:T(8,128)(2,1)} collective-permute-done((bf16[2048,256]{1,0:T(8,128)(2,1)}, bf16[2048,256]{1,0:T(8,128)(2,1)}, u32[]{:S(2)}, u32[]{:S(2)}) %collective-permute-start.8) | collective-permute-done | bytes 1048608 | tf_op jit(solution)/shard_map/ppermute | solution.py:316
  432.0 56.9 %spread.2.core_w.first_w = bf16[10,8192,128]{2,1,0:T(8,128)(2,1)} custom-call(bf16[11,2,32,32,256]{4,3,2,1,0:T(8,128)(2,1)} %bitcast.5, bf16[11,2,32,32,256]{4,3,2,1,0:T(8,128)(2,1)} %bitcast.6), custom_call_target="tpu_custom_call" | custom-call | flops 2500000000 | bytes 2500000 | tf_op jit(solution)/shard_map/spread/pallas_call | solution.py:136
  488.9 57.1 %spread.3.second_w.refs_8_.refs_9_.refs_10_.refs_11_ = bf16[10,8192,128]{2,1,0:T(8,128)(2,1)} custom-call(bf16[11,2,32,32,256]{4,3,2,1,0:T(8,128)(2,1)} %bitcast.7, bf16[11,2,32,32,256]{4,3,2,1,0:T(8,128)(2,1)} %bitcast.8), custom_call_target="tpu_custom_call" | custom-call | flops 2500000000 | bytes 2500000 | tf_op jit(solution)/shard_map/spread/pallas_call | solution.py:136
  546.9 46.4 %middle.7.refs_0_.refs_1_.refs_2_.refs_3_ = bf16[8192,256]{1,0:T(8,128)(2,1)} custom-call(s32[1]{0:T(128)} %bitcast.chip_ref, bf16[2048,256]{1,0:T(8,128)(2,1)} %get-tuple-element.135.x0, bf16[2048,256]{1,0:T(8,128)(2,1)} %copy-done.1, bf16[2048,256]{1,0:T(8,128)(2,1)} %copy-done.2, bf16[2048,256]{1,0:T(8,128)(2,1)} %copy-done.3, ...), custom_call_target="tpu_custom_call" | custom-call | flops 3500000000 | bytes 3500000 | tf_op jit(solution)/shard_map/middle/pallas_call | solution.py:253
  593.6 46.2 %middle.6.refs_0_.refs_1_.refs_2_.refs_3_ = bf16[8192,256]{1,0:T(8,128)(2,1)} custom-call(s32[1]{0:T(128)} %bitcast.chip_ref, bf16[2048,256]{1,0:T(8,128)(2,1)} %get-tuple-element.118.x0, bf16[2048,256]{1,0:T(8,128)(2,1)} %collective-permute-done.43.x1, bf16[2048,256]{1,0:T(8,128)(2,1)} %collective-permute-done.44.x2, ...), custom_call_target="tpu_custom_call" | custom-call | flops 3500000000 | bytes 3500000 | tf_op jit(solution)/shard_map/middle/pallas_call | solution.py:253
  640.1 46.5 %middle.4.refs_0_.refs_1_.refs_2_.refs_3_ = bf16[8192,256]{1,0:T(8,128)(2,1)} custom-call(s32[1]{0:T(128)} %bitcast.chip_ref, bf16[2048,256]{1,0:T(8,128)(2,1)} %get-tuple-element.82.x0, bf16[2048,256]{1,0:T(8,128)(2,1)} %collective-permute-done.6.x1, bf16[2048,256]{1,0:T(8,128)(2,1)} %collective-permute-done.7.x2, ...), custom_call_target="tpu_custom_call" | custom-call | flops 3500000000 | bytes 3500000 | tf_op jit(solution)/shard_map/middle/pallas_call | solution.py:253
  688.0 46.2 %middle.5.refs_0_.refs_1_.refs_2_.refs_3_ = bf16[8192,256]{1,0:T(8,128)(2,1)} custom-call(s32[1]{0:T(128)} %bitcast.chip_ref, bf16[2048,256]{1,0:T(8,128)(2,1)} %get-tuple-element.101.x0, bf16[2048,256]{1,0:T(8,128)(2,1)} %collective-permute-done.26.x1, bf16[2048,256]{1,0:T(8,128)(2,1)} %collective-permute-done.27.x2, bf16[2048,256]{1,0:T(8,128)(2,1)} %copy-done.4, ...), custom_call_target="tpu_custom_call" | custom-call | flops 3500000000 | bytes 3500000 | tf_op jit(solution)/shard_map/middle/pallas_call | solution.py:253
  734.6 7.4 pack_pair.3
  745.8 12.6 %collective-permute-done.17.d1 = bf16[2048,128]{1,0:T(8,128)(2,1)S(1)} collective-permute-done((bf16[2048,128]{1,0:T(8,128)(2,1)S(1)}, bf16[2048,128]{1,0:T(8,128)(2,1)S(1)}, u32[]{:S(2)}, u32[]{:S(2)}) %collective-permute-start.17) | collective-permute-done | bytes 524320 | tf_op jit(solution)/shard_map/ppermute | solution.py:316
  761.9 8.5 core_stage.7
  775.6 8.7 collective-permute-done.19.d3
  785.7 8.5 core_stage.6
  797.5 8.5 core_stage.4
  806.2 14.4 %collective-permute-done.68.x1 = bf16[2048,256]{1,0:T(8,128)(2,1)S(1)} collective-permute-done((bf16[2048,256]{1,0:T(8,128)(2,1)}, bf16[2048,256]{1,0:T(8,128)(2,1)S(1)}, u32[]{:S(2)}, u32[]{:S(2)}) %collective-permute-start.68) | collective-permute-done | bytes 1048608 | tf_op jit(solution)/shard_map/ppermute | solution.py:316
  825.6 8.5 core_stage.5
  835.2 10.8 collective-permute-done.51.x1
  847.1 40.9 %collective-permute-done.14.x1 = bf16[2048,256]{1,0:T(8,128)(2,1)} collective-permute-done((bf16[2048,256]{1,0:T(8,128)(2,1)}, bf16[2048,256]{1,0:T(8,128)(2,1)}, u32[]{:S(2)}, u32[]{:S(2)}) %collective-permute-start.14) | collective-permute-done | bytes 1048608 | tf_op jit(solution)/shard_map/ppermute | solution.py:316
  888.0 7.3 expand_pair.3
  895.3 5.7 collective-permute-start.52
  901.0 9.3 chip_stages.9
  910.3 42.0 %collective-permute-done.34.x1 = bf16[2048,256]{1,0:T(8,128)(2,1)S(1)} collective-permute-done((bf16[2048,256]{1,0:T(8,128)(2,1)}, bf16[2048,256]{1,0:T(8,128)(2,1)S(1)}, u32[]{:S(2)}, u32[]{:S(2)}) %collective-permute-start.34) | collective-permute-done | bytes 1048608 | tf_op jit(solution)/shard_map/ppermute | solution.py:316
  958.2 9.4 chip_stages.15
  967.6 9.3 chip_stages.11
  977.0 6.1 broadcast_in_dim.6
  990.1 9.3 chip_stages.13
  1018.9 28.4 %collective-permute-done.37 = bf16[2048,256]{1,0:T(8,128)(2,1)} collective-permute-done((bf16[2048,256]{1,0:T(8,128)(2,1)}, bf16[2048,256]{1,0:T(8,128)(2,1)}, u32[]{:S(2)}, u32[]{:S(2)}) %collective-permute-start.37) | collective-permute-done | bytes 1048608 | tf_op jit(solution)/shard_map/ppermute | solution.py:316
  1063.8 28.4 %collective-permute-done.54 = bf16[2048,256]{1,0:T(8,128)(2,1)S(1)} collective-permute-done((bf16[2048,256]{1,0:T(8,128)(2,1)}, bf16[2048,256]{1,0:T(8,128)(2,1)S(1)}, u32[]{:S(2)}, u32[]{:S(2)}) %collective-permute-start.54) | collective-permute-done | bytes 1048608 | tf_op jit(solution)/shard_map/ppermute | solution.py:316
  1094.3 9.9 collective-permute-done.56
  1106.3 27.8 %collective-permute-done.71 = bf16[2048,256]{1,0:T(8,128)(2,1)S(1)} collective-permute-done((bf16[2048,256]{1,0:T(8,128)(2,1)}, bf16[2048,256]{1,0:T(8,128)(2,1)S(1)}, u32[]{:S(2)}, u32[]{:S(2)}) %collective-permute-start.71) | collective-permute-done | bytes 1048608 | tf_op jit(solution)/shard_map/ppermute | solution.py:316
  1136.1 12.0 %collective-permute-done.73 = bf16[2048,256]{1,0:T(8,128)(2,1)S(1)} collective-permute-done((bf16[2048,256]{1,0:T(8,128)(2,1)S(1)}, bf16[2048,256]{1,0:T(8,128)(2,1)S(1)}, u32[]{:S(2)}, u32[]{:S(2)}) %collective-permute-start.73) | collective-permute-done | bytes 1048608 | tf_op jit(solution)/shard_map/ppermute | solution.py:316
  (210 shorter events, 151.1 us)
Async XLA Ops:
  14.8 76.8 %collective-permute-start.57 = (bf16[2048,256]{1,0:T(8,128)(2,1)}, bf16[2048,256]{1,0:T(8,128)(2,1)}, u32[]{:S(2)}, u32[]{:S(2)}) collective-permute-start(bf16[2048,256]{1,0:T(8,128)(2,1)} %get-tuple-element.132), channel_id=1, source_target_pairs={{0,6},{1,7},{2,0},{3,1},{4,2},{5,3},{6,4},{7,5},{8,14},{9,15},{10,... | collective-permute-start | bytes 3145736 | tf_op jit(solution)/shard_map/ppermute | solution.py:316
  18.7 74.2 %collective-permute-start.58 = (bf16[2048,256]{1,0:T(8,128)(2,1)}, bf16[2048,256]{1,0:T(8,128)(2,1)}, u32[]{:S(2)}, u32[]{:S(2)}) collective-permute-start(bf16[2048,256]{1,0:T(8,128)(2,1)} %get-tuple-element.133), channel_id=1, source_target_pairs={{0,4},{1,5},{2,6},{3,7},{4,0},{5,1},{6,2},{7,3},{8,12},{9,13},{10,... | collective-permute-start | bytes 3145736 | tf_op jit(solution)/shard_map/ppermute | solution.py:316
  29.0 57.3 %collective-permute-start.3 = (bf16[2048,128]{1,0:T(8,128)(2,1)S(1)}, bf16[2048,128]{1,0:T(8,128)(2,1)S(1)}, u32[]{:S(2)}, u32[]{:S(2)}) collective-permute-start(bf16[2048,128]{1,0:T(8,128)(2,1)S(1)} %get-tuple-element.169), channel_id=1, source_target_pairs={{0,6},{1,7},{2,0},{3,1},{4,2},{5,3},{6,4},{7,5},{8,14},{9,15},{10,... | collective-permute-start | bytes 1572872 | tf_op jit(solution)/shard_map/ppermute | solution.py:316
  29.6 56.7 %collective-permute-start.4 = (bf16[2048,128]{1,0:T(8,128)(2,1)S(1)}, bf16[2048,128]{1,0:T(8,128)(2,1)}, u32[]{:S(2)}, u32[]{:S(2)}) collective-permute-start(bf16[2048,128]{1,0:T(8,128)(2,1)S(1)} %get-tuple-element.168), channel_id=1, source_target_pairs={{0,4},{1,5},{2,6},{3,7},{4,0},{5,1},{6,2},{7,3},{8,12},{9,13},{10,... | collective-permute-start | bytes 1572872 | tf_op jit(solution)/shard_map/ppermute | solution.py:316
  32.1 58.0 %collective-permute-start.5 = (bf16[2048,128]{1,0:T(8,128)(2,1)S(1)}, bf16[2048,128]{1,0:T(8,128)(2,1)}, u32[]{:S(2)}, u32[]{:S(2)}) collective-permute-start(bf16[2048,128]{1,0:T(8,128)(2,1)S(1)} %get-tuple-element.167), channel_id=1, source_target_pairs={{0,2},{1,3},{2,4},{3,5},{4,6},{5,7},{6,0},{7,1},{8,10},{9,11},{10,... | collective-permute-start | bytes 1572872 | tf_op jit(solution)/shard_map/ppermute | solution.py:316
  91.6 88.5 %collective-permute-start.42 = (bf16[2048,256]{1,0:T(8,128)(2,1)}, bf16[2048,256]{1,0:T(8,128)(2,1)S(1)}, u32[]{:S(2)}, u32[]{:S(2)}) collective-permute-start(bf16[2048,256]{1,0:T(8,128)(2,1)} %get-tuple-element.117), channel_id=1, source_target_pairs={{0,2},{1,3},{2,4},{3,5},{4,6},{5,7},{6,0},{7,1},{8,10},{9,11},{10,... | collective-permute-start | bytes 3145736 | tf_op jit(solution)/shard_map/ppermute | solution.py:316
  92.9 88.4 %collective-permute-start.23 = (bf16[2048,256]{1,0:T(8,128)(2,1)S(1)}, bf16[2048,256]{1,0:T(8,128)(2,1)S(1)}, u32[]{:S(2)}, u32[]{:S(2)}) collective-permute-start(bf16[2048,256]{1,0:T(8,128)(2,1)S(1)} %get-tuple-element.98), channel_id=1, source_target_pairs={{0,6},{1,7},{2,0},{3,1},{4,2},{5,3},{6,4},{7,5},{8,14},{9,15},{10,... | collective-permute-start | bytes 3145736 | tf_op jit(solution)/shard_map/ppermute | solution.py:316
  135.2 64.7 %collective-permute-start.24 = (bf16[2048,256]{1,0:T(8,128)(2,1)}, bf16[2048,256]{1,0:T(8,128)(2,1)}, u32[]{:S(2)}, u32[]{:S(2)}) collective-permute-start(bf16[2048,256]{1,0:T(8,128)(2,1)} %get-tuple-element.99), channel_id=1, source_target_pairs={{0,4},{1,5},{2,6},{3,7},{4,0},{5,1},{6,2},{7,3},{8,12},{9,13},{10,... | collective-permute-start | bytes 3145736 | tf_op jit(solution)/shard_map/ppermute | solution.py:316
  136.4 88.7 %collective-permute-start.25 = (bf16[2048,256]{1,0:T(8,128)(2,1)S(1)}, bf16[2048,256]{1,0:T(8,128)(2,1)}, u32[]{:S(2)}, u32[]{:S(2)}) collective-permute-start(bf16[2048,256]{1,0:T(8,128)(2,1)S(1)} %get-tuple-element.100), channel_id=1, source_target_pairs={{0,2},{1,3},{2,4},{3,5},{4,6},{5,7},{6,0},{7,1},{8,10},{9,11},{10,... | collective-permute-start | bytes 3145736 | tf_op jit(solution)/shard_map/ppermute | solution.py:316
  138.2 88.0 %collective-permute-start = (bf16[2048,256]{1,0:T(8,128)(2,1)S(1)}, bf16[2048,256]{1,0:T(8,128)(2,1)}, u32[]{:S(2)}, u32[]{:S(2)}) collective-permute-start(bf16[2048,256]{1,0:T(8,128)(2,1)S(1)} %get-tuple-element.77), channel_id=1, source_target_pairs={{0,6},{1,7},{2,0},{3,1},{4,2},{5,3},{6,4},{7,5},{8,14},{9,15},{10,... | collective-permute-start | bytes 3145736 | tf_op jit(solution)/shard_map/ppermute | solution.py:316
  182.3 87.7 %collective-permute-start.2 = (bf16[2048,256]{1,0:T(8,128)(2,1)}, bf16[2048,256]{1,0:T(8,128)(2,1)}, u32[]{:S(2)}, u32[]{:S(2)}) collective-permute-start(bf16[2048,256]{1,0:T(8,128)(2,1)} %get-tuple-element.79), channel_id=1, source_target_pairs={{0,2},{1,3},{2,4},{3,5},{4,6},{5,7},{6,0},{7,1},{8,10},{9,11},{10,... | collective-permute-start | bytes 3145736 | tf_op jit(solution)/shard_map/ppermute | solution.py:316
  199.9 71.1 %collective-permute-start.60 = (bf16[2048,256]{1,0:T(8,128)(2,1)}, bf16[2048,256]{1,0:T(8,128)(2,1)S(1)}, u32[]{:S(2)}, u32[]{:S(2)}) collective-permute-start(bf16[2048,256]{1,0:T(8,128)(2,1)} %get-tuple-element.136), channel_id=1, source_target_pairs={{0,6},{1,7},{2,0},{3,1},{4,2},{5,3},{6,4},{7,5},{8,14},{9,15},{10,... | collective-permute-start | bytes 3145736 | tf_op jit(solution)/shard_map/ppermute | solution.py:316
  226.2 88.6 %collective-permute-start.62 = (bf16[2048,256]{1,0:T(8,128)(2,1)}, bf16[2048,256]{1,0:T(8,128)(2,1)S(1)}, u32[]{:S(2)}, u32[]{:S(2)}) collective-permute-start(bf16[2048,256]{1,0:T(8,128)(2,1)} %get-tuple-element.138), channel_id=1, source_target_pairs={{0,2},{1,3},{2,4},{3,5},{4,6},{5,7},{6,0},{7,1},{8,10},{9,11},{10,... | collective-permute-start | bytes 3145736 | tf_op jit(solution)/shard_map/ppermute | solution.py:316
  228.3 96.2 %collective-permute-start.63 = (bf16[2048,256]{1,0:T(8,128)(2,1)}, bf16[2048,256]{1,0:T(8,128)(2,1)}, u32[]{:S(2)}, u32[]{:S(2)}) collective-permute-start(bf16[2048,256]{1,0:T(8,128)(2,1)} %get-tuple-element.135.x0), channel_id=1, source_target_pairs={{0,1},{1,0},{2,3},{3,2},{4,5},{5,4},{6,7},{7,6},{8,9},{9,8},{10,11... | collective-permute-start | bytes 3145736 | tf_op jit(solution)/shard_map/ppermute | solution.py:319
  271.0 62.9 %collective-permute-start.44 = (bf16[2048,256]{1,0:T(8,128)(2,1)}, bf16[2048,256]{1,0:T(8,128)(2,1)}, u32[]{:S(2)}, u32[]{:S(2)}) collective-permute-start(bf16[2048,256]{1,0:T(8,128)(2,1)} %get-tuple-element.120), channel_id=1, source_target_pairs={{0,4},{1,5},{2,6},{3,7},{4,0},{5,1},{6,2},{7,3},{8,12},{9,13},{10,... | collective-permute-start | bytes 3145736 | tf_op jit(solution)/shard_map/ppermute | solution.py:316
  273.2 64.8 %collective-permute-start.45 = (bf16[2048,256]{1,0:T(8,128)(2,1)}, bf16[2048,256]{1,0:T(8,128)(2,1)}, u32[]{:S(2)}, u32[]{:S(2)}) collective-permute-start(bf16[2048,256]{1,0:T(8,128)(2,1)} %get-tuple-element.121), channel_id=1, source_target_pairs={{0,2},{1,3},{2,4},{3,5},{4,6},{5,7},{6,0},{7,1},{8,10},{9,11},{10,... | collective-permute-start | bytes 3145736 | tf_op jit(solution)/shard_map/ppermute | solution.py:316
  337.9 57.9 %collective-permute-start.6 = (bf16[2048,256]{1,0:T(8,128)(2,1)}, bf16[2048,256]{1,0:T(8,128)(2,1)}, u32[]{:S(2)}, u32[]{:S(2)}) collective-permute-start(bf16[2048,256]{1,0:T(8,128)(2,1)} %get-tuple-element.83), channel_id=1, source_target_pairs={{0,6},{1,7},{2,0},{3,1},{4,2},{5,3},{6,4},{7,5},{8,14},{9,15},{10,... | collective-permute-start | bytes 3145736 | tf_op jit(solution)/shard_map/ppermute | solution.py:316
  350.9 57.3 %collective-permute-start.7 = (bf16[2048,256]{1,0:T(8,128)(2,1)}, bf16[2048,256]{1,0:T(8,128)(2,1)}, u32[]{:S(2)}, u32[]{:S(2)}) collective-permute-start(bf16[2048,256]{1,0:T(8,128)(2,1)} %get-tuple-element.84), channel_id=1, source_target_pairs={{0,4},{1,5},{2,6},{3,7},{4,0},{5,1},{6,2},{7,3},{8,12},{9,13},{10,... | collective-permute-start | bytes 3145736 | tf_op jit(solution)/shard_map/ppermute | solution.py:316
  363.2 64.7 %collective-permute-start.8 = (bf16[2048,256]{1,0:T(8,128)(2,1)}, bf16[2048,256]{1,0:T(8,128)(2,1)}, u32[]{:S(2)}, u32[]{:S(2)}) collective-permute-start(bf16[2048,256]{1,0:T(8,128)(2,1)} %get-tuple-element.85), channel_id=1, source_target_pairs={{0,2},{1,3},{2,4},{3,5},{4,6},{5,7},{6,0},{7,1},{8,10},{9,11},{10,... | collective-permute-start | bytes 3145736 | tf_op jit(solution)/shard_map/ppermute | solution.py:316
  428.0 118.0 %collective-permute-start.48 = (bf16[2048,256]{1,0:T(8,128)(2,1)}, bf16[2048,256]{1,0:T(8,128)(2,1)}, u32[]{:S(2)}, u32[]{:S(2)}) collective-permute-start(bf16[2048,256]{1,0:T(8,128)(2,1)} %collective-permute-done.44.x2), channel_id=1, source_target_pairs={{0,1},{1,0},{2,3},{3,2},{4,5},{5,4},{6,7},{7,6},{8,9},{9,8},{10,11... | collective-permute-start | bytes 3145736 | tf_op jit(solution)/shard_map/ppermute | solution.py:319
  428.5 117.9 %collective-permute-start.49 = (bf16[2048,256]{1,0:T(8,128)(2,1)}, bf16[2048,256]{1,0:T(8,128)(2,1)}, u32[]{:S(2)}, u32[]{:S(2)}) collective-permute-start(bf16[2048,256]{1,0:T(8,128)(2,1)} %collective-permute-done.45.x3), channel_id=1, source_target_pairs={{0,1},{1,0},{2,3},{3,2},{4,5},{5,4},{6,7},{7,6},{8,9},{9,8},{10,11... | collective-permute-start | bytes 3145736 | tf_op jit(solution)/shard_map/ppermute | solution.py:319
  428.6 117.9 %collective-permute-start.10 = (bf16[2048,256]{1,0:T(8,128)(2,1)}, bf16[2048,256]{1,0:T(8,128)(2,1)}, u32[]{:S(2)}, u32[]{:S(2)}) collective-permute-start(bf16[2048,256]{1,0:T(8,128)(2,1)} %collective-permute-done.6.x1), channel_id=1, source_target_pairs={{0,1},{1,0},{2,3},{3,2},{4,5},{5,4},{6,7},{7,6},{8,9},{9,8},{10,11... | collective-permute-start | bytes 3145736 | tf_op jit(solution)/shard_map/ppermute | solution.py:319
  429.0 164.3 %collective-permute-start.11 = (bf16[2048,256]{1,0:T(8,128)(2,1)}, bf16[2048,256]{1,0:T(8,128)(2,1)}, u32[]{:S(2)}, u32[]{:S(2)}) collective-permute-start(bf16[2048,256]{1,0:T(8,128)(2,1)} %collective-permute-done.7.x2), channel_id=1, source_target_pairs={{0,1},{1,0},{2,3},{3,2},{4,5},{5,4},{6,7},{7,6},{8,9},{9,8},{10,11... | collective-permute-start | bytes 3145736 | tf_op jit(solution)/shard_map/ppermute | solution.py:319
  431.8 208.0 %collective-permute-start.12 = (bf16[2048,256]{1,0:T(8,128)(2,1)}, bf16[2048,256]{1,0:T(8,128)(2,1)}, u32[]{:S(2)}, u32[]{:S(2)}) collective-permute-start(bf16[2048,256]{1,0:T(8,128)(2,1)} %collective-permute-done.8.x3), channel_id=1, source_target_pairs={{0,1},{1,0},{2,3},{3,2},{4,5},{5,4},{6,7},{7,6},{8,9},{9,8},{10,11... | collective-permute-start | bytes 3145736 | tf_op jit(solution)/shard_map/ppermute | solution.py:319
  546.0 140.6 %collective-permute-start.30 = (bf16[2048,256]{1,0:T(8,128)(2,1)}, bf16[2048,256]{1,0:T(8,128)(2,1)S(1)}, u32[]{:S(2)}, u32[]{:S(2)}) collective-permute-start(bf16[2048,256]{1,0:T(8,128)(2,1)} %collective-permute-done.26.x1), channel_id=1, source_target_pairs={{0,1},{1,0},{2,3},{3,2},{4,5},{5,4},{6,7},{7,6},{8,9},{9,8},{10,11... | collective-permute-start | bytes 3145736 | tf_op jit(solution)/shard_map/ppermute | solution.py:319
  546.4 140.6 %collective-permute-start.31 = (bf16[2048,256]{1,0:T(8,128)(2,1)}, bf16[2048,256]{1,0:T(8,128)(2,1)S(1)}, u32[]{:S(2)}, u32[]{:S(2)}) collective-permute-start(bf16[2048,256]{1,0:T(8,128)(2,1)} %collective-permute-done.27.x2), channel_id=1, source_target_pairs={{0,1},{1,0},{2,3},{3,2},{4,5},{5,4},{6,7},{7,6},{8,9},{9,8},{10,11... | collective-permute-start | bytes 3145736 | tf_op jit(solution)/shard_map/ppermute | solution.py:319
  546.5 140.5 %collective-permute-start.32 = (bf16[2048,256]{1,0:T(8,128)(2,1)S(1)}, bf16[2048,256]{1,0:T(8,128)(2,1)}, u32[]{:S(2)}, u32[]{:S(2)}) collective-permute-start(bf16[2048,256]{1,0:T(8,128)(2,1)S(1)} %copy-done.5), channel_id=1, source_target_pairs={{0,1},{1,0},{2,3},{3,2},{4,5},{5,4},{6,7},{7,6},{8,9},{9,8},{10,11... | collective-permute-start | bytes 3145736 | tf_op jit(solution)/shard_map/ppermute | solution.py:319
  593.3 166.2 %collective-permute-start.67 = (bf16[8192,256]{1,0:T(8,128)(2,1)}, bf16[8192,256]{1,0:T(8,128)(2,1)}, u32[]{:S(2)}, u32[]{:S(2)}) collective-permute-start(bf16[8192,256]{1,0:T(8,128)(2,1)} %middle.7.refs_0_.refs_1_.refs_2_.refs_3_), channel_id=1, source_target_pairs={{0,1},{1,0},{2,3},{3,2},{4,5},{5,4},{6,7},{7,6},{8,9},{9,8},{10,11... | collective-permute-start | bytes 12582920 | tf_op jit(solution)/shard_map/ppermute | solution.py:319
  639.8 145.8 %collective-permute-start.50 = (bf16[8192,256]{1,0:T(8,128)(2,1)}, bf16[8192,256]{1,0:T(8,128)(2,1)}, u32[]{:S(2)}, u32[]{:S(2)}) collective-permute-start(bf16[8192,256]{1,0:T(8,128)(2,1)} %middle.6.refs_0_.refs_1_.refs_2_.refs_3_), channel_id=1, source_target_pairs={{0,1},{1,0},{2,3},{3,2},{4,5},{5,4},{6,7},{7,6},{8,9},{9,8},{10,11... | collective-permute-start | bytes 12582920 | tf_op jit(solution)/shard_map/ppermute | solution.py:319
  686.6 107.6 %collective-permute-start.13 = (bf16[8192,256]{1,0:T(8,128)(2,1)}, bf16[8192,256]{1,0:T(8,128)(2,1)}, u32[]{:S(2)}, u32[]{:S(2)}) collective-permute-start(bf16[8192,256]{1,0:T(8,128)(2,1)} %middle.4.refs_0_.refs_1_.refs_2_.refs_3_), channel_id=1, source_target_pairs={{0,1},{1,0},{2,3},{3,2},{4,5},{5,4},{6,7},{7,6},{8,9},{9,8},{10,11... | collective-permute-start | bytes 12582920 | tf_op jit(solution)/shard_map/ppermute | solution.py:319
  734.3 71.8 %collective-permute-start.33 = (bf16[8192,256]{1,0:T(8,128)(2,1)}, bf16[8192,256]{1,0:T(8,128)(2,1)}, u32[]{:S(2)}, u32[]{:S(2)}) collective-permute-start(bf16[8192,256]{1,0:T(8,128)(2,1)} %middle.5.refs_0_.refs_1_.refs_2_.refs_3_), channel_id=1, source_target_pairs={{0,1},{1,0},{2,3},{3,2},{4,5},{5,4},{6,7},{7,6},{8,9},{9,8},{10,11... | collective-permute-start | bytes 12582920 | tf_op jit(solution)/shard_map/ppermute | solution.py:319
  806.1 81.9 %collective-permute-start.14 = (bf16[2048,256]{1,0:T(8,128)(2,1)}, bf16[2048,256]{1,0:T(8,128)(2,1)}, u32[]{:S(2)}, u32[]{:S(2)}) collective-permute-start(bf16[2048,256]{1,0:T(8,128)(2,1)} %get-tuple-element.87), channel_id=1, source_target_pairs={{0,6},{1,7},{2,0},{3,1},{4,2},{5,3},{6,4},{7,5},{8,14},{9,15},{10,... | collective-permute-start | bytes 3145736 | tf_op jit(solution)/shard_map/ppermute | solution.py:316
  820.6 74.6 %collective-permute-start.15 = (bf16[2048,256]{1,0:T(8,128)(2,1)}, bf16[2048,256]{1,0:T(8,128)(2,1)}, u32[]{:S(2)}, u32[]{:S(2)}) collective-permute-start(bf16[2048,256]{1,0:T(8,128)(2,1)} %get-tuple-element.88), channel_id=1, source_target_pairs={{0,4},{1,5},{2,6},{3,7},{4,0},{5,1},{6,2},{7,3},{8,12},{9,13},{10,... | collective-permute-start | bytes 3145736 | tf_op jit(solution)/shard_map/ppermute | solution.py:316
  820.6 80.3 %collective-permute-start.16 = (bf16[2048,256]{1,0:T(8,128)(2,1)}, bf16[2048,256]{1,0:T(8,128)(2,1)}, u32[]{:S(2)}, u32[]{:S(2)}) collective-permute-start(bf16[2048,256]{1,0:T(8,128)(2,1)} %get-tuple-element.89), channel_id=1, source_target_pairs={{0,2},{1,3},{2,4},{3,5},{4,6},{5,7},{6,0},{7,1},{8,10},{9,11},{10,... | collective-permute-start | bytes 3145736 | tf_op jit(solution)/shard_map/ppermute | solution.py:316
  834.7 117.6 %collective-permute-start.34 = (bf16[2048,256]{1,0:T(8,128)(2,1)}, bf16[2048,256]{1,0:T(8,128)(2,1)S(1)}, u32[]{:S(2)}, u32[]{:S(2)}) collective-permute-start(bf16[2048,256]{1,0:T(8,128)(2,1)} %get-tuple-element.106), channel_id=1, source_target_pairs={{0,6},{1,7},{2,0},{3,1},{4,2},{5,3},{6,4},{7,5},{8,14},{9,15},{10,... | collective-permute-start | bytes 3145736 | tf_op jit(solution)/shard_map/ppermute | solution.py:316
  846.0 110.4 %collective-permute-start.35 = (bf16[2048,256]{1,0:T(8,128)(2,1)}, bf16[2048,256]{1,0:T(8,128)(2,1)S(1)}, u32[]{:S(2)}, u32[]{:S(2)}) collective-permute-start(bf16[2048,256]{1,0:T(8,128)(2,1)} %get-tuple-element.107), channel_id=1, source_target_pairs={{0,4},{1,5},{2,6},{3,7},{4,0},{5,1},{6,2},{7,3},{8,12},{9,13},{10,... | collective-permute-start | bytes 3145736 | tf_op jit(solution)/shard_map/ppermute | solution.py:316
  888.0 69.4 %collective-permute-start.36 = (bf16[2048,256]{1,0:T(8,128)(2,1)}, bf16[2048,256]{1,0:T(8,128)(2,1)}, u32[]{:S(2)}, u32[]{:S(2)}) collective-permute-start(bf16[2048,256]{1,0:T(8,128)(2,1)} %get-tuple-element.108), channel_id=1, source_target_pairs={{0,2},{1,3},{2,4},{3,5},{4,6},{5,7},{6,0},{7,1},{8,10},{9,11},{10,... | collective-permute-start | bytes 3145736 | tf_op jit(solution)/shard_map/ppermute | solution.py:316
  895.3 90.2 %collective-permute-start.52 = (bf16[2048,256]{1,0:T(8,128)(2,1)}, bf16[2048,256]{1,0:T(8,128)(2,1)}, u32[]{:S(2)}, u32[]{:S(2)}) collective-permute-start(bf16[2048,256]{1,0:T(8,128)(2,1)} %get-tuple-element.124), channel_id=1, source_target_pairs={{0,4},{1,5},{2,6},{3,7},{4,0},{5,1},{6,2},{7,3},{8,12},{9,13},{10,... | collective-permute-start | bytes 3145736 | tf_op jit(solution)/shard_map/ppermute | solution.py:316
  901.0 86.9 %collective-permute-start.53 = (bf16[2048,256]{1,0:T(8,128)(2,1)}, bf16[2048,256]{1,0:T(8,128)(2,1)}, u32[]{:S(2)}, u32[]{:S(2)}) collective-permute-start(bf16[2048,256]{1,0:T(8,128)(2,1)} %get-tuple-element.125), channel_id=1, source_target_pairs={{0,2},{1,3},{2,4},{3,5},{4,6},{5,7},{6,0},{7,1},{8,10},{9,11},{10,... | collective-permute-start | bytes 3145736 | tf_op jit(solution)/shard_map/ppermute | solution.py:316
  957.4 57.0 %collective-permute-start.22 = (bf16[2048,256]{1,0:T(8,128)(2,1)}, bf16[2048,256]{1,0:T(8,128)(2,1)S(1)}, u32[]{:S(2)}, u32[]{:S(2)}) collective-permute-start(bf16[2048,256]{1,0:T(8,128)(2,1)} %get-tuple-element.95), channel_id=1, source_target_pairs={{0,2},{1,3},{2,4},{3,5},{4,6},{5,7},{6,0},{7,1},{8,10},{9,11},{10,... | collective-permute-start | bytes 3145736 | tf_op jit(solution)/shard_map/ppermute | solution.py:316
  985.4 61.9 %collective-permute-start.37 = (bf16[2048,256]{1,0:T(8,128)(2,1)}, bf16[2048,256]{1,0:T(8,128)(2,1)}, u32[]{:S(2)}, u32[]{:S(2)}) collective-permute-start(bf16[2048,256]{1,0:T(8,128)(2,1)} %get-tuple-element.110), channel_id=1, source_target_pairs={{0,6},{1,7},{2,0},{3,1},{4,2},{5,3},{6,4},{7,5},{8,14},{9,15},{10,... | collective-permute-start | bytes 3145736 | tf_op jit(solution)/shard_map/ppermute | solution.py:316
  987.8 61.7 %collective-permute-start.38 = (bf16[2048,256]{1,0:T(8,128)(2,1)}, bf16[2048,256]{1,0:T(8,128)(2,1)}, u32[]{:S(2)}, u32[]{:S(2)}) collective-permute-start(bf16[2048,256]{1,0:T(8,128)(2,1)} %get-tuple-element.111), channel_id=1, source_target_pairs={{0,4},{1,5},{2,6},{3,7},{4,0},{5,1},{6,2},{7,3},{8,12},{9,13},{10,... | collective-permute-start | bytes 3145736 | tf_op jit(solution)/shard_map/ppermute | solution.py:316
  1002.4 56.9 %collective-permute-start.39 = (bf16[2048,256]{1,0:T(8,128)(2,1)}, bf16[2048,256]{1,0:T(8,128)(2,1)S(1)}, u32[]{:S(2)}, u32[]{:S(2)}) collective-permute-start(bf16[2048,256]{1,0:T(8,128)(2,1)} %get-tuple-element.112), channel_id=1, source_target_pairs={{0,2},{1,3},{2,4},{3,5},{4,6},{5,7},{6,0},{7,1},{8,10},{9,11},{10,... | collective-permute-start | bytes 3145736 | tf_op jit(solution)/shard_map/ppermute | solution.py:316
  1004.7 87.5 %collective-permute-start.54 = (bf16[2048,256]{1,0:T(8,128)(2,1)}, bf16[2048,256]{1,0:T(8,128)(2,1)S(1)}, u32[]{:S(2)}, u32[]{:S(2)}) collective-permute-start(bf16[2048,256]{1,0:T(8,128)(2,1)} %get-tuple-element.127), channel_id=1, source_target_pairs={{0,6},{1,7},{2,0},{3,1},{4,2},{5,3},{6,4},{7,5},{8,14},{9,15},{10,... | collective-permute-start | bytes 3145736 | tf_op jit(solution)/shard_map/ppermute | solution.py:316
  1014.4 78.8 %collective-permute-start.55 = (bf16[2048,256]{1,0:T(8,128)(2,1)}, bf16[2048,256]{1,0:T(8,128)(2,1)S(1)}, u32[]{:S(2)}, u32[]{:S(2)}) collective-permute-start(bf16[2048,256]{1,0:T(8,128)(2,1)} %get-tuple-element.128), channel_id=1, source_target_pairs={{0,4},{1,5},{2,6},{3,7},{4,0},{5,1},{6,2},{7,3},{8,12},{9,13},{10,... | collective-permute-start | bytes 3145736 | tf_op jit(solution)/shard_map/ppermute | solution.py:316
  1047.3 56.9 %collective-permute-start.56 = (bf16[2048,256]{1,0:T(8,128)(2,1)}, bf16[2048,256]{1,0:T(8,128)(2,1)S(1)}, u32[]{:S(2)}, u32[]{:S(2)}) collective-permute-start(bf16[2048,256]{1,0:T(8,128)(2,1)} %get-tuple-element.129), channel_id=1, source_target_pairs={{0,2},{1,3},{2,4},{3,5},{4,6},{5,7},{6,0},{7,1},{8,10},{9,11},{10,... | collective-permute-start | bytes 3145736 | tf_op jit(solution)/shard_map/ppermute | solution.py:316
  1049.6 84.5 %collective-permute-start.71 = (bf16[2048,256]{1,0:T(8,128)(2,1)}, bf16[2048,256]{1,0:T(8,128)(2,1)S(1)}, u32[]{:S(2)}, u32[]{:S(2)}) collective-permute-start(bf16[2048,256]{1,0:T(8,128)(2,1)} %get-tuple-element.144), channel_id=1, source_target_pairs={{0,6},{1,7},{2,0},{3,1},{4,2},{5,3},{6,4},{7,5},{8,14},{9,15},{10,... | collective-permute-start | bytes 3145736 | tf_op jit(solution)/shard_map/ppermute | solution.py:316
  1059.3 75.8 %collective-permute-start.72 = (bf16[2048,256]{1,0:T(8,128)(2,1)}, bf16[2048,256]{1,0:T(8,128)(2,1)S(1)}, u32[]{:S(2)}, u32[]{:S(2)}) collective-permute-start(bf16[2048,256]{1,0:T(8,128)(2,1)} %get-tuple-element.145), channel_id=1, source_target_pairs={{0,4},{1,5},{2,6},{3,7},{4,0},{5,1},{6,2},{7,3},{8,12},{9,13},{10,... | collective-permute-start | bytes 3145736 | tf_op jit(solution)/shard_map/ppermute | solution.py:316
  (56 other events, 2403.2 us)
where the time goes:
time: 1150 us
  waiting for transfers between devices  568 us (49%)
  Pallas kernels  437 us (38%)
  starting transfers between devices  87.8 us (8%)
  local copies, waits for them, and re-layouts  54.9 us (5%)
    ppermute x54, waiting for transfers between devices, to_chip(): return lax.ppermute(value, 'sp', pairs)  566 us
    pallas_call x4, Pallas kernels, middle(): pl.pallas_call(functools.partial(middle_kernel, blk), grid_spec=pltpu.Pre...  185 us
    pallas_call x2, Pallas kernels, spread(): pl.pallas_call(functools.partial(spread_kernel, first_map), grid=(5,), in...  114 us
    ppermute x54, starting transfers between devices, to_chip(): return lax.ppermute(value, 'sp', pairs)  83.8 us
    pallas_call x8, Pallas kernels, chip_stages(): pl.pallas_call(functools.partial(chip_kernel, blk), grid=(rows // tile,),...  74.8 us
    pallas_call x4, Pallas kernels, core_stage(): pl.pallas_call(functools.partial(core_kernel, blk), grid_spec=pltpu.Prefe...  34 us
    dynamic_update_slice x16, local copies, waits for them, and re-layouts, device_program(): result = lax.dynamic_update_slice(result, parts[r], at)  24 us
  transfers between devices with their start and end apart: 74, of which 37 were waited for; matrix products, arithmetic and copies ran while one was open for 3% of the time, Pallas kernels for 38%

commit v1 on v0

--- a/solution.py
+++ b/solution.py
@@ -310,6 +310,7 @@
 
 def solution(mesh):
     members = mesh.shape["sp"]
+    groups = mesh.shape["dp"]
 
     def to_chip(value, shift):
         pairs = [(d, (d + shift * CORES) % members) for d in range(members)]
@@ -332,14 +333,26 @@
         chunks = channels // width
         chip = lax.axis_index("sp") // CORES
         odd = chip % 2
+        side = lax.axis_index("dp") % 2
         chip_arr = jnp.full((1,), chip, jnp.int32)
 
-        def quarter(array, rel, col, wide):
-            return lax.dynamic_slice(array, (((chip + rel) % CHIPS) * group, col), (group, wide))
+        def quarter(array, rel, col, wide, half=None):
+            start = ((chip + rel) % CHIPS) * group
+            if half is None:
+                return lax.dynamic_slice(array, (start, col), (group, wide))
+            return lax.dynamic_slice(array, (start + half * (group // 2), col), (group // 2, wide))
 
         def chip_weights(weights, hi, lo):
             packed = pack_pair(weights, hi, lo)
-            got = swap([quarter(packed, r, 0, LANES) for r in range(CHIPS)])
+            if groups % 2:
+                got = swap([quarter(packed, r, 0, LANES) for r in range(CHIPS)])
+            else:
+                own = quarter(packed, 0, 0, LANES)
+                mine = swap([own] + [quarter(packed, r, 0, LANES, side) for r in range(1, CHIPS)])[1:]
+            if groups % 2 == 0:
+                theirs = [lax.ppermute(m, "dp", [(g, g ^ 1) for g in range(groups)]) for m in mine]
+                both = [(jnp.where(side == 0, m, t), jnp.where(side == 0, t, m)) for m, t in zip(mine, theirs)]
+                got = [own] + [jnp.concatenate(b, axis=0) for b in both]
             return expand_pair(got, odd, blk)
 
         w_first, w_second = (jnp.transpose(w, (0, 2, 3, 4, 1)) for w in (w_first, w_second))

time: 1150 us -> 1120 us (0.974)
  waiting for transfers between devices: 568 us -> 441 us
  starting transfers between devices: 87.8 us -> 171 us
    ppermute x54, waiting for transfers between devices: 566 us -> 433 us  [to_chip(): return lax.ppermute(value, 'sp', pairs)]
    ppermute x54, starting transfers between devices: 83.8 us -> 158 us  [to_chip(): return lax.ppermute(value, 'sp', pairs)]
    dynamic_slice x6 -> x8, local copies, waits for them, and re-layouts: 18 us -> 24.2 us  [the longest x6 20.3 us: quarter(): return lax.dynamic_slice(array, (start, col), (group, wide))]
  transfers between devices with their start and end apart: 74 -> 80, of which waited for: 37 -> 30; matrix products, arithmetic and copies ran while one was open for 3% -> 6% of each run, Pallas kernels for 38% -> 38%
where the time goes in v1:
time: 1120 us
  waiting for transfers between devices  441 us (39%)
  Pallas kernels  437 us (39%)
  starting transfers between devices  171 us (15%)
  local copies, waits for them, and re-layouts  61.5 us (5%)
    ppermute x54, waiting for transfers between devices, to_chip(): return lax.ppermute(value, 'sp', pairs)  433 us
    pallas_call x4, Pallas kernels, middle(): pl.pallas_call(functools.partial(middle_kernel, blk), grid_spec=pltpu.Pre...  185 us
    ppermute x54, starting transfers between devices, to_chip(): return lax.ppermute(value, 'sp', pairs)  158 us
    pallas_call x2, Pallas kernels, spread(): pl.pallas_call(functools.partial(spread_kernel, first_map), grid=(5,), in...  114 us
    pallas_call x8, Pallas kernels, chip_stages(): pl.pallas_call(functools.partial(chip_kernel, blk), grid=(rows // tile,),...  74.8 us
    pallas_call x4, Pallas kernels, core_stage(): pl.pallas_call(functools.partial(core_kernel, blk), grid_spec=pltpu.Prefe...  34.1 us
    dynamic_update_slice x16, local copies, waits for them, and re-layouts, device_program(): result = lax.dynamic_update_slice(result, parts[r], at)  24 us
  transfers between devices with their start and end apart: 80, of which 30 were waited for; matrix products, arithmetic and copies ran while one was open for 6% of the time, Pallas kernels for 38%

profile of v1, /device:TPU:112, one launch (start us, length us, event | category | flops | bytes accessed | tf_op | source)
XLA Modules:
  0.0 1120.9 jit_solution(14590902557293444118)
XLA Ops:
  0.0 7.4 pack_pair.3
  13.2 7.4 pack_pair.2
  48.1 51.5 %collective-permute-done.3 = bf16[1024,128]{1,0:T(8,128)(2,1)} collective-permute-done((bf16[1024,128]{1,0:T(8,128)(2,1)S(1)}, bf16[1024,128]{1,0:T(8,128)(2,1)}, u32[]{:S(2)}, u32[]{:S(2)}) %collective-permute-start.3) | collective-permute-done | bytes 262176 | tf_op jit(solution)/shard_map/ppermute | solution.py:317
  121.2 34.0 %collective-permute-done.65.x3 = bf16[2048,256]{1,0:T(8,128)(2,1)} collective-permute-done((bf16[2048,256]{1,0:T(8,128)(2,1)}, bf16[2048,256]{1,0:T(8,128)(2,1)}, u32[]{:S(2)}, u32[]{:S(2)}) %collective-permute-start.65) | collective-permute-done | bytes 1048608 | tf_op jit(solution)/shard_map/ppermute | solution.py:317
  164.9 35.3 %collective-permute-done.48.x3 = bf16[2048,256]{1,0:T(8,128)(2,1)} collective-permute-done((bf16[2048,256]{1,0:T(8,128)(2,1)}, bf16[2048,256]{1,0:T(8,128)(2,1)}, u32[]{:S(2)}, u32[]{:S(2)}) %collective-permute-start.48) | collective-permute-done | bytes 1048608 | tf_op jit(solution)/shard_map/ppermute | solution.py:317
  204.3 7.1 expand_pair.2
  211.4 9.3 chip_stages.14
  226.0 19.1 %collective-permute-done.31.x3 = bf16[2048,256]{1,0:T(8,128)(2,1)} collective-permute-done((bf16[2048,256]{1,0:T(8,128)(2,1)S(1)}, bf16[2048,256]{1,0:T(8,128)(2,1)}, u32[]{:S(2)}, u32[]{:S(2)}) %collective-permute-start.31) | collective-permute-done | bytes 1048608 | tf_op jit(solution)/shard_map/ppermute | solution.py:317
  248.3 9.3 chip_stages.12
  262.4 9.6 collective-permute-done.66.x1
  272.0 7.7 collective-permute-done.67.x2
  279.8 13.8 %collective-permute-start.51 = (bf16[2048,256]{1,0:T(8,128)(2,1)}, bf16[2048,256]{1,0:T(8,128)(2,1)}, u32[]{:S(2)}, u32[]{:S(2)}) collective-permute-start(bf16[2048,256]{1,0:T(8,128)(2,1)} %get-tuple-element.121), channel_id=1, source_target_pairs={{0,2},{1,3},{2,4},{3,5},{4,6},{5,7},{6,0},{7,1},{8,10},{9,11},{10,... | collective-permute-start | bytes 3145736 | tf_op jit(solution)/shard_map/ppermute | solution.py:317
  293.6 16.8 %collective-permute-done.68.x3 = bf16[2048,256]{1,0:T(8,128)(2,1)S(1)} collective-permute-done((bf16[2048,256]{1,0:T(8,128)(2,1)}, bf16[2048,256]{1,0:T(8,128)(2,1)S(1)}, u32[]{:S(2)}, u32[]{:S(2)}) %collective-permute-start.68) | collective-permute-done | bytes 1048608 | tf_op jit(solution)/shard_map/ppermute | solution.py:317
  310.4 9.7 chip_stages.10
  324.1 9.3 chip_stages.8
  338.2 30.8 %collective-permute-done.32.x1 = bf16[2048,256]{1,0:T(8,128)(2,1)} collective-permute-done((bf16[2048,256]{1,0:T(8,128)(2,1)}, bf16[2048,256]{1,0:T(8,128)(2,1)}, u32[]{:S(2)}, u32[]{:S(2)}) %collective-permute-start.32) | collective-permute-done | bytes 1048608 | tf_op jit(solution)/shard_map/ppermute | solution.py:317
  373.6 5.3 collective-permute-done.34.x3
  379.4 33.5 %collective-permute-done.9.x1 = bf16[2048,256]{1,0:T(8,128)(2,1)} collective-permute-done((bf16[2048,256]{1,0:T(8,128)(2,1)}, bf16[2048,256]{1,0:T(8,128)(2,1)}, u32[]{:S(2)}, u32[]{:S(2)}) %collective-permute-start.9) | collective-permute-done | bytes 1048608 | tf_op jit(solution)/shard_map/ppermute | solution.py:317
  413.4 5.8 collective-permute-done.11.x3
  423.3 57.0 %spread.3.second_w.refs_8_.refs_9_.refs_10_.refs_11_ = bf16[10,8192,128]{2,1,0:T(8,128)(2,1)} custom-call(bf16[11,2,32,32,256]{4,3,2,1,0:T(8,128)(2,1)} %bitcast.5, bf16[11,2,32,32,256]{4,3,2,1,0:T(8,128)(2,1)} %bitcast.6), custom_call_target="tpu_custom_call" | custom-call | flops 2500000000 | bytes 2500000 | tf_op jit(solution)/shard_map/spread/pallas_call | solution.py:136
  481.2 56.9 %spread.2.core_w.first_w = bf16[10,8192,128]{2,1,0:T(8,128)(2,1)} custom-call(bf16[11,2,32,32,256]{4,3,2,1,0:T(8,128)(2,1)} %bitcast.9, bf16[11,2,32,32,256]{4,3,2,1,0:T(8,128)(2,1)} %bitcast.10), custom_call_target="tpu_custom_call" | custom-call | flops 2500000000 | bytes 2500000 | tf_op jit(solution)/shard_map/spread/pallas_call | solution.py:136
  538.2 46.4 %middle.7.refs_0_.refs_1_.refs_2_.refs_3_ = bf16[8192,256]{1,0:T(8,128)(2,1)} custom-call(s32[1]{0:T(128)} %bitcast.chip_ref, bf16[2048,256]{1,0:T(8,128)(2,1)} %get-tuple-element.135.x0, bf16[2048,256]{1,0:T(8,128)(2,1)} %copy-done, bf16[2048,256]{1,0:T(8,128)(2,1)} %copy-done.1, bf16[2048,256]{1,0:T(8,128)(2,1)} %copy-done.2, ...), custom_call_target="tpu_custom_call" | custom-call | flops 3500000000 | bytes 3500000 | tf_op jit(solution)/shard_map/middle/pallas_call | solution.py:253
  584.9 46.2 %middle.6.refs_0_.refs_1_.refs_2_.refs_3_ = bf16[8192,256]{1,0:T(8,128)(2,1)} custom-call(s32[1]{0:T(128)} %bitcast.chip_ref, bf16[2048,256]{1,0:T(8,128)(2,1)} %get-tuple-element.118.x0, bf16[2048,256]{1,0:T(8,128)(2,1)} %collective-permute-done.49.x1, bf16[2048,256]{1,0:T(8,128)(2,1)} %collective-permute-done.50.x2, ...), custom_call_target="tpu_custom_call" | custom-call | flops 3500000000 | bytes 3500000 | tf_op jit(solution)/shard_map/middle/pallas_call | solution.py:253
  631.5 46.4 %middle.4.refs_0_.refs_1_.refs_2_.refs_3_ = bf16[8192,256]{1,0:T(8,128)(2,1)} custom-call(s32[1]{0:T(128)} %bitcast.chip_ref, bf16[2048,256]{1,0:T(8,128)(2,1)} %get-tuple-element.82.x0, bf16[2048,256]{1,0:T(8,128)(2,1)} %collective-permute-done.9.x1, bf16[2048,256]{1,0:T(8,128)(2,1)} %collective-permute-done.10.x2, ...), custom_call_target="tpu_custom_call" | custom-call | flops 3500000000 | bytes 3500000 | tf_op jit(solution)/shard_map/middle/pallas_call | solution.py:253
  680.3 46.3 %middle.5.refs_0_.refs_1_.refs_2_.refs_3_ = bf16[8192,256]{1,0:T(8,128)(2,1)} custom-call(s32[1]{0:T(128)} %bitcast.chip_ref, bf16[2048,256]{1,0:T(8,128)(2,1)} %get-tuple-element.101.x0, bf16[2048,256]{1,0:T(8,128)(2,1)} %collective-permute-done.32.x1, bf16[2048,256]{1,0:T(8,128)(2,1)} %collective-permute-done.33.x2, bf16[2048,256]{1,0:T(8,128)(2,1)} %copy-done.3, ...), custom_call_target="tpu_custom_call" | custom-call | flops 3500000000 | bytes 3500000 | tf_op jit(solution)/shard_map/middle/pallas_call | solution.py:253
  727.9 8.8 collective-permute-done.22
  736.8 8.8 collective-permute-done.24
  747.6 8.6 core_stage.7
  759.0 8.5 core_stage.6
  770.5 8.5 core_stage.4
  782.8 17.8 %collective-permute-done.74.x1 = bf16[2048,256]{1,0:T(8,128)(2,1)S(1)} collective-permute-done((bf16[2048,256]{1,0:T(8,128)(2,1)}, bf16[2048,256]{1,0:T(8,128)(2,1)S(1)}, u32[]{:S(2)}, u32[]{:S(2)}) %collective-permute-start.74) | collective-permute-done | bytes 1048608 | tf_op jit(solution)/shard_map/ppermute | solution.py:317
  805.6 8.5 core_stage.5
  817.9 9.6 collective-permute-done.57.x1
  828.4 39.6 %collective-permute-done.17.x1 = bf16[2048,256]{1,0:T(8,128)(2,1)} collective-permute-done((bf16[2048,256]{1,0:T(8,128)(2,1)}, bf16[2048,256]{1,0:T(8,128)(2,1)}, u32[]{:S(2)}, u32[]{:S(2)}) %collective-permute-start.17) | collective-permute-done | bytes 1048608 | tf_op jit(solution)/shard_map/ppermute | solution.py:317
  872.9 7.2 expand_pair.3
  882.6 9.3 chip_stages.9
  896.9 41.4 %collective-permute-start.27 = (bf16[2048,256]{1,0:T(8,128)(2,1)}, bf16[2048,256]{1,0:T(8,128)(2,1)S(1)}, u32[]{:S(2)}, u32[]{:S(2)}) collective-permute-start(bf16[2048,256]{1,0:T(8,128)(2,1)} %get-tuple-element.94), channel_id=1, source_target_pairs={{0,4},{1,5},{2,6},{3,7},{4,0},{5,1},{6,2},{7,3},{8,12},{9,13},{10,... | collective-permute-start | bytes 3145736 | tf_op jit(solution)/shard_map/ppermute | solution.py:317
  938.3 9.3 chip_stages.15
  947.6 9.3 chip_stages.11
  956.9 6.1 broadcast_in_dim.6
  968.6 9.3 chip_stages.13
  978.0 6.0 collective-permute-start.45
  988.6 20.0 %collective-permute-done.28 = bf16[2048,256]{1,0:T(8,128)(2,1)S(1)} collective-permute-done((bf16[2048,256]{1,0:T(8,128)(2,1)}, bf16[2048,256]{1,0:T(8,128)(2,1)S(1)}, u32[]{:S(2)}, u32[]{:S(2)}) %collective-permute-start.28) | collective-permute-done | bytes 1048608 | tf_op jit(solution)/shard_map/ppermute | solution.py:317
  1013.0 15.9 %collective-permute-start.62 = (bf16[2048,256]{1,0:T(8,128)(2,1)}, bf16[2048,256]{1,0:T(8,128)(2,1)S(1)}, u32[]{:S(2)}, u32[]{:S(2)}) collective-permute-start(bf16[2048,256]{1,0:T(8,128)(2,1)} %get-tuple-element.129), channel_id=1, source_target_pairs={{0,2},{1,3},{2,4},{3,5},{4,6},{5,7},{6,0},{7,1},{8,10},{9,11},{10,... | collective-permute-start | bytes 3145736 | tf_op jit(solution)/shard_map/ppermute | solution.py:317
  1034.9 18.6 %collective-permute-done.45 = bf16[2048,256]{1,0:T(8,128)(2,1)S(1)} collective-permute-done((bf16[2048,256]{1,0:T(8,128)(2,1)}, bf16[2048,256]{1,0:T(8,128)(2,1)S(1)}, u32[]{:S(2)}, u32[]{:S(2)}) %collective-permute-start.45) | collective-permute-done | bytes 1048608 | tf_op jit(solution)/shard_map/ppermute | solution.py:317
  1057.9 15.8 %collective-permute-start.79 = (bf16[2048,256]{1,0:T(8,128)(2,1)S(1)}, bf16[2048,256]{1,0:T(8,128)(2,1)S(1)}, u32[]{:S(2)}, u32[]{:S(2)}) collective-permute-start(bf16[2048,256]{1,0:T(8,128)(2,1)S(1)} %copy-done.28), channel_id=1, source_target_pairs={{0,2},{1,3},{2,4},{3,5},{4,6},{5,7},{6,0},{7,1},{8,10},{9,11},{10,... | collective-permute-start | bytes 3145736 | tf_op jit(solution)/shard_map/ppermute | solution.py:317
  1075.8 22.6 %collective-permute-done.62 = bf16[2048,256]{1,0:T(8,128)(2,1)S(1)} collective-permute-done((bf16[2048,256]{1,0:T(8,128)(2,1)}, bf16[2048,256]{1,0:T(8,128)(2,1)S(1)}, u32[]{:S(2)}, u32[]{:S(2)}) %collective-permute-start.62) | collective-permute-done | bytes 1048608 | tf_op jit(solution)/shard_map/ppermute | solution.py:317
  1102.6 17.3 %collective-permute-done.79 = bf16[2048,256]{1,0:T(8,128)(2,1)S(1)} collective-permute-done((bf16[2048,256]{1,0:T(8,128)(2,1)S(1)}, bf16[2048,256]{1,0:T(8,128)(2,1)S(1)}, u32[]{:S(2)}, u32[]{:S(2)}) %collective-permute-start.79) | collective-permute-done | bytes 1048608 | tf_op jit(solution)/shard_map/ppermute | solution.py:317
  (231 shorter events, 171.8 us)
Async XLA Ops:
  39.1 75.5 %collective-permute-start.63 = (bf16[2048,256]{1,0:T(8,128)(2,1)}, bf16[2048,256]{1,0:T(8,128)(2,1)}, u32[]{:S(2)}, u32[]{:S(2)}) collective-permute-start(bf16[2048,256]{1,0:T(8,128)(2,1)} %get-tuple-element.132), channel_id=1, source_target_pairs={{0,6},{1,7},{2,0},{3,1},{4,2},{5,3},{6,4},{7,5},{8,14},{9,15},{10,... | collective-permute-start | bytes 3145736 | tf_op jit(solution)/shard_map/ppermute | solution.py:317
  42.4 57.2 %collective-permute-start.3 = (bf16[1024,128]{1,0:T(8,128)(2,1)S(1)}, bf16[1024,128]{1,0:T(8,128)(2,1)}, u32[]{:S(2)}, u32[]{:S(2)}) collective-permute-start(bf16[1024,128]{1,0:T(8,128)(2,1)S(1)} %copy-done.25), channel_id=1, source_target_pairs={{0,6},{1,7},{2,0},{3,1},{4,2},{5,3},{6,4},{7,5},{8,14},{9,15},{10,... | collective-permute-start | bytes 786440 | tf_op jit(solution)/shard_map/ppermute | solution.py:317
  42.5 59.3 %collective-permute-start.5 = (bf16[1024,128]{1,0:T(8,128)(2,1)S(1)}, bf16[1024,128]{1,0:T(8,128)(2,1)}, u32[]{:S(2)}, u32[]{:S(2)}) collective-permute-start(bf16[1024,128]{1,0:T(8,128)(2,1)S(1)} %copy-done.23), channel_id=1, source_target_pairs={{0,4},{1,5},{2,6},{3,7},{4,0},{5,1},{6,2},{7,3},{8,12},{9,13},{10,... | collective-permute-start | bytes 786440 | tf_op jit(solution)/shard_map/ppermute | solution.py:317
  43.2 58.5 %collective-permute-start.21 = (bf16[1024,128]{1,0:T(8,128)(2,1)S(1)}, bf16[1024,128]{1,0:T(8,128)(2,1)S(1)}, u32[]{:S(2)}, u32[]{:S(2)}) collective-permute-start(bf16[1024,128]{1,0:T(8,128)(2,1)S(1)} %collective-permute-done.20), channel_id=1, source_target_pairs={{0,8},{8,0},{1,9},{9,1},{2,10},{10,2},{3,11},{11,3},{4,12},{12,4},... | collective-permute-start | bytes 786440 | tf_op jit(solution)/shard_map/ppermute | solution.py:353
  45.4 73.0 %collective-permute-start.64 = (bf16[2048,256]{1,0:T(8,128)(2,1)}, bf16[2048,256]{1,0:T(8,128)(2,1)}, u32[]{:S(2)}, u32[]{:S(2)}) collective-permute-start(bf16[2048,256]{1,0:T(8,128)(2,1)} %get-tuple-element.133), channel_id=1, source_target_pairs={{0,4},{1,5},{2,6},{3,7},{4,0},{5,1},{6,2},{7,3},{8,12},{9,13},{10,... | collective-permute-start | bytes 3145736 | tf_op jit(solution)/shard_map/ppermute | solution.py:317
  114.7 85.5 %collective-permute-start.48 = (bf16[2048,256]{1,0:T(8,128)(2,1)}, bf16[2048,256]{1,0:T(8,128)(2,1)}, u32[]{:S(2)}, u32[]{:S(2)}) collective-permute-start(bf16[2048,256]{1,0:T(8,128)(2,1)} %get-tuple-element.117), channel_id=1, source_target_pairs={{0,2},{1,3},{2,4},{3,5},{4,6},{5,7},{6,0},{7,1},{8,10},{9,11},{10,... | collective-permute-start | bytes 3145736 | tf_op jit(solution)/shard_map/ppermute | solution.py:317
  118.3 85.1 %collective-permute-start.29 = (bf16[2048,256]{1,0:T(8,128)(2,1)}, bf16[2048,256]{1,0:T(8,128)(2,1)}, u32[]{:S(2)}, u32[]{:S(2)}) collective-permute-start(bf16[2048,256]{1,0:T(8,128)(2,1)} %get-tuple-element.98), channel_id=1, source_target_pairs={{0,6},{1,7},{2,0},{3,1},{4,2},{5,3},{6,4},{7,5},{8,14},{9,15},{10,... | collective-permute-start | bytes 3145736 | tf_op jit(solution)/shard_map/ppermute | solution.py:317
  155.2 65.5 %collective-permute-start.30 = (bf16[2048,256]{1,0:T(8,128)(2,1)}, bf16[2048,256]{1,0:T(8,128)(2,1)S(1)}, u32[]{:S(2)}, u32[]{:S(2)}) collective-permute-start(bf16[2048,256]{1,0:T(8,128)(2,1)} %get-tuple-element.99), channel_id=1, source_target_pairs={{0,4},{1,5},{2,6},{3,7},{4,0},{5,1},{6,2},{7,3},{8,12},{9,13},{10,... | collective-permute-start | bytes 3145736 | tf_op jit(solution)/shard_map/ppermute | solution.py:317
  158.6 86.5 %collective-permute-start.31 = (bf16[2048,256]{1,0:T(8,128)(2,1)S(1)}, bf16[2048,256]{1,0:T(8,128)(2,1)}, u32[]{:S(2)}, u32[]{:S(2)}) collective-permute-start(bf16[2048,256]{1,0:T(8,128)(2,1)S(1)} %get-tuple-element.100), channel_id=1, source_target_pairs={{0,2},{1,3},{2,4},{3,5},{4,6},{5,7},{6,0},{7,1},{8,10},{9,11},{10,... | collective-permute-start | bytes 3145736 | tf_op jit(solution)/shard_map/ppermute | solution.py:317
  158.6 89.7 %collective-permute-start = (bf16[2048,256]{1,0:T(8,128)(2,1)S(1)}, bf16[2048,256]{1,0:T(8,128)(2,1)}, u32[]{:S(2)}, u32[]{:S(2)}) collective-permute-start(bf16[2048,256]{1,0:T(8,128)(2,1)S(1)} %get-tuple-element.77), channel_id=1, source_target_pairs={{0,6},{1,7},{2,0},{3,1},{4,2},{5,3},{6,4},{7,5},{8,14},{9,15},{10,... | collective-permute-start | bytes 3145736 | tf_op jit(solution)/shard_map/ppermute | solution.py:317
  203.5 58.3 %collective-permute-start.2 = (bf16[2048,256]{1,0:T(8,128)(2,1)}, bf16[2048,256]{1,0:T(8,128)(2,1)}, u32[]{:S(2)}, u32[]{:S(2)}) collective-permute-start(bf16[2048,256]{1,0:T(8,128)(2,1)} %get-tuple-element.79), channel_id=1, source_target_pairs={{0,2},{1,3},{2,4},{3,5},{4,6},{5,7},{6,0},{7,1},{8,10},{9,11},{10,... | collective-permute-start | bytes 3145736 | tf_op jit(solution)/shard_map/ppermute | solution.py:317
  248.2 62.1 %collective-permute-start.68 = (bf16[2048,256]{1,0:T(8,128)(2,1)}, bf16[2048,256]{1,0:T(8,128)(2,1)S(1)}, u32[]{:S(2)}, u32[]{:S(2)}) collective-permute-start(bf16[2048,256]{1,0:T(8,128)(2,1)} %get-tuple-element.138), channel_id=1, source_target_pairs={{0,2},{1,3},{2,4},{3,5},{4,6},{5,7},{6,0},{7,1},{8,10},{9,11},{10,... | collective-permute-start | bytes 3145736 | tf_op jit(solution)/shard_map/ppermute | solution.py:317
  248.2 71.8 %collective-permute-start.69 = (bf16[2048,256]{1,0:T(8,128)(2,1)}, bf16[2048,256]{1,0:T(8,128)(2,1)}, u32[]{:S(2)}, u32[]{:S(2)}) collective-permute-start(bf16[2048,256]{1,0:T(8,128)(2,1)} %get-tuple-element.135.x0), channel_id=1, source_target_pairs={{0,1},{1,0},{2,3},{3,2},{4,5},{5,4},{6,7},{7,6},{8,9},{9,8},{10,11... | collective-permute-start | bytes 3145736 | tf_op jit(solution)/shard_map/ppermute | solution.py:320
  261.7 62.4 %collective-permute-start.49 = (bf16[2048,256]{1,0:T(8,128)(2,1)}, bf16[2048,256]{1,0:T(8,128)(2,1)}, u32[]{:S(2)}, u32[]{:S(2)}) collective-permute-start(bf16[2048,256]{1,0:T(8,128)(2,1)} %get-tuple-element.119), channel_id=1, source_target_pairs={{0,6},{1,7},{2,0},{3,1},{4,2},{5,3},{6,4},{7,5},{8,14},{9,15},{10,... | collective-permute-start | bytes 3145736 | tf_op jit(solution)/shard_map/ppermute | solution.py:317
  272.0 61.4 %collective-permute-start.50 = (bf16[2048,256]{1,0:T(8,128)(2,1)}, bf16[2048,256]{1,0:T(8,128)(2,1)}, u32[]{:S(2)}, u32[]{:S(2)}) collective-permute-start(bf16[2048,256]{1,0:T(8,128)(2,1)} %get-tuple-element.120), channel_id=1, source_target_pairs={{0,4},{1,5},{2,6},{3,7},{4,0},{5,1},{6,2},{7,3},{8,12},{9,13},{10,... | collective-permute-start | bytes 3145736 | tf_op jit(solution)/shard_map/ppermute | solution.py:317
  279.8 58.3 %collective-permute-start.51 = (bf16[2048,256]{1,0:T(8,128)(2,1)}, bf16[2048,256]{1,0:T(8,128)(2,1)}, u32[]{:S(2)}, u32[]{:S(2)}) collective-permute-start(bf16[2048,256]{1,0:T(8,128)(2,1)} %get-tuple-element.121), channel_id=1, source_target_pairs={{0,2},{1,3},{2,4},{3,5},{4,6},{5,7},{6,0},{7,1},{8,10},{9,11},{10,... | collective-permute-start | bytes 3145736 | tf_op jit(solution)/shard_map/ppermute | solution.py:317
  338.1 74.9 %collective-permute-start.9 = (bf16[2048,256]{1,0:T(8,128)(2,1)}, bf16[2048,256]{1,0:T(8,128)(2,1)}, u32[]{:S(2)}, u32[]{:S(2)}) collective-permute-start(bf16[2048,256]{1,0:T(8,128)(2,1)} %get-tuple-element.83), channel_id=1, source_target_pairs={{0,6},{1,7},{2,0},{3,1},{4,2},{5,3},{6,4},{7,5},{8,14},{9,15},{10,... | collective-permute-start | bytes 3145736 | tf_op jit(solution)/shard_map/ppermute | solution.py:317
  419.3 61.0 %collective-permute-start.54 = (bf16[2048,256]{1,0:T(8,128)(2,1)}, bf16[2048,256]{1,0:T(8,128)(2,1)}, u32[]{:S(2)}, u32[]{:S(2)}) collective-permute-start(bf16[2048,256]{1,0:T(8,128)(2,1)} %collective-permute-done.50.x2), channel_id=1, source_target_pairs={{0,1},{1,0},{2,3},{3,2},{4,5},{5,4},{6,7},{7,6},{8,9},{9,8},{10,11... | collective-permute-start | bytes 3145736 | tf_op jit(solution)/shard_map/ppermute | solution.py:320
  419.8 60.9 %collective-permute-start.55 = (bf16[2048,256]{1,0:T(8,128)(2,1)}, bf16[2048,256]{1,0:T(8,128)(2,1)}, u32[]{:S(2)}, u32[]{:S(2)}) collective-permute-start(bf16[2048,256]{1,0:T(8,128)(2,1)} %collective-permute-done.51.x3), channel_id=1, source_target_pairs={{0,1},{1,0},{2,3},{3,2},{4,5},{5,4},{6,7},{7,6},{8,9},{9,8},{10,11... | collective-permute-start | bytes 3145736 | tf_op jit(solution)/shard_map/ppermute | solution.py:320
  419.9 61.0 %collective-permute-start.13 = (bf16[2048,256]{1,0:T(8,128)(2,1)}, bf16[2048,256]{1,0:T(8,128)(2,1)}, u32[]{:S(2)}, u32[]{:S(2)}) collective-permute-start(bf16[2048,256]{1,0:T(8,128)(2,1)} %collective-permute-done.9.x1), channel_id=1, source_target_pairs={{0,1},{1,0},{2,3},{3,2},{4,5},{5,4},{6,7},{7,6},{8,9},{9,8},{10,11... | collective-permute-start | bytes 3145736 | tf_op jit(solution)/shard_map/ppermute | solution.py:320
  420.3 164.3 %collective-permute-start.14 = (bf16[2048,256]{1,0:T(8,128)(2,1)}, bf16[2048,256]{1,0:T(8,128)(2,1)}, u32[]{:S(2)}, u32[]{:S(2)}) collective-permute-start(bf16[2048,256]{1,0:T(8,128)(2,1)} %collective-permute-done.10.x2), channel_id=1, source_target_pairs={{0,1},{1,0},{2,3},{3,2},{4,5},{5,4},{6,7},{7,6},{8,9},{9,8},{10,11... | collective-permute-start | bytes 3145736 | tf_op jit(solution)/shard_map/ppermute | solution.py:320
  423.1 208.0 %collective-permute-start.15 = (bf16[2048,256]{1,0:T(8,128)(2,1)}, bf16[2048,256]{1,0:T(8,128)(2,1)}, u32[]{:S(2)}, u32[]{:S(2)}) collective-permute-start(bf16[2048,256]{1,0:T(8,128)(2,1)} %collective-permute-done.11.x3), channel_id=1, source_target_pairs={{0,1},{1,0},{2,3},{3,2},{4,5},{5,4},{6,7},{7,6},{8,9},{9,8},{10,11... | collective-permute-start | bytes 3145736 | tf_op jit(solution)/shard_map/ppermute | solution.py:320
  480.3 197.7 %collective-permute-start.36 = (bf16[2048,256]{1,0:T(8,128)(2,1)}, bf16[2048,256]{1,0:T(8,128)(2,1)S(1)}, u32[]{:S(2)}, u32[]{:S(2)}) collective-permute-start(bf16[2048,256]{1,0:T(8,128)(2,1)} %collective-permute-done.32.x1), channel_id=1, source_target_pairs={{0,1},{1,0},{2,3},{3,2},{4,5},{5,4},{6,7},{7,6},{8,9},{9,8},{10,11... | collective-permute-start | bytes 3145736 | tf_op jit(solution)/shard_map/ppermute | solution.py:320
  480.7 197.5 %collective-permute-start.37 = (bf16[2048,256]{1,0:T(8,128)(2,1)}, bf16[2048,256]{1,0:T(8,128)(2,1)S(1)}, u32[]{:S(2)}, u32[]{:S(2)}) collective-permute-start(bf16[2048,256]{1,0:T(8,128)(2,1)} %collective-permute-done.33.x2), channel_id=1, source_target_pairs={{0,1},{1,0},{2,3},{3,2},{4,5},{5,4},{6,7},{7,6},{8,9},{9,8},{10,11... | collective-permute-start | bytes 3145736 | tf_op jit(solution)/shard_map/ppermute | solution.py:320
  480.9 197.4 %collective-permute-start.38 = (bf16[2048,256]{1,0:T(8,128)(2,1)}, bf16[2048,256]{1,0:T(8,128)(2,1)S(1)}, u32[]{:S(2)}, u32[]{:S(2)}) collective-permute-start(bf16[2048,256]{1,0:T(8,128)(2,1)} %copy-done.3), channel_id=1, source_target_pairs={{0,1},{1,0},{2,3},{3,2},{4,5},{5,4},{6,7},{7,6},{8,9},{9,8},{10,11... | collective-permute-start | bytes 3145736 | tf_op jit(solution)/shard_map/ppermute | solution.py:320
  584.6 162.7 %collective-permute-start.73 = (bf16[8192,256]{1,0:T(8,128)(2,1)}, bf16[8192,256]{1,0:T(8,128)(2,1)}, u32[]{:S(2)}, u32[]{:S(2)}) collective-permute-start(bf16[8192,256]{1,0:T(8,128)(2,1)} %middle.7.refs_0_.refs_1_.refs_2_.refs_3_), channel_id=1, source_target_pairs={{0,1},{1,0},{2,3},{3,2},{4,5},{5,4},{6,7},{7,6},{8,9},{9,8},{10,11... | collective-permute-start | bytes 12582920 | tf_op jit(solution)/shard_map/ppermute | solution.py:320
  631.1 127.6 %collective-permute-start.56 = (bf16[8192,256]{1,0:T(8,128)(2,1)}, bf16[8192,256]{1,0:T(8,128)(2,1)}, u32[]{:S(2)}, u32[]{:S(2)}) collective-permute-start(bf16[8192,256]{1,0:T(8,128)(2,1)} %middle.6.refs_0_.refs_1_.refs_2_.refs_3_), channel_id=1, source_target_pairs={{0,1},{1,0},{2,3},{3,2},{4,5},{5,4},{6,7},{7,6},{8,9},{9,8},{10,11... | collective-permute-start | bytes 12582920 | tf_op jit(solution)/shard_map/ppermute | solution.py:320
  677.9 89.6 %collective-permute-start.16 = (bf16[8192,256]{1,0:T(8,128)(2,1)}, bf16[8192,256]{1,0:T(8,128)(2,1)}, u32[]{:S(2)}, u32[]{:S(2)}) collective-permute-start(bf16[8192,256]{1,0:T(8,128)(2,1)} %middle.4.refs_0_.refs_1_.refs_2_.refs_3_), channel_id=1, source_target_pairs={{0,1},{1,0},{2,3},{3,2},{4,5},{5,4},{6,7},{7,6},{8,9},{9,8},{10,11... | collective-permute-start | bytes 12582920 | tf_op jit(solution)/shard_map/ppermute | solution.py:320
  758.7 55.5 %collective-permute-start.76 = (bf16[2048,256]{1,0:T(8,128)(2,1)}, bf16[2048,256]{1,0:T(8,128)(2,1)}, u32[]{:S(2)}, u32[]{:S(2)}) collective-permute-start(bf16[2048,256]{1,0:T(8,128)(2,1)} %get-tuple-element.142), channel_id=1, source_target_pairs={{0,2},{1,3},{2,4},{3,5},{4,6},{5,7},{6,0},{7,1},{8,10},{9,11},{10,... | collective-permute-start | bytes 3145736 | tf_op jit(solution)/shard_map/ppermute | solution.py:317
  767.5 60.0 %collective-permute-start.57 = (bf16[2048,256]{1,0:T(8,128)(2,1)}, bf16[2048,256]{1,0:T(8,128)(2,1)S(1)}, u32[]{:S(2)}, u32[]{:S(2)}) collective-permute-start(bf16[2048,256]{1,0:T(8,128)(2,1)} %get-tuple-element.123), channel_id=1, source_target_pairs={{0,6},{1,7},{2,0},{3,1},{4,2},{5,3},{6,4},{7,5},{8,14},{9,15},{10,... | collective-permute-start | bytes 3145736 | tf_op jit(solution)/shard_map/ppermute | solution.py:317
  779.1 88.9 %collective-permute-start.17 = (bf16[2048,256]{1,0:T(8,128)(2,1)}, bf16[2048,256]{1,0:T(8,128)(2,1)}, u32[]{:S(2)}, u32[]{:S(2)}) collective-permute-start(bf16[2048,256]{1,0:T(8,128)(2,1)} %get-tuple-element.87), channel_id=1, source_target_pairs={{0,6},{1,7},{2,0},{3,1},{4,2},{5,3},{6,4},{7,5},{8,14},{9,15},{10,... | collective-permute-start | bytes 3145736 | tf_op jit(solution)/shard_map/ppermute | solution.py:317
  800.6 79.4 %collective-permute-start.18 = (bf16[2048,256]{1,0:T(8,128)(2,1)}, bf16[2048,256]{1,0:T(8,128)(2,1)}, u32[]{:S(2)}, u32[]{:S(2)}) collective-permute-start(bf16[2048,256]{1,0:T(8,128)(2,1)} %get-tuple-element.88), channel_id=1, source_target_pairs={{0,4},{1,5},{2,6},{3,7},{4,0},{5,1},{6,2},{7,3},{8,12},{9,13},{10,... | collective-permute-start | bytes 3145736 | tf_op jit(solution)/shard_map/ppermute | solution.py:317
  802.9 79.7 %collective-permute-start.19 = (bf16[2048,256]{1,0:T(8,128)(2,1)}, bf16[2048,256]{1,0:T(8,128)(2,1)}, u32[]{:S(2)}, u32[]{:S(2)}) collective-permute-start(bf16[2048,256]{1,0:T(8,128)(2,1)} %get-tuple-element.89), channel_id=1, source_target_pairs={{0,2},{1,3},{2,4},{3,5},{4,6},{5,7},{6,0},{7,1},{8,10},{9,11},{10,... | collective-permute-start | bytes 3145736 | tf_op jit(solution)/shard_map/ppermute | solution.py:317
  814.2 80.8 %collective-permute-start.40 = (bf16[2048,256]{1,0:T(8,128)(2,1)}, bf16[2048,256]{1,0:T(8,128)(2,1)S(1)}, u32[]{:S(2)}, u32[]{:S(2)}) collective-permute-start(bf16[2048,256]{1,0:T(8,128)(2,1)} %get-tuple-element.106), channel_id=1, source_target_pairs={{0,6},{1,7},{2,0},{3,1},{4,2},{5,3},{6,4},{7,5},{8,14},{9,15},{10,... | collective-permute-start | bytes 3145736 | tf_op jit(solution)/shard_map/ppermute | solution.py:317
  827.5 67.8 %collective-permute-start.41 = (bf16[2048,256]{1,0:T(8,128)(2,1)}, bf16[2048,256]{1,0:T(8,128)(2,1)S(1)}, u32[]{:S(2)}, u32[]{:S(2)}) collective-permute-start(bf16[2048,256]{1,0:T(8,128)(2,1)} %get-tuple-element.107), channel_id=1, source_target_pairs={{0,4},{1,5},{2,6},{3,7},{4,0},{5,1},{6,2},{7,3},{8,12},{9,13},{10,... | collective-permute-start | bytes 3145736 | tf_op jit(solution)/shard_map/ppermute | solution.py:317
  868.0 70.3 %collective-permute-start.42 = (bf16[2048,256]{1,0:T(8,128)(2,1)}, bf16[2048,256]{1,0:T(8,128)(2,1)}, u32[]{:S(2)}, u32[]{:S(2)}) collective-permute-start(bf16[2048,256]{1,0:T(8,128)(2,1)} %get-tuple-element.108), channel_id=1, source_target_pairs={{0,2},{1,3},{2,4},{3,5},{4,6},{5,7},{6,0},{7,1},{8,10},{9,11},{10,... | collective-permute-start | bytes 3145736 | tf_op jit(solution)/shard_map/ppermute | solution.py:317
  880.0 85.4 %collective-permute-start.58 = (bf16[2048,256]{1,0:T(8,128)(2,1)}, bf16[2048,256]{1,0:T(8,128)(2,1)}, u32[]{:S(2)}, u32[]{:S(2)}) collective-permute-start(bf16[2048,256]{1,0:T(8,128)(2,1)} %get-tuple-element.124), channel_id=1, source_target_pairs={{0,4},{1,5},{2,6},{3,7},{4,0},{5,1},{6,2},{7,3},{8,12},{9,13},{10,... | collective-permute-start | bytes 3145736 | tf_op jit(solution)/shard_map/ppermute | solution.py:317
  882.6 86.1 %collective-permute-start.59 = (bf16[2048,256]{1,0:T(8,128)(2,1)}, bf16[2048,256]{1,0:T(8,128)(2,1)}, u32[]{:S(2)}, u32[]{:S(2)}) collective-permute-start(bf16[2048,256]{1,0:T(8,128)(2,1)} %get-tuple-element.125), channel_id=1, source_target_pairs={{0,2},{1,3},{2,4},{3,5},{4,6},{5,7},{6,0},{7,1},{8,10},{9,11},{10,... | collective-permute-start | bytes 3145736 | tf_op jit(solution)/shard_map/ppermute | solution.py:317
  894.9 83.0 %collective-permute-start.26 = (bf16[2048,256]{1,0:T(8,128)(2,1)}, bf16[2048,256]{1,0:T(8,128)(2,1)}, u32[]{:S(2)}, u32[]{:S(2)}) collective-permute-start(bf16[2048,256]{1,0:T(8,128)(2,1)} %get-tuple-element.93), channel_id=1, source_target_pairs={{0,6},{1,7},{2,0},{3,1},{4,2},{5,3},{6,4},{7,5},{8,14},{9,15},{10,... | collective-permute-start | bytes 3145736 | tf_op jit(solution)/shard_map/ppermute | solution.py:317
  896.9 89.3 %collective-permute-start.27 = (bf16[2048,256]{1,0:T(8,128)(2,1)}, bf16[2048,256]{1,0:T(8,128)(2,1)S(1)}, u32[]{:S(2)}, u32[]{:S(2)}) collective-permute-start(bf16[2048,256]{1,0:T(8,128)(2,1)} %get-tuple-element.94), channel_id=1, source_target_pairs={{0,4},{1,5},{2,6},{3,7},{4,0},{5,1},{6,2},{7,3},{8,12},{9,13},{10,... | collective-permute-start | bytes 3145736 | tf_op jit(solution)/shard_map/ppermute | solution.py:317
  938.3 70.3 %collective-permute-start.28 = (bf16[2048,256]{1,0:T(8,128)(2,1)}, bf16[2048,256]{1,0:T(8,128)(2,1)S(1)}, u32[]{:S(2)}, u32[]{:S(2)}) collective-permute-start(bf16[2048,256]{1,0:T(8,128)(2,1)} %get-tuple-element.95), channel_id=1, source_target_pairs={{0,2},{1,3},{2,4},{3,5},{4,6},{5,7},{6,0},{7,1},{8,10},{9,11},{10,... | collective-permute-start | bytes 3145736 | tf_op jit(solution)/shard_map/ppermute | solution.py:317
  968.6 62.5 %collective-permute-start.44 = (bf16[2048,256]{1,0:T(8,128)(2,1)}, bf16[2048,256]{1,0:T(8,128)(2,1)}, u32[]{:S(2)}, u32[]{:S(2)}) collective-permute-start(bf16[2048,256]{1,0:T(8,128)(2,1)} %get-tuple-element.111), channel_id=1, source_target_pairs={{0,4},{1,5},{2,6},{3,7},{4,0},{5,1},{6,2},{7,3},{8,12},{9,13},{10,... | collective-permute-start | bytes 3145736 | tf_op jit(solution)/shard_map/ppermute | solution.py:317
  978.0 75.5 %collective-permute-start.45 = (bf16[2048,256]{1,0:T(8,128)(2,1)}, bf16[2048,256]{1,0:T(8,128)(2,1)S(1)}, u32[]{:S(2)}, u32[]{:S(2)}) collective-permute-start(bf16[2048,256]{1,0:T(8,128)(2,1)} %get-tuple-element.112), channel_id=1, source_target_pairs={{0,2},{1,3},{2,4},{3,5},{4,6},{5,7},{6,0},{7,1},{8,10},{9,11},{10,... | collective-permute-start | bytes 3145736 | tf_op jit(solution)/shard_map/ppermute | solution.py:317
  986.2 71.6 %collective-permute-start.60 = (bf16[2048,256]{1,0:T(8,128)(2,1)}, bf16[2048,256]{1,0:T(8,128)(2,1)S(1)}, u32[]{:S(2)}, u32[]{:S(2)}) collective-permute-start(bf16[2048,256]{1,0:T(8,128)(2,1)} %get-tuple-element.127), channel_id=1, source_target_pairs={{0,6},{1,7},{2,0},{3,1},{4,2},{5,3},{6,4},{7,5},{8,14},{9,15},{10,... | collective-permute-start | bytes 3145736 | tf_op jit(solution)/shard_map/ppermute | solution.py:317
  1008.6 66.1 %collective-permute-start.61 = (bf16[2048,256]{1,0:T(8,128)(2,1)}, bf16[2048,256]{1,0:T(8,128)(2,1)S(1)}, u32[]{:S(2)}, u32[]{:S(2)}) collective-permute-start(bf16[2048,256]{1,0:T(8,128)(2,1)} %get-tuple-element.128), channel_id=1, source_target_pairs={{0,4},{1,5},{2,6},{3,7},{4,0},{5,1},{6,2},{7,3},{8,12},{9,13},{10,... | collective-permute-start | bytes 3145736 | tf_op jit(solution)/shard_map/ppermute | solution.py:317
  1013.0 85.4 %collective-permute-start.62 = (bf16[2048,256]{1,0:T(8,128)(2,1)}, bf16[2048,256]{1,0:T(8,128)(2,1)S(1)}, u32[]{:S(2)}, u32[]{:S(2)}) collective-permute-start(bf16[2048,256]{1,0:T(8,128)(2,1)} %get-tuple-element.129), channel_id=1, source_target_pairs={{0,2},{1,3},{2,4},{3,5},{4,6},{5,7},{6,0},{7,1},{8,10},{9,11},{10,... | collective-permute-start | bytes 3145736 | tf_op jit(solution)/shard_map/ppermute | solution.py:317
  1031.1 69.3 %collective-permute-start.77 = (bf16[2048,256]{1,0:T(8,128)(2,1)}, bf16[2048,256]{1,0:T(8,128)(2,1)S(1)}, u32[]{:S(2)}, u32[]{:S(2)}) collective-permute-start(bf16[2048,256]{1,0:T(8,128)(2,1)} %get-tuple-element.144), channel_id=1, source_target_pairs={{0,6},{1,7},{2,0},{3,1},{4,2},{5,3},{6,4},{7,5},{8,14},{9,15},{10,... | collective-permute-start | bytes 3145736 | tf_op jit(solution)/shard_map/ppermute | solution.py:317
  1057.9 62.0 %collective-permute-start.79 = (bf16[2048,256]{1,0:T(8,128)(2,1)S(1)}, bf16[2048,256]{1,0:T(8,128)(2,1)S(1)}, u32[]{:S(2)}, u32[]{:S(2)}) collective-permute-start(bf16[2048,256]{1,0:T(8,128)(2,1)S(1)} %copy-done.28), channel_id=1, source_target_pairs={{0,2},{1,3},{2,4},{3,5},{4,6},{5,7},{6,0},{7,1},{8,10},{9,11},{10,... | collective-permute-start | bytes 3145736 | tf_op jit(solution)/shard_map/ppermute | solution.py:317
  (61 other events, 2266.6 us)

commit v2 on v1

--- a/solution.py
+++ b/solution.py
@@ -11,6 +11,7 @@
 CORES = 2
 CHIPS = 4
 LANES = 128
+PAD = 8
 BF16 = jnp.bfloat16
 F32 = jnp.float32
 
@@ -30,6 +31,15 @@
 def turned(refs, i, sel):
     wide = jnp.concatenate([ref[0, slot, i] for ref in refs for slot in range(2)], axis=0)
     return lax.dot_general(wide, sel, (((0,), (0,)), ((), ())), preferred_element_type=F32)
+
+
+def unpad(tmp, out, pitch, blk):
+    @pl.loop(0, tmp.shape[0] // (pitch * 8))
+    def _(it):
+        for u in range(8):
+            b = it * 8 + u
+            src = pl.ds(pl.multiple_of(b * pitch, 8), blk)
+            out[pl.ds(pl.multiple_of(b * blk, blk), blk), :] = tmp[src, :].astype(BF16)
 
 
 def pack_kernel(a_ref, b_ref, out_ref, tmp):
@@ -42,9 +52,9 @@
     def _(it):
         for u in range(4):
             i = it * 4 + u
-            tmp[pl.ds(i, blocks, stride=blk), :] = turned((a_ref, b_ref), i, sel)
-
-    out_ref[...] = tmp[...].astype(BF16)
+            tmp[pl.ds(i, blocks, stride=blk + PAD), :] = turned((a_ref, b_ref), i, sel)
+
+    unpad(tmp, out_ref, blk + PAD, blk)
 
 
 def pack_pair(turned_w, hi, lo):
@@ -56,7 +66,7 @@
         in_specs=[spec(hi), spec(lo)],
         out_specs=pl.BlockSpec((blocks * blk, LANES), lambda i: (0, 0)),
         out_shape=jax.ShapeDtypeStruct((blocks * blk, LANES), BF16),
-        scratch_shapes=[pltpu.VMEM((blocks * blk, LANES), F32)],
+        scratch_shapes=[pltpu.VMEM((blocks * (blk + PAD), LANES), F32)],
         compiler_params=params(),
         cost_estimate=cost(5),
         name="pack_pair",
@@ -117,10 +127,10 @@
             for half, (mate, tmp) in enumerate(zip(mates, (tmp_a, tmp_b))):
                 both = wide[:, 2 * half * LANES : 2 * (half + 1) * LANES]
                 val = jnp.where(group == own, both[:, :LANES], jnp.where(group == mate, both[:, LANES:], 0.0))
-                tmp[pl.ds(it * 8 + u, blocks, stride=blk), :] = val
-
-    out_ref[0] = tmp_a[...].astype(BF16)
-    out_ref[1] = tmp_b[...].astype(BF16)
+                tmp[pl.ds(it * 8 + u, blocks, stride=blk + PAD), :] = val
+
+    unpad(tmp_a, out_ref.at[0], blk + PAD, blk)
+    unpad(tmp_b, out_ref.at[1], blk + PAD, blk)
 
 
 def spread(turned_w, first_map):
@@ -139,7 +149,7 @@
         in_specs=[spec(a_at), spec(b_at)],
         out_specs=pl.BlockSpec((2, rows, LANES), lambda i: (i, 0, 0)),
         out_shape=jax.ShapeDtypeStruct((10, rows, LANES), BF16),
-        scratch_shapes=[pltpu.VMEM((rows, LANES), F32)] * 2,
+        scratch_shapes=[pltpu.VMEM((blocks * (blk + PAD), LANES), F32)] * 2,
         compiler_params=params(),
         cost_estimate=cost(25),
         name="spread",
@@ -363,9 +373,12 @@
 
         result = jnp.zeros((rows, channels), BF16)
         for c in range(chunks):
-            parts = [quarter(signal, r, c * width, width) for r in range(CHIPS)]
+            far = quarter(signal, 2, c * width, width)
+            signal, far = lax.optimization_barrier((signal, far))
+            far = to_chip(far, 2)
+            parts = [quarter(signal, r, c * width, width) for r in (0, 1, 3)]
             signal, parts = lax.optimization_barrier((signal, parts))
-            parts = swap(parts)
+            parts = [parts[0], to_chip(parts[2], 3), far, to_chip(parts[1], 1)]
             parts = chip_stages(parts, hi_first, lo_first, blk)
             parts = swap(parts)
             mates = [to_core(p) for p in parts]

time: 1120 us -> 1070 us (0.955)
  Pallas kernels: 437 us -> 372 us
  waiting for transfers between devices: 441 us -> 459 us
  starting transfers between devices: 171 us -> 154 us
    pallas_call x2, Pallas kernels: 114 us -> 52.5 us  [spread(): pl.pallas_call(functools.partial(spread_kernel, first_map), grid=(5,), in...]
    ppermute x54, waiting for transfers between devices: 433 us -> 451 us  [to_chip(): return lax.ppermute(value, 'sp', pairs)]
    ppermute x54, starting transfers between devices: 158 us -> 142 us  [to_chip(): return lax.ppermute(value, 'sp', pairs)]
    dynamic_slice x6 -> x10, local copies, waits for them, and re-layouts: 20.3 us -> 25.6 us  [quarter(): return lax.dynamic_slice(array, (start, col), (group, wide))]
  transfers between devices with their start and end apart: 80 -> 80, of which waited for: 30 -> 33; matrix products, arithmetic and copies ran while one was open for 6% -> 6% of each run, Pallas kernels for 38% -> 35%
where the time goes in v2:
time: 1070 us; the launch traced here: 1060 us
  waiting for transfers between devices  459 us (43%)
  Pallas kernels  372 us (35%)
  starting transfers between devices  154 us (14%)
  local copies, waits for them, and re-layouts  66.3 us (6%)
    ppermute x54, waiting for transfers between devices, to_chip(): return lax.ppermute(value, 'sp', pairs)  451 us
    pallas_call x4, Pallas kernels, middle(): pl.pallas_call(functools.partial(middle_kernel, blk), grid_spec=pltpu.Pre...  185 us
    ppermute x54, starting transfers between devices, to_chip(): return lax.ppermute(value, 'sp', pairs)  142 us
    pallas_call x8, Pallas kernels, chip_stages(): pl.pallas_call(functools.partial(chip_kernel, blk), grid=(rows // tile,),...  74.8 us
    pallas_call x2, Pallas kernels, spread(): pl.pallas_call(functools.partial(spread_kernel, first_map), grid=(5,), in...  52.5 us
    pallas_call x4, Pallas kernels, core_stage(): pl.pallas_call(functools.partial(core_kernel, blk), grid_spec=pltpu.Prefe...  34 us
    dynamic_slice x10, local copies, waits for them, and re-layouts, quarter(): return lax.dynamic_slice(array, (start, col), (group, wide))  25.6 us
    dynamic_update_slice x16, local copies, waits for them, and re-layouts, device_program(): result = lax.dynamic_update_slice(result, parts[r], at)  24 us
  transfers between devices with their start and end apart: 80, of which 33 were waited for; matrix products, arithmetic and copies ran while one was open for 6% of the time, Pallas kernels for 35%

profile of v2, /device:TPU:112, one launch (start us, length us, event | category | flops | bytes accessed | tf_op | source)
XLA Modules:
  0.0 1062.3 jit_solution(12421586544648944114)
XLA Ops:
  47.9 29.3 %collective-permute-done.3 = bf16[1024,128]{1,0:T(8,128)(2,1)} collective-permute-done((bf16[1024,128]{1,0:T(8,128)(2,1)}, bf16[1024,128]{1,0:T(8,128)(2,1)}, u32[]{:S(2)}, u32[]{:S(2)}) %collective-permute-start.3) | collective-permute-done | bytes 262176 | tf_op jit(solution)/shard_map/ppermute | solution.py:327
  101.8 11.2 %collective-permute-done.64.x2 = bf16[2048,256]{1,0:T(8,128)(2,1)} collective-permute-done((bf16[2048,256]{1,0:T(8,128)(2,1)}, bf16[2048,256]{1,0:T(8,128)(2,1)}, u32[]{:S(2)}, u32[]{:S(2)}) %collective-permute-start.64) | collective-permute-done | bytes 1048608 | tf_op jit(solution)/shard_map/ppermute | solution.py:327
  115.1 22.5 %collective-permute-done.46.x1 = bf16[2048,256]{1,0:T(8,128)(2,1)} collective-permute-done((bf16[2048,256]{1,0:T(8,128)(2,1)}, bf16[2048,256]{1,0:T(8,128)(2,1)}, u32[]{:S(2)}, u32[]{:S(2)}) %collective-permute-start.46) | collective-permute-done | bytes 1048608 | tf_op jit(solution)/shard_map/ppermute | solution.py:327
  144.8 13.1 %collective-permute-done.47.x2 = bf16[2048,256]{1,0:T(8,128)(2,1)} collective-permute-done((bf16[2048,256]{1,0:T(8,128)(2,1)S(1)}, bf16[2048,256]{1,0:T(8,128)(2,1)}, u32[]{:S(2)}, u32[]{:S(2)}) %collective-permute-start.47) | collective-permute-done | bytes 1048608 | tf_op jit(solution)/shard_map/ppermute | solution.py:327
  160.9 21.6 %collective-permute-done.29.x1 = bf16[2048,256]{1,0:T(8,128)(2,1)} collective-permute-done((bf16[2048,256]{1,0:T(8,128)(2,1)}, bf16[2048,256]{1,0:T(8,128)(2,1)}, u32[]{:S(2)}, u32[]{:S(2)}) %collective-permute-start.29) | collective-permute-done | bytes 1048608 | tf_op jit(solution)/shard_map/ppermute | solution.py:327
  184.0 7.2 expand_pair.2
  191.2 9.4 chip_stages.14
  206.6 21.0 %collective-permute-done.x1 = bf16[2048,256]{1,0:T(8,128)(2,1)} collective-permute-done((bf16[2048,256]{1,0:T(8,128)(2,1)}, bf16[2048,256]{1,0:T(8,128)(2,1)}, u32[]{:S(2)}, u32[]{:S(2)}) %collective-permute-start) | collective-permute-done | bytes 1048608 | tf_op jit(solution)/shard_map/ppermute | solution.py:327
  227.6 9.3 chip_stages.12
  236.9 11.1 %collective-permute-done.1.x2 = bf16[2048,256]{1,0:T(8,128)(2,1)} collective-permute-done((bf16[2048,256]{1,0:T(8,128)(2,1)}, bf16[2048,256]{1,0:T(8,128)(2,1)}, u32[]{:S(2)}, u32[]{:S(2)}) %collective-permute-start.1) | collective-permute-done | bytes 1048608 | tf_op jit(solution)/shard_map/ppermute | solution.py:327
  252.8 19.7 %collective-permute-done.66.x1 = bf16[2048,256]{1,0:T(8,128)(2,1)S(1)} collective-permute-done((bf16[2048,256]{1,0:T(8,128)(2,1)}, bf16[2048,256]{1,0:T(8,128)(2,1)S(1)}, u32[]{:S(2)}, u32[]{:S(2)}) %collective-permute-start.66) | collective-permute-done | bytes 1048608 | tf_op jit(solution)/shard_map/ppermute | solution.py:327
  273.1 21.9 %collective-permute-start.51 = (bf16[2048,256]{1,0:T(8,128)(2,1)}, bf16[2048,256]{1,0:T(8,128)(2,1)}, u32[]{:S(2)}, u32[]{:S(2)}) collective-permute-start(bf16[2048,256]{1,0:T(8,128)(2,1)} %get-tuple-element.128), channel_id=1, source_target_pairs={{0,2},{1,3},{2,4},{3,5},{4,6},{5,7},{6,0},{7,1},{8,10},{9,11},{10,... | collective-permute-start | bytes 3145736 | tf_op jit(solution)/shard_map/ppermute | solution.py:327
  295.0 9.7 chip_stages.10
  307.8 9.8 collective-permute-done.49.x1
  318.1 9.3 chip_stages.8
  327.4 12.6 %collective-permute-start.34 = (bf16[2048,256]{1,0:T(8,128)(2,1)}, bf16[2048,256]{1,0:T(8,128)(2,1)S(1)}, u32[]{:S(2)}, u32[]{:S(2)}) collective-permute-start(bf16[2048,256]{1,0:T(8,128)(2,1)} %get-tuple-element.110), channel_id=1, source_target_pairs={{0,2},{1,3},{2,4},{3,5},{4,6},{5,7},{6,0},{7,1},{8,10},{9,11},{10,... | collective-permute-start | bytes 3145736 | tf_op jit(solution)/shard_map/ppermute | solution.py:327
  344.4 18.1 %collective-permute-done.32.x1 = bf16[2048,256]{1,0:T(8,128)(2,1)} collective-permute-done((bf16[2048,256]{1,0:T(8,128)(2,1)}, bf16[2048,256]{1,0:T(8,128)(2,1)}, u32[]{:S(2)}, u32[]{:S(2)}) %collective-permute-start.32) | collective-permute-done | bytes 1048608 | tf_op jit(solution)/shard_map/ppermute | solution.py:327
  363.1 21.9 %collective-permute-start.11 = (bf16[2048,256]{1,0:T(8,128)(2,1)}, bf16[2048,256]{1,0:T(8,128)(2,1)}, u32[]{:S(2)}, u32[]{:S(2)}) collective-permute-start(bf16[2048,256]{1,0:T(8,128)(2,1)} %get-tuple-element.90), channel_id=1, source_target_pairs={{0,2},{1,3},{2,4},{3,5},{4,6},{5,7},{6,0},{7,1},{8,10},{9,11},{10,... | collective-permute-start | bytes 3145736 | tf_op jit(solution)/shard_map/ppermute | solution.py:327
  389.9 17.6 %collective-permute-done.9.x1 = bf16[2048,256]{1,0:T(8,128)(2,1)} collective-permute-done((bf16[2048,256]{1,0:T(8,128)(2,1)}, bf16[2048,256]{1,0:T(8,128)(2,1)}, u32[]{:S(2)}, u32[]{:S(2)}) %collective-permute-start.9) | collective-permute-done | bytes 1048608 | tf_op jit(solution)/shard_map/ppermute | solution.py:327
  408.0 10.1 collective-permute-done.11.x3
  422.1 26.3 %spread.3.second_w.refs_8_.refs_9_.refs_10_.refs_11_ = bf16[10,8192,128]{2,1,0:T(8,128)(2,1)} custom-call(bf16[11,2,32,32,256]{4,3,2,1,0:T(8,128)(2,1)} %bitcast.5, bf16[11,2,32,32,256]{4,3,2,1,0:T(8,128)(2,1)} %bitcast.6), custom_call_target="tpu_custom_call" | custom-call | flops 2500000000 | bytes 2500000 | tf_op jit(solution)/shard_map/spread/pallas_call | solution.py:146
  449.4 26.2 %spread.2.core_w.first_w = bf16[10,8192,128]{2,1,0:T(8,128)(2,1)} custom-call(bf16[11,2,32,32,256]{4,3,2,1,0:T(8,128)(2,1)} %bitcast.9, bf16[11,2,32,32,256]{4,3,2,1,0:T(8,128)(2,1)} %bitcast.10), custom_call_target="tpu_custom_call" | custom-call | flops 2500000000 | bytes 2500000 | tf_op jit(solution)/shard_map/spread/pallas_call | solution.py:146
  475.6 46.4 %middle.7.refs_0_.refs_1_.refs_2_.refs_3_ = bf16[8192,256]{1,0:T(8,128)(2,1)} custom-call(s32[1]{0:T(128)} %bitcast.chip_ref, bf16[2048,256]{1,0:T(8,128)(2,1)} %get-tuple-element.143.x0, bf16[2048,256]{1,0:T(8,128)(2,1)} %copy-done, bf16[2048,256]{1,0:T(8,128)(2,1)} %copy-done.1, bf16[2048,256]{1,0:T(8,128)(2,1)} %copy-done.2, ...), custom_call_target="tpu_custom_call" | custom-call | flops 3500000000 | bytes 3500000 | tf_op jit(solution)/shard_map/middle/pallas_call | solution.py:263
  522.2 46.2 %middle.6.refs_0_.refs_1_.refs_2_.refs_3_ = bf16[8192,256]{1,0:T(8,128)(2,1)} custom-call(s32[1]{0:T(128)} %bitcast.chip_ref, bf16[2048,256]{1,0:T(8,128)(2,1)} %get-tuple-element.125.x0, bf16[2048,256]{1,0:T(8,128)(2,1)} %collective-permute-done.49.x1, bf16[2048,256]{1,0:T(8,128)(2,1)} %collective-permute-done.50.x2, ...), custom_call_target="tpu_custom_call" | custom-call | flops 3500000000 | bytes 3500000 | tf_op jit(solution)/shard_map/middle/pallas_call | solution.py:263
  569.0 46.5 %middle.4.refs_0_.refs_1_.refs_2_.refs_3_ = bf16[8192,256]{1,0:T(8,128)(2,1)} custom-call(s32[1]{0:T(128)} %bitcast.chip_ref, bf16[2048,256]{1,0:T(8,128)(2,1)} %get-tuple-element.87.x0, bf16[2048,256]{1,0:T(8,128)(2,1)} %collective-permute-done.9.x1, bf16[2048,256]{1,0:T(8,128)(2,1)} %collective-permute-done.10.x2, ...), custom_call_target="tpu_custom_call" | custom-call | flops 3500000000 | bytes 3500000 | tf_op jit(solution)/shard_map/middle/pallas_call | solution.py:263
  617.8 46.2 %middle.5.refs_0_.refs_1_.refs_2_.refs_3_ = bf16[8192,256]{1,0:T(8,128)(2,1)} custom-call(s32[1]{0:T(128)} %bitcast.chip_ref, bf16[2048,256]{1,0:T(8,128)(2,1)} %get-tuple-element.107.x0, bf16[2048,256]{1,0:T(8,128)(2,1)} %collective-permute-done.32.x1, bf16[2048,256]{1,0:T(8,128)(2,1)} %collective-permute-done.33.x2, bf16[2048,256]{1,0:T(8,128)(2,1)} %copy-done.3, ...), custom_call_target="tpu_custom_call" | custom-call | flops 3500000000 | bytes 3500000 | tf_op jit(solution)/shard_map/middle/pallas_call | solution.py:263
  666.1 8.2 collective-permute-done.22
  679.5 6.7 collective-permute-done.24
  688.1 8.5 core_stage.7
  701.8 8.5 core_stage.6
  712.6 8.5 core_stage.4
  723.9 20.7 %collective-permute-done.74.x1 = bf16[2048,256]{1,0:T(8,128)(2,1)S(1)} collective-permute-done((bf16[2048,256]{1,0:T(8,128)(2,1)}, bf16[2048,256]{1,0:T(8,128)(2,1)S(1)}, u32[]{:S(2)}, u32[]{:S(2)}) %collective-permute-start.74) | collective-permute-done | bytes 1048608 | tf_op jit(solution)/shard_map/ppermute | solution.py:327
  749.4 8.5 core_stage.5
  759.3 8.6 collective-permute-done.57.x1
  770.1 41.9 %collective-permute-done.17.x1 = bf16[2048,256]{1,0:T(8,128)(2,1)} collective-permute-done((bf16[2048,256]{1,0:T(8,128)(2,1)}, bf16[2048,256]{1,0:T(8,128)(2,1)}, u32[]{:S(2)}, u32[]{:S(2)}) %collective-permute-start.17) | collective-permute-done | bytes 1048608 | tf_op jit(solution)/shard_map/ppermute | solution.py:327
  815.6 7.2 expand_pair.3
  826.4 9.3 chip_stages.9
  835.7 39.2 %collective-permute-done.40.x1 = bf16[2048,256]{1,0:T(8,128)(2,1)S(1)} collective-permute-done((bf16[2048,256]{1,0:T(8,128)(2,1)}, bf16[2048,256]{1,0:T(8,128)(2,1)S(1)}, u32[]{:S(2)}, u32[]{:S(2)}) %collective-permute-start.40) | collective-permute-done | bytes 1048608 | tf_op jit(solution)/shard_map/ppermute | solution.py:327
  881.8 9.3 chip_stages.15
  891.1 9.3 chip_stages.11
  900.4 6.1 broadcast_in_dim.6
  912.6 9.3 chip_stages.13
  932.3 18.7 %collective-permute-done.28 = bf16[2048,256]{1,0:T(8,128)(2,1)S(1)} collective-permute-done((bf16[2048,256]{1,0:T(8,128)(2,1)}, bf16[2048,256]{1,0:T(8,128)(2,1)S(1)}, u32[]{:S(2)}, u32[]{:S(2)}) %collective-permute-start.28) | collective-permute-done | bytes 1048608 | tf_op jit(solution)/shard_map/ppermute | solution.py:327
  955.2 14.9 %collective-permute-done.43 = bf16[2048,256]{1,0:T(8,128)(2,1)} collective-permute-done((bf16[2048,256]{1,0:T(8,128)(2,1)}, bf16[2048,256]{1,0:T(8,128)(2,1)}, u32[]{:S(2)}, u32[]{:S(2)}) %collective-permute-start.43) | collective-permute-done | bytes 1048608 | tf_op jit(solution)/shard_map/ppermute | solution.py:327
  978.4 17.4 %collective-permute-done.45 = bf16[2048,256]{1,0:T(8,128)(2,1)S(1)} collective-permute-done((bf16[2048,256]{1,0:T(8,128)(2,1)}, bf16[2048,256]{1,0:T(8,128)(2,1)S(1)}, u32[]{:S(2)}, u32[]{:S(2)}) %collective-permute-start.45) | collective-permute-done | bytes 1048608 | tf_op jit(solution)/shard_map/ppermute | solution.py:327
  1000.1 14.9 %collective-permute-done.60 = bf16[2048,256]{1,0:T(8,128)(2,1)S(1)} collective-permute-done((bf16[2048,256]{1,0:T(8,128)(2,1)}, bf16[2048,256]{1,0:T(8,128)(2,1)S(1)}, u32[]{:S(2)}, u32[]{:S(2)}) %collective-permute-start.60) | collective-permute-done | bytes 1048608 | tf_op jit(solution)/shard_map/ppermute | solution.py:327
  1018.8 22.0 %collective-permute-done.62 = bf16[2048,256]{1,0:T(8,128)(2,1)S(1)} collective-permute-done((bf16[2048,256]{1,0:T(8,128)(2,1)}, bf16[2048,256]{1,0:T(8,128)(2,1)S(1)}, u32[]{:S(2)}, u32[]{:S(2)}) %collective-permute-start.62) | collective-permute-done | bytes 1048608 | tf_op jit(solution)/shard_map/ppermute | solution.py:327
  1045.1 16.1 %collective-permute-done.79 = bf16[2048,256]{1,0:T(8,128)(2,1)S(1)} collective-permute-done((bf16[2048,256]{1,0:T(8,128)(2,1)S(1)}, bf16[2048,256]{1,0:T(8,128)(2,1)S(1)}, u32[]{:S(2)}, u32[]{:S(2)}) %collective-permute-start.79) | collective-permute-done | bytes 1048608 | tf_op jit(solution)/shard_map/ppermute | solution.py:327
  (231 shorter events, 203.8 us)
Async XLA Ops:
  40.5 54.2 %collective-permute-start.63 = (bf16[2048,256]{1,0:T(8,128)(2,1)}, bf16[2048,256]{1,0:T(8,128)(2,1)}, u32[]{:S(2)}, u32[]{:S(2)}) collective-permute-start(bf16[2048,256]{1,0:T(8,128)(2,1)} %get-tuple-element.140), channel_id=1, source_target_pairs={{0,6},{1,7},{2,0},{3,1},{4,2},{5,3},{6,4},{7,5},{8,14},{9,15},{10,... | collective-permute-start | bytes 3145736 | tf_op jit(solution)/shard_map/ppermute | solution.py:327
  46.7 52.2 %collective-permute-start.65 = (bf16[2048,256]{1,0:T(8,128)(2,1)}, bf16[2048,256]{1,0:T(8,128)(2,1)}, u32[]{:S(2)}, u32[]{:S(2)}) collective-permute-start(bf16[2048,256]{1,0:T(8,128)(2,1)} %get-tuple-element.142), channel_id=1, source_target_pairs={{0,2},{1,3},{2,4},{3,5},{4,6},{5,7},{6,0},{7,1},{8,10},{9,11},{10,... | collective-permute-start | bytes 3145736 | tf_op jit(solution)/shard_map/ppermute | solution.py:327
  94.7 63.3 %collective-permute-start.47 = (bf16[2048,256]{1,0:T(8,128)(2,1)S(1)}, bf16[2048,256]{1,0:T(8,128)(2,1)}, u32[]{:S(2)}, u32[]{:S(2)}) collective-permute-start(bf16[2048,256]{1,0:T(8,128)(2,1)S(1)} %constant_dynamic-slice_fusion.19), channel_id=1, source_target_pairs={{0,4},{1,5},{2,6},{3,7},{4,0},{5,1},{6,2},{7,3},{8,12},{9,13},{10,... | collective-permute-start | bytes 3145736 | tf_op jit(solution)/shard_map/ppermute | solution.py:327
  98.9 83.7 %collective-permute-start.29 = (bf16[2048,256]{1,0:T(8,128)(2,1)}, bf16[2048,256]{1,0:T(8,128)(2,1)}, u32[]{:S(2)}, u32[]{:S(2)}) collective-permute-start(bf16[2048,256]{1,0:T(8,128)(2,1)} %get-tuple-element.104), channel_id=1, source_target_pairs={{0,6},{1,7},{2,0},{3,1},{4,2},{5,3},{6,4},{7,5},{8,14},{9,15},{10,... | collective-permute-start | bytes 3145736 | tf_op jit(solution)/shard_map/ppermute | solution.py:327
  113.0 87.5 %collective-permute-start.31 = (bf16[2048,256]{1,0:T(8,128)(2,1)}, bf16[2048,256]{1,0:T(8,128)(2,1)S(1)}, u32[]{:S(2)}, u32[]{:S(2)}) collective-permute-start(bf16[2048,256]{1,0:T(8,128)(2,1)} %get-tuple-element.106), channel_id=1, source_target_pairs={{0,2},{1,3},{2,4},{3,5},{4,6},{5,7},{6,0},{7,1},{8,10},{9,11},{10,... | collective-permute-start | bytes 3145736 | tf_op jit(solution)/shard_map/ppermute | solution.py:327
  137.6 66.0 %collective-permute-start.30 = (bf16[2048,256]{1,0:T(8,128)(2,1)S(1)}, bf16[2048,256]{1,0:T(8,128)(2,1)}, u32[]{:S(2)}, u32[]{:S(2)}) collective-permute-start(bf16[2048,256]{1,0:T(8,128)(2,1)S(1)} %constant_dynamic-slice_fusion.23), channel_id=1, source_target_pairs={{0,4},{1,5},{2,6},{3,7},{4,0},{5,1},{6,2},{7,3},{8,12},{9,13},{10,... | collective-permute-start | bytes 3145736 | tf_op jit(solution)/shard_map/ppermute | solution.py:327
  142.7 84.8 %collective-permute-start = (bf16[2048,256]{1,0:T(8,128)(2,1)}, bf16[2048,256]{1,0:T(8,128)(2,1)}, u32[]{:S(2)}, u32[]{:S(2)}) collective-permute-start(bf16[2048,256]{1,0:T(8,128)(2,1)} %get-tuple-element.82), channel_id=1, source_target_pairs={{0,6},{1,7},{2,0},{3,1},{4,2},{5,3},{6,4},{7,5},{8,14},{9,15},{10,... | collective-permute-start | bytes 3145736 | tf_op jit(solution)/shard_map/ppermute | solution.py:327
  158.0 69.6 %collective-permute-start.2 = (bf16[2048,256]{1,0:T(8,128)(2,1)}, bf16[2048,256]{1,0:T(8,128)(2,1)}, u32[]{:S(2)}, u32[]{:S(2)}) collective-permute-start(bf16[2048,256]{1,0:T(8,128)(2,1)} %get-tuple-element.84), channel_id=1, source_target_pairs={{0,2},{1,3},{2,4},{3,5},{4,6},{5,7},{6,0},{7,1},{8,10},{9,11},{10,... | collective-permute-start | bytes 3145736 | tf_op jit(solution)/shard_map/ppermute | solution.py:327
  182.6 65.4 %collective-permute-start.1 = (bf16[2048,256]{1,0:T(8,128)(2,1)}, bf16[2048,256]{1,0:T(8,128)(2,1)}, u32[]{:S(2)}, u32[]{:S(2)}) collective-permute-start(bf16[2048,256]{1,0:T(8,128)(2,1)} %constant_dynamic-slice_fusion.11), channel_id=1, source_target_pairs={{0,4},{1,5},{2,6},{3,7},{4,0},{5,1},{6,2},{7,3},{8,12},{9,13},{10,... | collective-permute-start | bytes 3145736 | tf_op jit(solution)/shard_map/ppermute | solution.py:327
  201.6 70.9 %collective-permute-start.66 = (bf16[2048,256]{1,0:T(8,128)(2,1)}, bf16[2048,256]{1,0:T(8,128)(2,1)S(1)}, u32[]{:S(2)}, u32[]{:S(2)}) collective-permute-start(bf16[2048,256]{1,0:T(8,128)(2,1)} %get-tuple-element.144), channel_id=1, source_target_pairs={{0,6},{1,7},{2,0},{3,1},{4,2},{5,3},{6,4},{7,5},{8,14},{9,15},{10,... | collective-permute-start | bytes 3145736 | tf_op jit(solution)/shard_map/ppermute | solution.py:327
  203.6 69.5 %collective-permute-start.67 = (bf16[2048,256]{1,0:T(8,128)(2,1)}, bf16[2048,256]{1,0:T(8,128)(2,1)S(1)}, u32[]{:S(2)}, u32[]{:S(2)}) collective-permute-start(bf16[2048,256]{1,0:T(8,128)(2,1)} %get-tuple-element.145), channel_id=1, source_target_pairs={{0,4},{1,5},{2,6},{3,7},{4,0},{5,1},{6,2},{7,3},{8,12},{9,13},{10,... | collective-permute-start | bytes 3145736 | tf_op jit(solution)/shard_map/ppermute | solution.py:327
  227.6 67.4 %collective-permute-start.68 = (bf16[2048,256]{1,0:T(8,128)(2,1)}, bf16[2048,256]{1,0:T(8,128)(2,1)S(1)}, u32[]{:S(2)}, u32[]{:S(2)}) collective-permute-start(bf16[2048,256]{1,0:T(8,128)(2,1)} %get-tuple-element.146), channel_id=1, source_target_pairs={{0,2},{1,3},{2,4},{3,5},{4,6},{5,7},{6,0},{7,1},{8,10},{9,11},{10,... | collective-permute-start | bytes 3145736 | tf_op jit(solution)/shard_map/ppermute | solution.py:327
  227.6 77.1 %collective-permute-start.69 = (bf16[2048,256]{1,0:T(8,128)(2,1)}, bf16[2048,256]{1,0:T(8,128)(2,1)}, u32[]{:S(2)}, u32[]{:S(2)}) collective-permute-start(bf16[2048,256]{1,0:T(8,128)(2,1)} %get-tuple-element.143.x0), channel_id=1, source_target_pairs={{0,1},{1,0},{2,3},{3,2},{4,5},{5,4},{6,7},{7,6},{8,9},{9,8},{10,11... | collective-permute-start | bytes 3145736 | tf_op jit(solution)/shard_map/ppermute | solution.py:330
  248.0 69.5 %collective-permute-start.49 = (bf16[2048,256]{1,0:T(8,128)(2,1)}, bf16[2048,256]{1,0:T(8,128)(2,1)}, u32[]{:S(2)}, u32[]{:S(2)}) collective-permute-start(bf16[2048,256]{1,0:T(8,128)(2,1)} %get-tuple-element.126), channel_id=1, source_target_pairs={{0,6},{1,7},{2,0},{3,1},{4,2},{5,3},{6,4},{7,5},{8,14},{9,15},{10,... | collective-permute-start | bytes 3145736 | tf_op jit(solution)/shard_map/ppermute | solution.py:327
  272.4 55.0 %collective-permute-start.50 = (bf16[2048,256]{1,0:T(8,128)(2,1)}, bf16[2048,256]{1,0:T(8,128)(2,1)}, u32[]{:S(2)}, u32[]{:S(2)}) collective-permute-start(bf16[2048,256]{1,0:T(8,128)(2,1)} %get-tuple-element.127), channel_id=1, source_target_pairs={{0,4},{1,5},{2,6},{3,7},{4,0},{5,1},{6,2},{7,3},{8,12},{9,13},{10,... | collective-permute-start | bytes 3145736 | tf_op jit(solution)/shard_map/ppermute | solution.py:327
  273.1 71.3 %collective-permute-start.51 = (bf16[2048,256]{1,0:T(8,128)(2,1)}, bf16[2048,256]{1,0:T(8,128)(2,1)}, u32[]{:S(2)}, u32[]{:S(2)}) collective-permute-start(bf16[2048,256]{1,0:T(8,128)(2,1)} %get-tuple-element.128), channel_id=1, source_target_pairs={{0,2},{1,3},{2,4},{3,5},{4,6},{5,7},{6,0},{7,1},{8,10},{9,11},{10,... | collective-permute-start | bytes 3145736 | tf_op jit(solution)/shard_map/ppermute | solution.py:327
  304.7 57.8 %collective-permute-start.32 = (bf16[2048,256]{1,0:T(8,128)(2,1)}, bf16[2048,256]{1,0:T(8,128)(2,1)}, u32[]{:S(2)}, u32[]{:S(2)}) collective-permute-start(bf16[2048,256]{1,0:T(8,128)(2,1)} %get-tuple-element.108), channel_id=1, source_target_pairs={{0,6},{1,7},{2,0},{3,1},{4,2},{5,3},{6,4},{7,5},{8,14},{9,15},{10,... | collective-permute-start | bytes 3145736 | tf_op jit(solution)/shard_map/ppermute | solution.py:327
  327.4 61.9 %collective-permute-start.34 = (bf16[2048,256]{1,0:T(8,128)(2,1)}, bf16[2048,256]{1,0:T(8,128)(2,1)S(1)}, u32[]{:S(2)}, u32[]{:S(2)}) collective-permute-start(bf16[2048,256]{1,0:T(8,128)(2,1)} %get-tuple-element.110), channel_id=1, source_target_pairs={{0,2},{1,3},{2,4},{3,5},{4,6},{5,7},{6,0},{7,1},{8,10},{9,11},{10,... | collective-permute-start | bytes 3145736 | tf_op jit(solution)/shard_map/ppermute | solution.py:327
  344.4 63.1 %collective-permute-start.9 = (bf16[2048,256]{1,0:T(8,128)(2,1)}, bf16[2048,256]{1,0:T(8,128)(2,1)}, u32[]{:S(2)}, u32[]{:S(2)}) collective-permute-start(bf16[2048,256]{1,0:T(8,128)(2,1)} %get-tuple-element.88), channel_id=1, source_target_pairs={{0,6},{1,7},{2,0},{3,1},{4,2},{5,3},{6,4},{7,5},{8,14},{9,15},{10,... | collective-permute-start | bytes 3145736 | tf_op jit(solution)/shard_map/ppermute | solution.py:327
  363.1 55.0 %collective-permute-start.11 = (bf16[2048,256]{1,0:T(8,128)(2,1)}, bf16[2048,256]{1,0:T(8,128)(2,1)}, u32[]{:S(2)}, u32[]{:S(2)}) collective-permute-start(bf16[2048,256]{1,0:T(8,128)(2,1)} %get-tuple-element.90), channel_id=1, source_target_pairs={{0,2},{1,3},{2,4},{3,5},{4,6},{5,7},{6,0},{7,1},{8,10},{9,11},{10,... | collective-permute-start | bytes 3145736 | tf_op jit(solution)/shard_map/ppermute | solution.py:327
  419.1 102.9 %collective-permute-start.14 = (bf16[2048,256]{1,0:T(8,128)(2,1)}, bf16[2048,256]{1,0:T(8,128)(2,1)}, u32[]{:S(2)}, u32[]{:S(2)}) collective-permute-start(bf16[2048,256]{1,0:T(8,128)(2,1)} %collective-permute-done.10.x2), channel_id=1, source_target_pairs={{0,1},{1,0},{2,3},{3,2},{4,5},{5,4},{6,7},{7,6},{8,9},{9,8},{10,11... | collective-permute-start | bytes 3145736 | tf_op jit(solution)/shard_map/ppermute | solution.py:330
  422.0 146.5 %collective-permute-start.15 = (bf16[2048,256]{1,0:T(8,128)(2,1)}, bf16[2048,256]{1,0:T(8,128)(2,1)}, u32[]{:S(2)}, u32[]{:S(2)}) collective-permute-start(bf16[2048,256]{1,0:T(8,128)(2,1)} %collective-permute-done.11.x3), channel_id=1, source_target_pairs={{0,1},{1,0},{2,3},{3,2},{4,5},{5,4},{6,7},{7,6},{8,9},{9,8},{10,11... | collective-permute-start | bytes 3145736 | tf_op jit(solution)/shard_map/ppermute | solution.py:330
  448.4 167.1 %collective-permute-start.36 = (bf16[2048,256]{1,0:T(8,128)(2,1)}, bf16[2048,256]{1,0:T(8,128)(2,1)S(1)}, u32[]{:S(2)}, u32[]{:S(2)}) collective-permute-start(bf16[2048,256]{1,0:T(8,128)(2,1)} %collective-permute-done.32.x1), channel_id=1, source_target_pairs={{0,1},{1,0},{2,3},{3,2},{4,5},{5,4},{6,7},{7,6},{8,9},{9,8},{10,11... | collective-permute-start | bytes 3145736 | tf_op jit(solution)/shard_map/ppermute | solution.py:330
  448.9 166.7 %collective-permute-start.37 = (bf16[2048,256]{1,0:T(8,128)(2,1)}, bf16[2048,256]{1,0:T(8,128)(2,1)S(1)}, u32[]{:S(2)}, u32[]{:S(2)}) collective-permute-start(bf16[2048,256]{1,0:T(8,128)(2,1)} %collective-permute-done.33.x2), channel_id=1, source_target_pairs={{0,1},{1,0},{2,3},{3,2},{4,5},{5,4},{6,7},{7,6},{8,9},{9,8},{10,11... | collective-permute-start | bytes 3145736 | tf_op jit(solution)/shard_map/ppermute | solution.py:330
  449.0 166.6 %collective-permute-start.38 = (bf16[2048,256]{1,0:T(8,128)(2,1)}, bf16[2048,256]{1,0:T(8,128)(2,1)S(1)}, u32[]{:S(2)}, u32[]{:S(2)}) collective-permute-start(bf16[2048,256]{1,0:T(8,128)(2,1)} %copy-done.3), channel_id=1, source_target_pairs={{0,1},{1,0},{2,3},{3,2},{4,5},{5,4},{6,7},{7,6},{8,9},{9,8},{10,11... | collective-permute-start | bytes 3145736 | tf_op jit(solution)/shard_map/ppermute | solution.py:330
  522.0 165.8 %collective-permute-start.73 = (bf16[8192,256]{1,0:T(8,128)(2,1)}, bf16[8192,256]{1,0:T(8,128)(2,1)}, u32[]{:S(2)}, u32[]{:S(2)}) collective-permute-start(bf16[8192,256]{1,0:T(8,128)(2,1)} %middle.7.refs_0_.refs_1_.refs_2_.refs_3_), channel_id=1, source_target_pairs={{0,1},{1,0},{2,3},{3,2},{4,5},{5,4},{6,7},{7,6},{8,9},{9,8},{10,11... | collective-permute-start | bytes 12582920 | tf_op jit(solution)/shard_map/ppermute | solution.py:330
  568.4 132.3 %collective-permute-start.56 = (bf16[8192,256]{1,0:T(8,128)(2,1)}, bf16[8192,256]{1,0:T(8,128)(2,1)}, u32[]{:S(2)}, u32[]{:S(2)}) collective-permute-start(bf16[8192,256]{1,0:T(8,128)(2,1)} %middle.6.refs_0_.refs_1_.refs_2_.refs_3_), channel_id=1, source_target_pairs={{0,1},{1,0},{2,3},{3,2},{4,5},{5,4},{6,7},{7,6},{8,9},{9,8},{10,11... | collective-permute-start | bytes 12582920 | tf_op jit(solution)/shard_map/ppermute | solution.py:330
  615.5 94.8 %collective-permute-start.16 = (bf16[8192,256]{1,0:T(8,128)(2,1)}, bf16[8192,256]{1,0:T(8,128)(2,1)}, u32[]{:S(2)}, u32[]{:S(2)}) collective-permute-start(bf16[8192,256]{1,0:T(8,128)(2,1)} %middle.4.refs_0_.refs_1_.refs_2_.refs_3_), channel_id=1, source_target_pairs={{0,1},{1,0},{2,3},{3,2},{4,5},{5,4},{6,7},{7,6},{8,9},{9,8},{10,11... | collective-permute-start | bytes 12582920 | tf_op jit(solution)/shard_map/ppermute | solution.py:330
  664.1 57.0 %collective-permute-start.39 = (bf16[8192,256]{1,0:T(8,128)(2,1)}, bf16[8192,256]{1,0:T(8,128)(2,1)}, u32[]{:S(2)}, u32[]{:S(2)}) collective-permute-start(bf16[8192,256]{1,0:T(8,128)(2,1)} %middle.5.refs_0_.refs_1_.refs_2_.refs_3_), channel_id=1, source_target_pairs={{0,1},{1,0},{2,3},{3,2},{4,5},{5,4},{6,7},{7,6},{8,9},{9,8},{10,11... | collective-permute-start | bytes 12582920 | tf_op jit(solution)/shard_map/ppermute | solution.py:330
  700.7 57.2 %collective-permute-start.76 = (bf16[2048,256]{1,0:T(8,128)(2,1)}, bf16[2048,256]{1,0:T(8,128)(2,1)}, u32[]{:S(2)}, u32[]{:S(2)}) collective-permute-start(bf16[2048,256]{1,0:T(8,128)(2,1)} %get-tuple-element.150), channel_id=1, source_target_pairs={{0,2},{1,3},{2,4},{3,5},{4,6},{5,7},{6,0},{7,1},{8,10},{9,11},{10,... | collective-permute-start | bytes 3145736 | tf_op jit(solution)/shard_map/ppermute | solution.py:327
  710.3 57.7 %collective-permute-start.57 = (bf16[2048,256]{1,0:T(8,128)(2,1)}, bf16[2048,256]{1,0:T(8,128)(2,1)S(1)}, u32[]{:S(2)}, u32[]{:S(2)}) collective-permute-start(bf16[2048,256]{1,0:T(8,128)(2,1)} %get-tuple-element.130), channel_id=1, source_target_pairs={{0,6},{1,7},{2,0},{3,1},{4,2},{5,3},{6,4},{7,5},{8,14},{9,15},{10,... | collective-permute-start | bytes 3145736 | tf_op jit(solution)/shard_map/ppermute | solution.py:327
  721.1 90.9 %collective-permute-start.17 = (bf16[2048,256]{1,0:T(8,128)(2,1)}, bf16[2048,256]{1,0:T(8,128)(2,1)}, u32[]{:S(2)}, u32[]{:S(2)}) collective-permute-start(bf16[2048,256]{1,0:T(8,128)(2,1)} %get-tuple-element.92), channel_id=1, source_target_pairs={{0,6},{1,7},{2,0},{3,1},{4,2},{5,3},{6,4},{7,5},{8,14},{9,15},{10,... | collective-permute-start | bytes 3145736 | tf_op jit(solution)/shard_map/ppermute | solution.py:327
  744.7 78.2 %collective-permute-start.18 = (bf16[2048,256]{1,0:T(8,128)(2,1)}, bf16[2048,256]{1,0:T(8,128)(2,1)}, u32[]{:S(2)}, u32[]{:S(2)}) collective-permute-start(bf16[2048,256]{1,0:T(8,128)(2,1)} %get-tuple-element.93), channel_id=1, source_target_pairs={{0,4},{1,5},{2,6},{3,7},{4,0},{5,1},{6,2},{7,3},{8,12},{9,13},{10,... | collective-permute-start | bytes 3145736 | tf_op jit(solution)/shard_map/ppermute | solution.py:327
  745.9 80.5 %collective-permute-start.19 = (bf16[2048,256]{1,0:T(8,128)(2,1)}, bf16[2048,256]{1,0:T(8,128)(2,1)}, u32[]{:S(2)}, u32[]{:S(2)}) collective-permute-start(bf16[2048,256]{1,0:T(8,128)(2,1)} %get-tuple-element.94), channel_id=1, source_target_pairs={{0,2},{1,3},{2,4},{3,5},{4,6},{5,7},{6,0},{7,1},{8,10},{9,11},{10,... | collective-permute-start | bytes 3145736 | tf_op jit(solution)/shard_map/ppermute | solution.py:327
  758.0 116.9 %collective-permute-start.40 = (bf16[2048,256]{1,0:T(8,128)(2,1)}, bf16[2048,256]{1,0:T(8,128)(2,1)S(1)}, u32[]{:S(2)}, u32[]{:S(2)}) collective-permute-start(bf16[2048,256]{1,0:T(8,128)(2,1)} %get-tuple-element.112), channel_id=1, source_target_pairs={{0,6},{1,7},{2,0},{3,1},{4,2},{5,3},{6,4},{7,5},{8,14},{9,15},{10,... | collective-permute-start | bytes 3145736 | tf_op jit(solution)/shard_map/ppermute | solution.py:327
  768.0 111.0 %collective-permute-start.41 = (bf16[2048,256]{1,0:T(8,128)(2,1)}, bf16[2048,256]{1,0:T(8,128)(2,1)S(1)}, u32[]{:S(2)}, u32[]{:S(2)}) collective-permute-start(bf16[2048,256]{1,0:T(8,128)(2,1)} %get-tuple-element.113), channel_id=1, source_target_pairs={{0,4},{1,5},{2,6},{3,7},{4,0},{5,1},{6,2},{7,3},{8,12},{9,13},{10,... | collective-permute-start | bytes 3145736 | tf_op jit(solution)/shard_map/ppermute | solution.py:327
  812.0 69.2 %collective-permute-start.42 = (bf16[2048,256]{1,0:T(8,128)(2,1)}, bf16[2048,256]{1,0:T(8,128)(2,1)}, u32[]{:S(2)}, u32[]{:S(2)}) collective-permute-start(bf16[2048,256]{1,0:T(8,128)(2,1)} %get-tuple-element.114), channel_id=1, source_target_pairs={{0,2},{1,3},{2,4},{3,5},{4,6},{5,7},{6,0},{7,1},{8,10},{9,11},{10,... | collective-permute-start | bytes 3145736 | tf_op jit(solution)/shard_map/ppermute | solution.py:327
  822.8 86.1 %collective-permute-start.58 = (bf16[2048,256]{1,0:T(8,128)(2,1)}, bf16[2048,256]{1,0:T(8,128)(2,1)}, u32[]{:S(2)}, u32[]{:S(2)}) collective-permute-start(bf16[2048,256]{1,0:T(8,128)(2,1)} %get-tuple-element.131), channel_id=1, source_target_pairs={{0,4},{1,5},{2,6},{3,7},{4,0},{5,1},{6,2},{7,3},{8,12},{9,13},{10,... | collective-permute-start | bytes 3145736 | tf_op jit(solution)/shard_map/ppermute | solution.py:327
  826.4 85.1 %collective-permute-start.59 = (bf16[2048,256]{1,0:T(8,128)(2,1)}, bf16[2048,256]{1,0:T(8,128)(2,1)}, u32[]{:S(2)}, u32[]{:S(2)}) collective-permute-start(bf16[2048,256]{1,0:T(8,128)(2,1)} %get-tuple-element.132), channel_id=1, source_target_pairs={{0,2},{1,3},{2,4},{3,5},{4,6},{5,7},{6,0},{7,1},{8,10},{9,11},{10,... | collective-permute-start | bytes 3145736 | tf_op jit(solution)/shard_map/ppermute | solution.py:327
  874.8 50.3 %collective-permute-start.26 = (bf16[2048,256]{1,0:T(8,128)(2,1)}, bf16[2048,256]{1,0:T(8,128)(2,1)}, u32[]{:S(2)}, u32[]{:S(2)}) collective-permute-start(bf16[2048,256]{1,0:T(8,128)(2,1)} %get-tuple-element.98), channel_id=1, source_target_pairs={{0,6},{1,7},{2,0},{3,1},{4,2},{5,3},{6,4},{7,5},{8,14},{9,15},{10,... | collective-permute-start | bytes 3145736 | tf_op jit(solution)/shard_map/ppermute | solution.py:327
  881.2 69.8 %collective-permute-start.28 = (bf16[2048,256]{1,0:T(8,128)(2,1)}, bf16[2048,256]{1,0:T(8,128)(2,1)S(1)}, u32[]{:S(2)}, u32[]{:S(2)}) collective-permute-start(bf16[2048,256]{1,0:T(8,128)(2,1)} %get-tuple-element.100), channel_id=1, source_target_pairs={{0,2},{1,3},{2,4},{3,5},{4,6},{5,7},{6,0},{7,1},{8,10},{9,11},{10,... | collective-permute-start | bytes 3145736 | tf_op jit(solution)/shard_map/ppermute | solution.py:327
  908.9 61.2 %collective-permute-start.43 = (bf16[2048,256]{1,0:T(8,128)(2,1)}, bf16[2048,256]{1,0:T(8,128)(2,1)}, u32[]{:S(2)}, u32[]{:S(2)}) collective-permute-start(bf16[2048,256]{1,0:T(8,128)(2,1)} %get-tuple-element.116), channel_id=1, source_target_pairs={{0,6},{1,7},{2,0},{3,1},{4,2},{5,3},{6,4},{7,5},{8,14},{9,15},{10,... | collective-permute-start | bytes 3145736 | tf_op jit(solution)/shard_map/ppermute | solution.py:327
  911.5 62.6 %collective-permute-start.44 = (bf16[2048,256]{1,0:T(8,128)(2,1)}, bf16[2048,256]{1,0:T(8,128)(2,1)}, u32[]{:S(2)}, u32[]{:S(2)}) collective-permute-start(bf16[2048,256]{1,0:T(8,128)(2,1)} %get-tuple-element.117), channel_id=1, source_target_pairs={{0,4},{1,5},{2,6},{3,7},{4,0},{5,1},{6,2},{7,3},{8,12},{9,13},{10,... | collective-permute-start | bytes 3145736 | tf_op jit(solution)/shard_map/ppermute | solution.py:327
  925.1 70.7 %collective-permute-start.45 = (bf16[2048,256]{1,0:T(8,128)(2,1)}, bf16[2048,256]{1,0:T(8,128)(2,1)S(1)}, u32[]{:S(2)}, u32[]{:S(2)}) collective-permute-start(bf16[2048,256]{1,0:T(8,128)(2,1)} %get-tuple-element.118), channel_id=1, source_target_pairs={{0,2},{1,3},{2,4},{3,5},{4,6},{5,7},{6,0},{7,1},{8,10},{9,11},{10,... | collective-permute-start | bytes 3145736 | tf_op jit(solution)/shard_map/ppermute | solution.py:327
  929.2 85.8 %collective-permute-start.60 = (bf16[2048,256]{1,0:T(8,128)(2,1)}, bf16[2048,256]{1,0:T(8,128)(2,1)S(1)}, u32[]{:S(2)}, u32[]{:S(2)}) collective-permute-start(bf16[2048,256]{1,0:T(8,128)(2,1)} %get-tuple-element.134), channel_id=1, source_target_pairs={{0,6},{1,7},{2,0},{3,1},{4,2},{5,3},{6,4},{7,5},{8,14},{9,15},{10,... | collective-permute-start | bytes 3145736 | tf_op jit(solution)/shard_map/ppermute | solution.py:327
  951.0 66.8 %collective-permute-start.61 = (bf16[2048,256]{1,0:T(8,128)(2,1)}, bf16[2048,256]{1,0:T(8,128)(2,1)S(1)}, u32[]{:S(2)}, u32[]{:S(2)}) collective-permute-start(bf16[2048,256]{1,0:T(8,128)(2,1)} %get-tuple-element.135), channel_id=1, source_target_pairs={{0,4},{1,5},{2,6},{3,7},{4,0},{5,1},{6,2},{7,3},{8,12},{9,13},{10,... | collective-permute-start | bytes 3145736 | tf_op jit(solution)/shard_map/ppermute | solution.py:327
  970.1 70.7 %collective-permute-start.62 = (bf16[2048,256]{1,0:T(8,128)(2,1)}, bf16[2048,256]{1,0:T(8,128)(2,1)S(1)}, u32[]{:S(2)}, u32[]{:S(2)}) collective-permute-start(bf16[2048,256]{1,0:T(8,128)(2,1)} %get-tuple-element.136), channel_id=1, source_target_pairs={{0,2},{1,3},{2,4},{3,5},{4,6},{5,7},{6,0},{7,1},{8,10},{9,11},{10,... | collective-permute-start | bytes 3145736 | tf_op jit(solution)/shard_map/ppermute | solution.py:327
  974.1 68.7 %collective-permute-start.77 = (bf16[2048,256]{1,0:T(8,128)(2,1)}, bf16[2048,256]{1,0:T(8,128)(2,1)S(1)}, u32[]{:S(2)}, u32[]{:S(2)}) collective-permute-start(bf16[2048,256]{1,0:T(8,128)(2,1)} %get-tuple-element.152), channel_id=1, source_target_pairs={{0,6},{1,7},{2,0},{3,1},{4,2},{5,3},{6,4},{7,5},{8,14},{9,15},{10,... | collective-permute-start | bytes 3145736 | tf_op jit(solution)/shard_map/ppermute | solution.py:327
  (59 other events, 2080.8 us)

commit v3 on v2

--- a/solution.py
+++ b/solution.py
@@ -176,7 +176,7 @@
 
 def chip_stages(parts, ea, eb, blk):
     rows, width = parts[0].shape
-    tile = rows // 8
+    tile = rows // 4
     spec = pl.BlockSpec((tile, width), lambda i: (i, 0))
     wspec = pl.BlockSpec((CHIPS, tile, LANES), lambda i: (0, i, 0))
     return pl.pallas_call(
@@ -199,7 +199,7 @@
 def middle_kernel(blk, chip_ref, x0, x1, x2, x3, p0, p1, p2, p3, core_w, first_w, second_w, buf):
     step = pl.program_id(0)
     group_rows = x0.shape[0]
-    unroll = 8
+    unroll = 16
 
     @pl.when(step == 0)
     def _():
@@ -387,10 +387,15 @@
             parts = core_stage(chip_arr, act, twin, mid_second, blk)
             parts = swap(parts)
             parts = chip_stages(parts, lo_second, hi_second, blk)
-            parts = swap(parts)
-            for r in range(CHIPS):
-                at = (((chip + r) % CHIPS) * group, c * width)
-                result = lax.dynamic_update_slice(result, parts[r], at)
+            far = parts[2]
+            cuts = 1 if c + 1 < chunks else 2
+            size = group // cuts
+            far = [to_chip(far[i * size : (i + 1) * size], 2) for i in range(cuts)]
+            pieces = [(0, 0, parts[0]), (3, 0, to_chip(parts[1], 1)), (1, 0, to_chip(parts[3], 3))]
+            pieces += [(2, i * size, piece) for i, piece in enumerate(far)]
+            for r, row, piece in pieces:
+                at = (((chip + r) % CHIPS) * group + row, c * width)
+                result = lax.dynamic_update_slice(result, piece, at)
         return result
 
     row_spec = P(("dp", "sp"), None)

time: 1070 us -> 1040 us (0.972)
  Pallas kernels: 372 us -> 326 us
  starting transfers between devices: 154 us -> 183 us
    ppermute x54 -> x55, starting transfers between devices: 142 us -> 170 us  [to_chip(): return lax.ppermute(value, 'sp', pairs)]
    pallas_call x4, Pallas kernels: 185 us -> 159 us  [middle(): pl.pallas_call(functools.partial(middle_kernel, blk), grid_spec=pltpu.Pre...]
    pallas_call x8, Pallas kernels: 74.8 us -> 55.2 us  [chip_stages(): pl.pallas_call(functools.partial(chip_kernel, blk), grid=(rows // tile,),...]
    ppermute x54 -> x55, waiting for transfers between devices: 451 us -> 443 us  [to_chip(): return lax.ppermute(value, 'sp', pairs)]
    dynamic_update_slice x16 -> x17, local copies, waits for them, and re-layouts: 24 us -> 23.3 us  [device_program(): result = lax.dynamic_update_slice(result, piece, at)]
  transfers between devices with their start and end apart: 80 -> 81, of which waited for: 33 -> 38; matrix products, arithmetic and copies ran while one was open for 6% -> 6% of each run, Pallas kernels for 35% -> 31%
where the time goes in v3:
time: 1040 us; the launch traced here: 1030 us
  waiting for transfers between devices  450 us (43%)
  Pallas kernels  326 us (31%)
  starting transfers between devices  183 us (18%)
  local copies, waits for them, and re-layouts  63.8 us (6%)
    ppermute x55, waiting for transfers between devices, to_chip(): return lax.ppermute(value, 'sp', pairs)  443 us
    ppermute x55, starting transfers between devices, to_chip(): return lax.ppermute(value, 'sp', pairs)  170 us
    pallas_call x4, Pallas kernels, middle(): pl.pallas_call(functools.partial(middle_kernel, blk), grid_spec=pltpu.Pre...  159 us
    pallas_call x8, Pallas kernels, chip_stages(): pl.pallas_call(functools.partial(chip_kernel, blk), grid=(rows // tile,),...  55.2 us
    pallas_call x2, Pallas kernels, spread(): pl.pallas_call(functools.partial(spread_kernel, first_map), grid=(5,), in...  52.5 us
    pallas_call x4, Pallas kernels, core_stage(): pl.pallas_call(functools.partial(core_kernel, blk), grid_spec=pltpu.Prefe...  34.3 us
    dynamic_slice x10, local copies, waits for them, and re-layouts, quarter(): return lax.dynamic_slice(array, (start, col), (group, wide))  24.5 us
    dynamic_update_slice x17, local copies, waits for them, and re-layouts, device_program(): result = lax.dynamic_update_slice(result, piece, at)  23.3 us
  transfers between devices with their start and end apart: 81, of which 38 were waited for; matrix products, arithmetic and copies ran while one was open for 6% of the time, Pallas kernels for 31%

profile of v3, /device:TPU:112, one launch (start us, length us, event | category | flops | bytes accessed | tf_op | source)
XLA Modules:
  0.0 1033.3 jit_solution(8878142668728625071)
XLA Ops:
  47.0 29.3 %collective-permute-done.3 = bf16[1024,128]{1,0:T(8,128)(2,1)} collective-permute-done((bf16[1024,128]{1,0:T(8,128)(2,1)}, bf16[1024,128]{1,0:T(8,128)(2,1)}, u32[]{:S(2)}, u32[]{:S(2)}) %collective-permute-start.3) | collective-permute-done | bytes 262176 | tf_op jit(solution)/shard_map/ppermute | solution.py:327
  101.0 11.0 %collective-permute-done.64.x2 = bf16[2048,256]{1,0:T(8,128)(2,1)} collective-permute-done((bf16[2048,256]{1,0:T(8,128)(2,1)S(1)}, bf16[2048,256]{1,0:T(8,128)(2,1)}, u32[]{:S(2)}, u32[]{:S(2)}) %collective-permute-start.64) | collective-permute-done | bytes 1048608 | tf_op jit(solution)/shard_map/ppermute | solution.py:327
  114.0 22.5 %collective-permute-done.46.x1 = bf16[2048,256]{1,0:T(8,128)(2,1)} collective-permute-done((bf16[2048,256]{1,0:T(8,128)(2,1)}, bf16[2048,256]{1,0:T(8,128)(2,1)}, u32[]{:S(2)}, u32[]{:S(2)}) %collective-permute-start.46) | collective-permute-done | bytes 1048608 | tf_op jit(solution)/shard_map/ppermute | solution.py:327
  143.9 13.2 %collective-permute-done.47.x2 = bf16[2048,256]{1,0:T(8,128)(2,1)} collective-permute-done((bf16[2048,256]{1,0:T(8,128)(2,1)S(1)}, bf16[2048,256]{1,0:T(8,128)(2,1)}, u32[]{:S(2)}, u32[]{:S(2)}) %collective-permute-start.47) | collective-permute-done | bytes 1048608 | tf_op jit(solution)/shard_map/ppermute | solution.py:327
  159.8 21.6 %collective-permute-done.29.x1 = bf16[2048,256]{1,0:T(8,128)(2,1)} collective-permute-done((bf16[2048,256]{1,0:T(8,128)(2,1)}, bf16[2048,256]{1,0:T(8,128)(2,1)}, u32[]{:S(2)}, u32[]{:S(2)}) %collective-permute-start.29) | collective-permute-done | bytes 1048608 | tf_op jit(solution)/shard_map/ppermute | solution.py:327
  182.9 7.2 expand_pair.2
  190.1 6.9 chip_stages.14
  203.0 23.4 %collective-permute-done.x1 = bf16[2048,256]{1,0:T(8,128)(2,1)} collective-permute-done((bf16[2048,256]{1,0:T(8,128)(2,1)}, bf16[2048,256]{1,0:T(8,128)(2,1)}, u32[]{:S(2)}, u32[]{:S(2)}) %collective-permute-start) | collective-permute-done | bytes 1048608 | tf_op jit(solution)/shard_map/ppermute | solution.py:327
  226.5 6.9 chip_stages.12
  233.4 13.7 %collective-permute-done.1.x2 = bf16[2048,256]{1,0:T(8,128)(2,1)} collective-permute-done((bf16[2048,256]{1,0:T(8,128)(2,1)S(1)}, bf16[2048,256]{1,0:T(8,128)(2,1)}, u32[]{:S(2)}, u32[]{:S(2)}) %collective-permute-start.1) | collective-permute-done | bytes 1048608 | tf_op jit(solution)/shard_map/ppermute | solution.py:327
  251.6 19.7 %collective-permute-done.66.x1 = bf16[2048,256]{1,0:T(8,128)(2,1)S(1)} collective-permute-done((bf16[2048,256]{1,0:T(8,128)(2,1)}, bf16[2048,256]{1,0:T(8,128)(2,1)S(1)}, u32[]{:S(2)}, u32[]{:S(2)}) %collective-permute-start.66) | collective-permute-done | bytes 1048608 | tf_op jit(solution)/shard_map/ppermute | solution.py:327
  271.9 22.0 %collective-permute-start.51 = (bf16[2048,256]{1,0:T(8,128)(2,1)}, bf16[2048,256]{1,0:T(8,128)(2,1)}, u32[]{:S(2)}, u32[]{:S(2)}) collective-permute-start(bf16[2048,256]{1,0:T(8,128)(2,1)} %get-tuple-element.128), channel_id=1, source_target_pairs={{0,2},{1,3},{2,4},{3,5},{4,6},{5,7},{6,0},{7,1},{8,10},{9,11},{10,... | collective-permute-start | bytes 3145736 | tf_op jit(solution)/shard_map/ppermute | solution.py:327
  294.0 6.9 chip_stages.10
  303.6 12.7 %collective-permute-done.49.x1 = bf16[2048,256]{1,0:T(8,128)(2,1)S(1)} collective-permute-done((bf16[2048,256]{1,0:T(8,128)(2,1)}, bf16[2048,256]{1,0:T(8,128)(2,1)S(1)}, u32[]{:S(2)}, u32[]{:S(2)}) %collective-permute-start.49) | collective-permute-done | bytes 1048608 | tf_op jit(solution)/shard_map/ppermute | solution.py:327
  323.8 15.0 %collective-permute-start.34 = (bf16[2048,256]{1,0:T(8,128)(2,1)}, bf16[2048,256]{1,0:T(8,128)(2,1)}, u32[]{:S(2)}, u32[]{:S(2)}) collective-permute-start(bf16[2048,256]{1,0:T(8,128)(2,1)} %get-tuple-element.110), channel_id=1, source_target_pairs={{0,2},{1,3},{2,4},{3,5},{4,6},{5,7},{6,0},{7,1},{8,10},{9,11},{10,... | collective-permute-start | bytes 3145736 | tf_op jit(solution)/shard_map/ppermute | solution.py:327
  343.4 18.0 %collective-permute-done.32.x1 = bf16[2048,256]{1,0:T(8,128)(2,1)} collective-permute-done((bf16[2048,256]{1,0:T(8,128)(2,1)}, bf16[2048,256]{1,0:T(8,128)(2,1)}, u32[]{:S(2)}, u32[]{:S(2)}) %collective-permute-start.32) | collective-permute-done | bytes 1048608 | tf_op jit(solution)/shard_map/ppermute | solution.py:327
  362.0 21.9 %collective-permute-start.11 = (bf16[2048,256]{1,0:T(8,128)(2,1)}, bf16[2048,256]{1,0:T(8,128)(2,1)}, u32[]{:S(2)}, u32[]{:S(2)}) collective-permute-start(bf16[2048,256]{1,0:T(8,128)(2,1)} %get-tuple-element.90), channel_id=1, source_target_pairs={{0,2},{1,3},{2,4},{3,5},{4,6},{5,7},{6,0},{7,1},{8,10},{9,11},{10,... | collective-permute-start | bytes 3145736 | tf_op jit(solution)/shard_map/ppermute | solution.py:327
  388.8 17.6 %collective-permute-done.9.x1 = bf16[2048,256]{1,0:T(8,128)(2,1)} collective-permute-done((bf16[2048,256]{1,0:T(8,128)(2,1)}, bf16[2048,256]{1,0:T(8,128)(2,1)}, u32[]{:S(2)}, u32[]{:S(2)}) %collective-permute-start.9) | collective-permute-done | bytes 1048608 | tf_op jit(solution)/shard_map/ppermute | solution.py:327
  406.9 10.3 collective-permute-done.11.x3
  421.2 26.3 %spread.3.second_w.refs_8_.refs_9_.refs_10_.refs_11_ = bf16[10,8192,128]{2,1,0:T(8,128)(2,1)} custom-call(bf16[11,2,32,32,256]{4,3,2,1,0:T(8,128)(2,1)} %bitcast.5, bf16[11,2,32,32,256]{4,3,2,1,0:T(8,128)(2,1)} %bitcast.6), custom_call_target="tpu_custom_call" | custom-call | flops 2500000000 | bytes 2500000 | tf_op jit(solution)/shard_map/spread/pallas_call | solution.py:146
  448.5 26.2 %spread.2.core_w.first_w = bf16[10,8192,128]{2,1,0:T(8,128)(2,1)} custom-call(bf16[11,2,32,32,256]{4,3,2,1,0:T(8,128)(2,1)} %bitcast.9, bf16[11,2,32,32,256]{4,3,2,1,0:T(8,128)(2,1)} %bitcast.10), custom_call_target="tpu_custom_call" | custom-call | flops 2500000000 | bytes 2500000 | tf_op jit(solution)/shard_map/spread/pallas_call | solution.py:146
  474.7 39.8 %middle.7.refs_0_.refs_1_.refs_2_.refs_3_ = bf16[8192,256]{1,0:T(8,128)(2,1)} custom-call(s32[1]{0:T(128)} %bitcast.chip_ref, bf16[2048,256]{1,0:T(8,128)(2,1)} %get-tuple-element.143.x0, bf16[2048,256]{1,0:T(8,128)(2,1)} %copy-done.2, bf16[2048,256]{1,0:T(8,128)(2,1)} %collective-permute-done.67.x2, bf16[2048,256]{1,0:T(8,128)(2,1)} %collective-permute-done.68.x3, ...), custom_call_target="tpu_custom_call" | custom-call | flops 3500000000 | bytes 3500000 | tf_op jit(solution)/shard_map/middle/pallas_call | solution.py:263
  514.6 39.6 %middle.5.refs_0_.refs_1_.refs_2_.refs_3_ = bf16[8192,256]{1,0:T(8,128)(2,1)} custom-call(s32[1]{0:T(128)} %bitcast.chip_ref, bf16[2048,256]{1,0:T(8,128)(2,1)} %get-tuple-element.107.x0, bf16[2048,256]{1,0:T(8,128)(2,1)} %collective-permute-done.32.x1, bf16[2048,256]{1,0:T(8,128)(2,1)} %collective-permute-done.33.x2, ...), custom_call_target="tpu_custom_call" | custom-call | flops 3500000000 | bytes 3500000 | tf_op jit(solution)/shard_map/middle/pallas_call | solution.py:263
  554.7 39.9 %middle.4.refs_0_.refs_1_.refs_2_.refs_3_ = bf16[8192,256]{1,0:T(8,128)(2,1)} custom-call(s32[1]{0:T(128)} %bitcast.chip_ref, bf16[2048,256]{1,0:T(8,128)(2,1)} %get-tuple-element.87.x0, bf16[2048,256]{1,0:T(8,128)(2,1)} %collective-permute-done.9.x1, bf16[2048,256]{1,0:T(8,128)(2,1)} %collective-permute-done.10.x2, ...), custom_call_target="tpu_custom_call" | custom-call | flops 3500000000 | bytes 3500000 | tf_op jit(solution)/shard_map/middle/pallas_call | solution.py:263
  595.6 39.7 %middle.6.refs_0_.refs_1_.refs_2_.refs_3_ = bf16[8192,256]{1,0:T(8,128)(2,1)} custom-call(s32[1]{0:T(128)} %bitcast.chip_ref, bf16[2048,256]{1,0:T(8,128)(2,1)} %get-tuple-element.125.x0, bf16[2048,256]{1,0:T(8,128)(2,1)} %copy-done, bf16[2048,256]{1,0:T(8,128)(2,1)} %copy-done.1, bf16[2048,256]{1,0:T(8,128)(2,1)} %collective-permute-done.51.x3, ...), custom_call_target="tpu_custom_call" | custom-call | flops 3500000000 | bytes 3500000 | tf_op jit(solution)/shard_map/middle/pallas_call | solution.py:263
  637.3 8.3 collective-permute-done.22
  649.2 7.5 collective-permute-done.24
  658.7 8.7 core_stage.7
  672.6 8.6 core_stage.5
  682.6 8.5 core_stage.4
  694.0 21.2 %collective-permute-done.74.x1 = bf16[2048,256]{1,0:T(8,128)(2,1)S(1)} collective-permute-done((bf16[2048,256]{1,0:T(8,128)(2,1)}, bf16[2048,256]{1,0:T(8,128)(2,1)S(1)}, u32[]{:S(2)}, u32[]{:S(2)}) %collective-permute-start.74) | collective-permute-done | bytes 1048608 | tf_op jit(solution)/shard_map/ppermute | solution.py:327
  721.2 17.6 %collective-permute-done.40.x1 = bf16[2048,256]{1,0:T(8,128)(2,1)} collective-permute-done((bf16[2048,256]{1,0:T(8,128)(2,1)}, bf16[2048,256]{1,0:T(8,128)(2,1)}, u32[]{:S(2)}, u32[]{:S(2)}) %collective-permute-start.40) | collective-permute-done | bytes 1048608 | tf_op jit(solution)/shard_map/ppermute | solution.py:327
  739.9 8.5 core_stage.6
  748.4 12.9 %collective-permute-done.17.x1 = bf16[2048,256]{1,0:T(8,128)(2,1)} collective-permute-done((bf16[2048,256]{1,0:T(8,128)(2,1)}, bf16[2048,256]{1,0:T(8,128)(2,1)}, u32[]{:S(2)}, u32[]{:S(2)}) %collective-permute-start.17) | collective-permute-done | bytes 1048608 | tf_op jit(solution)/shard_map/ppermute | solution.py:327
  761.3 43.5 %collective-permute-start.57 = (bf16[2048,256]{1,0:T(8,128)(2,1)}, bf16[2048,256]{1,0:T(8,128)(2,1)}, u32[]{:S(2)}, u32[]{:S(2)}) collective-permute-start(bf16[2048,256]{1,0:T(8,128)(2,1)} %get-tuple-element.130), channel_id=1, source_target_pairs={{0,6},{1,7},{2,0},{3,1},{4,2},{5,3},{6,4},{7,5},{8,14},{9,15},{10,... | collective-permute-start | bytes 3145736 | tf_op jit(solution)/shard_map/ppermute | solution.py:327
  806.4 7.2 expand_pair.3
  814.6 6.9 chip_stages.9
  824.9 7.0 chip_stages.15
  831.8 6.9 chip_stages.11
  838.7 12.2 %collective-permute-done.57.x1 = bf16[2048,256]{1,0:T(8,128)(2,1)} collective-permute-done((bf16[2048,256]{1,0:T(8,128)(2,1)}, bf16[2048,256]{1,0:T(8,128)(2,1)}, u32[]{:S(2)}, u32[]{:S(2)}) %collective-permute-start.57) | collective-permute-done | bytes 1048608 | tf_op jit(solution)/shard_map/ppermute | solution.py:327
  864.6 6.9 chip_stages.13
  871.5 14.9 %collective-permute-done.26 = bf16[2048,256]{1,0:T(8,128)(2,1)S(1)} collective-permute-done((bf16[2048,256]{1,0:T(8,128)(2,1)}, bf16[2048,256]{1,0:T(8,128)(2,1)S(1)}, u32[]{:S(2)}, u32[]{:S(2)}) %collective-permute-start.26) | collective-permute-done | bytes 1048608 | tf_op jit(solution)/shard_map/ppermute | solution.py:327
  896.9 12.2 %collective-permute-done.28 = bf16[2048,256]{1,0:T(8,128)(2,1)} collective-permute-done((bf16[2048,256]{1,0:T(8,128)(2,1)}, bf16[2048,256]{1,0:T(8,128)(2,1)}, u32[]{:S(2)}, u32[]{:S(2)}) %collective-permute-start.28) | collective-permute-done | bytes 1048608 | tf_op jit(solution)/shard_map/ppermute | solution.py:327
  913.7 17.8 %collective-permute-done.43 = bf16[2048,256]{1,0:T(8,128)(2,1)} collective-permute-done((bf16[2048,256]{1,0:T(8,128)(2,1)}, bf16[2048,256]{1,0:T(8,128)(2,1)}, u32[]{:S(2)}, u32[]{:S(2)}) %collective-permute-start.43) | collective-permute-done | bytes 1048608 | tf_op jit(solution)/shard_map/ppermute | solution.py:327
  943.1 10.8 %collective-permute-done.45 = bf16[2048,256]{1,0:T(8,128)(2,1)S(1)} collective-permute-done((bf16[2048,256]{1,0:T(8,128)(2,1)}, bf16[2048,256]{1,0:T(8,128)(2,1)S(1)}, u32[]{:S(2)}, u32[]{:S(2)}) %collective-permute-start.45) | collective-permute-done | bytes 1048608 | tf_op jit(solution)/shard_map/ppermute | solution.py:327
  957.2 19.1 %collective-permute-done.60 = bf16[2048,256]{1,0:T(8,128)(2,1)S(1)} collective-permute-done((bf16[2048,256]{1,0:T(8,128)(2,1)}, bf16[2048,256]{1,0:T(8,128)(2,1)S(1)}, u32[]{:S(2)}, u32[]{:S(2)}) %collective-permute-start.60) | collective-permute-done | bytes 1048608 | tf_op jit(solution)/shard_map/ppermute | solution.py:327
  986.8 12.0 %collective-permute-done.62 = bf16[2048,256]{1,0:T(8,128)(2,1)S(1)} collective-permute-done((bf16[2048,256]{1,0:T(8,128)(2,1)}, bf16[2048,256]{1,0:T(8,128)(2,1)S(1)}, u32[]{:S(2)}, u32[]{:S(2)}) %collective-permute-start.62) | collective-permute-done | bytes 1048608 | tf_op jit(solution)/shard_map/ppermute | solution.py:327
  1000.9 20.2 %collective-permute-done.77 = bf16[2048,256]{1,0:T(8,128)(2,1)S(1)} collective-permute-done((bf16[2048,256]{1,0:T(8,128)(2,1)}, bf16[2048,256]{1,0:T(8,128)(2,1)S(1)}, u32[]{:S(2)}, u32[]{:S(2)}) %collective-permute-start.77) | collective-permute-done | bytes 1048608 | tf_op jit(solution)/shard_map/ppermute | solution.py:327
  (223 shorter events, 222.1 us)
Async XLA Ops:
  39.6 54.2 %collective-permute-start.63 = (bf16[2048,256]{1,0:T(8,128)(2,1)}, bf16[2048,256]{1,0:T(8,128)(2,1)}, u32[]{:S(2)}, u32[]{:S(2)}) collective-permute-start(bf16[2048,256]{1,0:T(8,128)(2,1)} %get-tuple-element.140), channel_id=1, source_target_pairs={{0,6},{1,7},{2,0},{3,1},{4,2},{5,3},{6,4},{7,5},{8,14},{9,15},{10,... | collective-permute-start | bytes 3145736 | tf_op jit(solution)/shard_map/ppermute | solution.py:327
  45.8 52.2 %collective-permute-start.65 = (bf16[2048,256]{1,0:T(8,128)(2,1)}, bf16[2048,256]{1,0:T(8,128)(2,1)}, u32[]{:S(2)}, u32[]{:S(2)}) collective-permute-start(bf16[2048,256]{1,0:T(8,128)(2,1)} %get-tuple-element.142), channel_id=1, source_target_pairs={{0,2},{1,3},{2,4},{3,5},{4,6},{5,7},{6,0},{7,1},{8,10},{9,11},{10,... | collective-permute-start | bytes 3145736 | tf_op jit(solution)/shard_map/ppermute | solution.py:327
  93.8 63.3 %collective-permute-start.47 = (bf16[2048,256]{1,0:T(8,128)(2,1)S(1)}, bf16[2048,256]{1,0:T(8,128)(2,1)}, u32[]{:S(2)}, u32[]{:S(2)}) collective-permute-start(bf16[2048,256]{1,0:T(8,128)(2,1)S(1)} %constant_dynamic-slice_fusion.19), channel_id=1, source_target_pairs={{0,4},{1,5},{2,6},{3,7},{4,0},{5,1},{6,2},{7,3},{8,12},{9,13},{10,... | collective-permute-start | bytes 3145736 | tf_op jit(solution)/shard_map/ppermute | solution.py:327
  98.0 83.4 %collective-permute-start.29 = (bf16[2048,256]{1,0:T(8,128)(2,1)}, bf16[2048,256]{1,0:T(8,128)(2,1)}, u32[]{:S(2)}, u32[]{:S(2)}) collective-permute-start(bf16[2048,256]{1,0:T(8,128)(2,1)} %get-tuple-element.104), channel_id=1, source_target_pairs={{0,6},{1,7},{2,0},{3,1},{4,2},{5,3},{6,4},{7,5},{8,14},{9,15},{10,... | collective-permute-start | bytes 3145736 | tf_op jit(solution)/shard_map/ppermute | solution.py:327
  112.1 84.9 %collective-permute-start.31 = (bf16[2048,256]{1,0:T(8,128)(2,1)}, bf16[2048,256]{1,0:T(8,128)(2,1)S(1)}, u32[]{:S(2)}, u32[]{:S(2)}) collective-permute-start(bf16[2048,256]{1,0:T(8,128)(2,1)} %get-tuple-element.106), channel_id=1, source_target_pairs={{0,2},{1,3},{2,4},{3,5},{4,6},{5,7},{6,0},{7,1},{8,10},{9,11},{10,... | collective-permute-start | bytes 3145736 | tf_op jit(solution)/shard_map/ppermute | solution.py:327
  136.5 65.6 %collective-permute-start.30 = (bf16[2048,256]{1,0:T(8,128)(2,1)}, bf16[2048,256]{1,0:T(8,128)(2,1)}, u32[]{:S(2)}, u32[]{:S(2)}) collective-permute-start(bf16[2048,256]{1,0:T(8,128)(2,1)} %constant_dynamic-slice_fusion.23), channel_id=1, source_target_pairs={{0,4},{1,5},{2,6},{3,7},{4,0},{5,1},{6,2},{7,3},{8,12},{9,13},{10,... | collective-permute-start | bytes 3145736 | tf_op jit(solution)/shard_map/ppermute | solution.py:327
  141.8 84.6 %collective-permute-start = (bf16[2048,256]{1,0:T(8,128)(2,1)}, bf16[2048,256]{1,0:T(8,128)(2,1)}, u32[]{:S(2)}, u32[]{:S(2)}) collective-permute-start(bf16[2048,256]{1,0:T(8,128)(2,1)} %get-tuple-element.82), channel_id=1, source_target_pairs={{0,6},{1,7},{2,0},{3,1},{4,2},{5,3},{6,4},{7,5},{8,14},{9,15},{10,... | collective-permute-start | bytes 3145736 | tf_op jit(solution)/shard_map/ppermute | solution.py:327
  157.1 69.4 %collective-permute-start.2 = (bf16[2048,256]{1,0:T(8,128)(2,1)}, bf16[2048,256]{1,0:T(8,128)(2,1)}, u32[]{:S(2)}, u32[]{:S(2)}) collective-permute-start(bf16[2048,256]{1,0:T(8,128)(2,1)} %get-tuple-element.84), channel_id=1, source_target_pairs={{0,2},{1,3},{2,4},{3,5},{4,6},{5,7},{6,0},{7,1},{8,10},{9,11},{10,... | collective-permute-start | bytes 3145736 | tf_op jit(solution)/shard_map/ppermute | solution.py:327
  181.5 65.6 %collective-permute-start.1 = (bf16[2048,256]{1,0:T(8,128)(2,1)S(1)}, bf16[2048,256]{1,0:T(8,128)(2,1)}, u32[]{:S(2)}, u32[]{:S(2)}) collective-permute-start(bf16[2048,256]{1,0:T(8,128)(2,1)S(1)} %constant_dynamic-slice_fusion.11), channel_id=1, source_target_pairs={{0,4},{1,5},{2,6},{3,7},{4,0},{5,1},{6,2},{7,3},{8,12},{9,13},{10,... | collective-permute-start | bytes 3145736 | tf_op jit(solution)/shard_map/ppermute | solution.py:327
  198.0 73.3 %collective-permute-start.66 = (bf16[2048,256]{1,0:T(8,128)(2,1)}, bf16[2048,256]{1,0:T(8,128)(2,1)S(1)}, u32[]{:S(2)}, u32[]{:S(2)}) collective-permute-start(bf16[2048,256]{1,0:T(8,128)(2,1)} %get-tuple-element.144), channel_id=1, source_target_pairs={{0,6},{1,7},{2,0},{3,1},{4,2},{5,3},{6,4},{7,5},{8,14},{9,15},{10,... | collective-permute-start | bytes 3145736 | tf_op jit(solution)/shard_map/ppermute | solution.py:327
  202.1 69.9 %collective-permute-start.67 = (bf16[2048,256]{1,0:T(8,128)(2,1)}, bf16[2048,256]{1,0:T(8,128)(2,1)}, u32[]{:S(2)}, u32[]{:S(2)}) collective-permute-start(bf16[2048,256]{1,0:T(8,128)(2,1)} %get-tuple-element.145), channel_id=1, source_target_pairs={{0,4},{1,5},{2,6},{3,7},{4,0},{5,1},{6,2},{7,3},{8,12},{9,13},{10,... | collective-permute-start | bytes 3145736 | tf_op jit(solution)/shard_map/ppermute | solution.py:327
  226.4 67.5 %collective-permute-start.68 = (bf16[2048,256]{1,0:T(8,128)(2,1)}, bf16[2048,256]{1,0:T(8,128)(2,1)}, u32[]{:S(2)}, u32[]{:S(2)}) collective-permute-start(bf16[2048,256]{1,0:T(8,128)(2,1)} %get-tuple-element.146), channel_id=1, source_target_pairs={{0,2},{1,3},{2,4},{3,5},{4,6},{5,7},{6,0},{7,1},{8,10},{9,11},{10,... | collective-permute-start | bytes 3145736 | tf_op jit(solution)/shard_map/ppermute | solution.py:327
  226.5 74.4 %collective-permute-start.69 = (bf16[2048,256]{1,0:T(8,128)(2,1)}, bf16[2048,256]{1,0:T(8,128)(2,1)}, u32[]{:S(2)}, u32[]{:S(2)}) collective-permute-start(bf16[2048,256]{1,0:T(8,128)(2,1)} %get-tuple-element.143.x0), channel_id=1, source_target_pairs={{0,1},{1,0},{2,3},{3,2},{4,5},{5,4},{6,7},{7,6},{8,9},{9,8},{10,11... | collective-permute-start | bytes 3145736 | tf_op jit(solution)/shard_map/ppermute | solution.py:330
  247.1 69.2 %collective-permute-start.49 = (bf16[2048,256]{1,0:T(8,128)(2,1)}, bf16[2048,256]{1,0:T(8,128)(2,1)S(1)}, u32[]{:S(2)}, u32[]{:S(2)}) collective-permute-start(bf16[2048,256]{1,0:T(8,128)(2,1)} %get-tuple-element.126), channel_id=1, source_target_pairs={{0,6},{1,7},{2,0},{3,1},{4,2},{5,3},{6,4},{7,5},{8,14},{9,15},{10,... | collective-permute-start | bytes 3145736 | tf_op jit(solution)/shard_map/ppermute | solution.py:327
  271.3 52.5 %collective-permute-start.50 = (bf16[2048,256]{1,0:T(8,128)(2,1)}, bf16[2048,256]{1,0:T(8,128)(2,1)S(1)}, u32[]{:S(2)}, u32[]{:S(2)}) collective-permute-start(bf16[2048,256]{1,0:T(8,128)(2,1)} %get-tuple-element.127), channel_id=1, source_target_pairs={{0,4},{1,5},{2,6},{3,7},{4,0},{5,1},{6,2},{7,3},{8,12},{9,13},{10,... | collective-permute-start | bytes 3145736 | tf_op jit(solution)/shard_map/ppermute | solution.py:327
  271.9 71.4 %collective-permute-start.51 = (bf16[2048,256]{1,0:T(8,128)(2,1)}, bf16[2048,256]{1,0:T(8,128)(2,1)}, u32[]{:S(2)}, u32[]{:S(2)}) collective-permute-start(bf16[2048,256]{1,0:T(8,128)(2,1)} %get-tuple-element.128), channel_id=1, source_target_pairs={{0,2},{1,3},{2,4},{3,5},{4,6},{5,7},{6,0},{7,1},{8,10},{9,11},{10,... | collective-permute-start | bytes 3145736 | tf_op jit(solution)/shard_map/ppermute | solution.py:327
  300.8 60.6 %collective-permute-start.32 = (bf16[2048,256]{1,0:T(8,128)(2,1)}, bf16[2048,256]{1,0:T(8,128)(2,1)}, u32[]{:S(2)}, u32[]{:S(2)}) collective-permute-start(bf16[2048,256]{1,0:T(8,128)(2,1)} %get-tuple-element.108), channel_id=1, source_target_pairs={{0,6},{1,7},{2,0},{3,1},{4,2},{5,3},{6,4},{7,5},{8,14},{9,15},{10,... | collective-permute-start | bytes 3145736 | tf_op jit(solution)/shard_map/ppermute | solution.py:327
  323.8 64.5 %collective-permute-start.34 = (bf16[2048,256]{1,0:T(8,128)(2,1)}, bf16[2048,256]{1,0:T(8,128)(2,1)}, u32[]{:S(2)}, u32[]{:S(2)}) collective-permute-start(bf16[2048,256]{1,0:T(8,128)(2,1)} %get-tuple-element.110), channel_id=1, source_target_pairs={{0,2},{1,3},{2,4},{3,5},{4,6},{5,7},{6,0},{7,1},{8,10},{9,11},{10,... | collective-permute-start | bytes 3145736 | tf_op jit(solution)/shard_map/ppermute | solution.py:327
  343.4 63.0 %collective-permute-start.9 = (bf16[2048,256]{1,0:T(8,128)(2,1)}, bf16[2048,256]{1,0:T(8,128)(2,1)}, u32[]{:S(2)}, u32[]{:S(2)}) collective-permute-start(bf16[2048,256]{1,0:T(8,128)(2,1)} %get-tuple-element.88), channel_id=1, source_target_pairs={{0,6},{1,7},{2,0},{3,1},{4,2},{5,3},{6,4},{7,5},{8,14},{9,15},{10,... | collective-permute-start | bytes 3145736 | tf_op jit(solution)/shard_map/ppermute | solution.py:327
  362.0 55.2 %collective-permute-start.11 = (bf16[2048,256]{1,0:T(8,128)(2,1)}, bf16[2048,256]{1,0:T(8,128)(2,1)}, u32[]{:S(2)}, u32[]{:S(2)}) collective-permute-start(bf16[2048,256]{1,0:T(8,128)(2,1)} %get-tuple-element.90), channel_id=1, source_target_pairs={{0,2},{1,3},{2,4},{3,5},{4,6},{5,7},{6,0},{7,1},{8,10},{9,11},{10,... | collective-permute-start | bytes 3145736 | tf_op jit(solution)/shard_map/ppermute | solution.py:327
  420.7 93.8 %collective-permute-start.14 = (bf16[2048,256]{1,0:T(8,128)(2,1)}, bf16[2048,256]{1,0:T(8,128)(2,1)}, u32[]{:S(2)}, u32[]{:S(2)}) collective-permute-start(bf16[2048,256]{1,0:T(8,128)(2,1)} %collective-permute-done.10.x2), channel_id=1, source_target_pairs={{0,1},{1,0},{2,3},{3,2},{4,5},{5,4},{6,7},{7,6},{8,9},{9,8},{10,11... | collective-permute-start | bytes 3145736 | tf_op jit(solution)/shard_map/ppermute | solution.py:330
  421.1 133.1 %collective-permute-start.15 = (bf16[2048,256]{1,0:T(8,128)(2,1)}, bf16[2048,256]{1,0:T(8,128)(2,1)}, u32[]{:S(2)}, u32[]{:S(2)}) collective-permute-start(bf16[2048,256]{1,0:T(8,128)(2,1)} %collective-permute-done.11.x3), channel_id=1, source_target_pairs={{0,1},{1,0},{2,3},{3,2},{4,5},{5,4},{6,7},{7,6},{8,9},{9,8},{10,11... | collective-permute-start | bytes 3145736 | tf_op jit(solution)/shard_map/ppermute | solution.py:330
  447.5 147.1 %collective-permute-start.53 = (bf16[2048,256]{1,0:T(8,128)(2,1)S(1)}, bf16[2048,256]{1,0:T(8,128)(2,1)S(1)}, u32[]{:S(2)}, u32[]{:S(2)}) collective-permute-start(bf16[2048,256]{1,0:T(8,128)(2,1)S(1)} %collective-permute-done.49.x1), channel_id=1, source_target_pairs={{0,1},{1,0},{2,3},{3,2},{4,5},{5,4},{6,7},{7,6},{8,9},{9,8},{10,11... | collective-permute-start | bytes 3145736 | tf_op jit(solution)/shard_map/ppermute | solution.py:330
  448.0 146.9 %collective-permute-start.54 = (bf16[2048,256]{1,0:T(8,128)(2,1)S(1)}, bf16[2048,256]{1,0:T(8,128)(2,1)}, u32[]{:S(2)}, u32[]{:S(2)}) collective-permute-start(bf16[2048,256]{1,0:T(8,128)(2,1)S(1)} %collective-permute-done.50.x2), channel_id=1, source_target_pairs={{0,1},{1,0},{2,3},{3,2},{4,5},{5,4},{6,7},{7,6},{8,9},{9,8},{10,11... | collective-permute-start | bytes 3145736 | tf_op jit(solution)/shard_map/ppermute | solution.py:330
  448.1 146.7 %collective-permute-start.55 = (bf16[2048,256]{1,0:T(8,128)(2,1)}, bf16[2048,256]{1,0:T(8,128)(2,1)}, u32[]{:S(2)}, u32[]{:S(2)}) collective-permute-start(bf16[2048,256]{1,0:T(8,128)(2,1)} %collective-permute-done.51.x3), channel_id=1, source_target_pairs={{0,1},{1,0},{2,3},{3,2},{4,5},{5,4},{6,7},{7,6},{8,9},{9,8},{10,11... | collective-permute-start | bytes 3145736 | tf_op jit(solution)/shard_map/ppermute | solution.py:330
  514.4 144.1 %collective-permute-start.73 = (bf16[8192,256]{1,0:T(8,128)(2,1)}, bf16[8192,256]{1,0:T(8,128)(2,1)}, u32[]{:S(2)}, u32[]{:S(2)}) collective-permute-start(bf16[8192,256]{1,0:T(8,128)(2,1)} %middle.7.refs_0_.refs_1_.refs_2_.refs_3_), channel_id=1, source_target_pairs={{0,1},{1,0},{2,3},{3,2},{4,5},{5,4},{6,7},{7,6},{8,9},{9,8},{10,11... | collective-permute-start | bytes 12582920 | tf_op jit(solution)/shard_map/ppermute | solution.py:330
  554.2 116.5 %collective-permute-start.39 = (bf16[8192,256]{1,0:T(8,128)(2,1)}, bf16[8192,256]{1,0:T(8,128)(2,1)}, u32[]{:S(2)}, u32[]{:S(2)}) collective-permute-start(bf16[8192,256]{1,0:T(8,128)(2,1)} %middle.5.refs_0_.refs_1_.refs_2_.refs_3_), channel_id=1, source_target_pairs={{0,1},{1,0},{2,3},{3,2},{4,5},{5,4},{6,7},{7,6},{8,9},{9,8},{10,11... | collective-permute-start | bytes 12582920 | tf_op jit(solution)/shard_map/ppermute | solution.py:330
  594.6 86.5 %collective-permute-start.16 = (bf16[8192,256]{1,0:T(8,128)(2,1)}, bf16[8192,256]{1,0:T(8,128)(2,1)}, u32[]{:S(2)}, u32[]{:S(2)}) collective-permute-start(bf16[8192,256]{1,0:T(8,128)(2,1)} %middle.4.refs_0_.refs_1_.refs_2_.refs_3_), channel_id=1, source_target_pairs={{0,1},{1,0},{2,3},{3,2},{4,5},{5,4},{6,7},{7,6},{8,9},{9,8},{10,11... | collective-permute-start | bytes 12582920 | tf_op jit(solution)/shard_map/ppermute | solution.py:330
  635.3 55.8 %collective-permute-start.56 = (bf16[8192,256]{1,0:T(8,128)(2,1)}, bf16[8192,256]{1,0:T(8,128)(2,1)}, u32[]{:S(2)}, u32[]{:S(2)}) collective-permute-start(bf16[8192,256]{1,0:T(8,128)(2,1)} %middle.6.refs_0_.refs_1_.refs_2_.refs_3_), channel_id=1, source_target_pairs={{0,1},{1,0},{2,3},{3,2},{4,5},{5,4},{6,7},{7,6},{8,9},{9,8},{10,11... | collective-permute-start | bytes 12582920 | tf_op jit(solution)/shard_map/ppermute | solution.py:330
  681.2 57.6 %collective-permute-start.40 = (bf16[2048,256]{1,0:T(8,128)(2,1)}, bf16[2048,256]{1,0:T(8,128)(2,1)}, u32[]{:S(2)}, u32[]{:S(2)}) collective-permute-start(bf16[2048,256]{1,0:T(8,128)(2,1)} %get-tuple-element.112), channel_id=1, source_target_pairs={{0,6},{1,7},{2,0},{3,1},{4,2},{5,3},{6,4},{7,5},{8,14},{9,15},{10,... | collective-permute-start | bytes 3145736 | tf_op jit(solution)/shard_map/ppermute | solution.py:327
  691.2 70.1 %collective-permute-start.17 = (bf16[2048,256]{1,0:T(8,128)(2,1)}, bf16[2048,256]{1,0:T(8,128)(2,1)}, u32[]{:S(2)}, u32[]{:S(2)}) collective-permute-start(bf16[2048,256]{1,0:T(8,128)(2,1)} %get-tuple-element.92), channel_id=1, source_target_pairs={{0,6},{1,7},{2,0},{3,1},{4,2},{5,3},{6,4},{7,5},{8,14},{9,15},{10,... | collective-permute-start | bytes 3145736 | tf_op jit(solution)/shard_map/ppermute | solution.py:327
  715.3 106.2 %collective-permute-start.41 = (bf16[2048,256]{1,0:T(8,128)(2,1)}, bf16[2048,256]{1,0:T(8,128)(2,1)}, u32[]{:S(2)}, u32[]{:S(2)}) collective-permute-start(bf16[2048,256]{1,0:T(8,128)(2,1)} %get-tuple-element.113), channel_id=1, source_target_pairs={{0,4},{1,5},{2,6},{3,7},{4,0},{5,1},{6,2},{7,3},{8,12},{9,13},{10,... | collective-permute-start | bytes 3145736 | tf_op jit(solution)/shard_map/ppermute | solution.py:327
  715.3 98.4 %collective-permute-start.18 = (bf16[2048,256]{1,0:T(8,128)(2,1)}, bf16[2048,256]{1,0:T(8,128)(2,1)}, u32[]{:S(2)}, u32[]{:S(2)}) collective-permute-start(bf16[2048,256]{1,0:T(8,128)(2,1)} %get-tuple-element.93), channel_id=1, source_target_pairs={{0,4},{1,5},{2,6},{3,7},{4,0},{5,1},{6,2},{7,3},{8,12},{9,13},{10,... | collective-permute-start | bytes 3145736 | tf_op jit(solution)/shard_map/ppermute | solution.py:327
  719.8 94.0 %collective-permute-start.19 = (bf16[2048,256]{1,0:T(8,128)(2,1)}, bf16[2048,256]{1,0:T(8,128)(2,1)}, u32[]{:S(2)}, u32[]{:S(2)}) collective-permute-start(bf16[2048,256]{1,0:T(8,128)(2,1)} %get-tuple-element.94), channel_id=1, source_target_pairs={{0,2},{1,3},{2,4},{3,5},{4,6},{5,7},{6,0},{7,1},{8,10},{9,11},{10,... | collective-permute-start | bytes 3145736 | tf_op jit(solution)/shard_map/ppermute | solution.py:327
  738.8 85.4 %collective-permute-start.42 = (bf16[2048,256]{1,0:T(8,128)(2,1)}, bf16[2048,256]{1,0:T(8,128)(2,1)}, u32[]{:S(2)}, u32[]{:S(2)}) collective-permute-start(bf16[2048,256]{1,0:T(8,128)(2,1)} %get-tuple-element.114), channel_id=1, source_target_pairs={{0,2},{1,3},{2,4},{3,5},{4,6},{5,7},{6,0},{7,1},{8,10},{9,11},{10,... | collective-permute-start | bytes 3145736 | tf_op jit(solution)/shard_map/ppermute | solution.py:327
  761.3 89.7 %collective-permute-start.57 = (bf16[2048,256]{1,0:T(8,128)(2,1)}, bf16[2048,256]{1,0:T(8,128)(2,1)}, u32[]{:S(2)}, u32[]{:S(2)}) collective-permute-start(bf16[2048,256]{1,0:T(8,128)(2,1)} %get-tuple-element.130), channel_id=1, source_target_pairs={{0,6},{1,7},{2,0},{3,1},{4,2},{5,3},{6,4},{7,5},{8,14},{9,15},{10,... | collective-permute-start | bytes 3145736 | tf_op jit(solution)/shard_map/ppermute | solution.py:327
  821.5 64.9 %collective-permute-start.26 = (bf16[2048,256]{1,0:T(8,128)(2,1)}, bf16[2048,256]{1,0:T(8,128)(2,1)S(1)}, u32[]{:S(2)}, u32[]{:S(2)}) collective-permute-start(bf16[2048,256]{1,0:T(8,128)(2,1)} %get-tuple-element.98), channel_id=1, source_target_pairs={{0,2},{1,3},{2,4},{3,5},{4,6},{5,7},{6,0},{7,1},{8,10},{9,11},{10,... | collective-permute-start | bytes 3145736 | tf_op jit(solution)/shard_map/ppermute | solution.py:327
  824.2 71.6 %collective-permute-start.27 = (bf16[2048,256]{1,0:T(8,128)(2,1)}, bf16[2048,256]{1,0:T(8,128)(2,1)S(1)}, u32[]{:S(2)}, u32[]{:S(2)}) collective-permute-start(bf16[2048,256]{1,0:T(8,128)(2,1)} %get-tuple-element.99), channel_id=1, source_target_pairs={{0,6},{1,7},{2,0},{3,1},{4,2},{5,3},{6,4},{7,5},{8,14},{9,15},{10,... | collective-permute-start | bytes 3145736 | tf_op jit(solution)/shard_map/ppermute | solution.py:327
  851.0 58.2 %collective-permute-start.28 = (bf16[2048,256]{1,0:T(8,128)(2,1)}, bf16[2048,256]{1,0:T(8,128)(2,1)}, u32[]{:S(2)}, u32[]{:S(2)}) collective-permute-start(bf16[2048,256]{1,0:T(8,128)(2,1)} %get-tuple-element.100), channel_id=1, source_target_pairs={{0,4},{1,5},{2,6},{3,7},{4,0},{5,1},{6,2},{7,3},{8,12},{9,13},{10,... | collective-permute-start | bytes 3145736 | tf_op jit(solution)/shard_map/ppermute | solution.py:327
  859.0 72.5 %collective-permute-start.43 = (bf16[2048,256]{1,0:T(8,128)(2,1)}, bf16[2048,256]{1,0:T(8,128)(2,1)}, u32[]{:S(2)}, u32[]{:S(2)}) collective-permute-start(bf16[2048,256]{1,0:T(8,128)(2,1)} %get-tuple-element.116), channel_id=1, source_target_pairs={{0,2},{1,3},{2,4},{3,5},{4,6},{5,7},{6,0},{7,1},{8,10},{9,11},{10,... | collective-permute-start | bytes 3145736 | tf_op jit(solution)/shard_map/ppermute | solution.py:327
  863.7 77.2 %collective-permute-start.44 = (bf16[2048,256]{1,0:T(8,128)(2,1)}, bf16[2048,256]{1,0:T(8,128)(2,1)}, u32[]{:S(2)}, u32[]{:S(2)}) collective-permute-start(bf16[2048,256]{1,0:T(8,128)(2,1)} %get-tuple-element.117), channel_id=1, source_target_pairs={{0,6},{1,7},{2,0},{3,1},{4,2},{5,3},{6,4},{7,5},{8,14},{9,15},{10,... | collective-permute-start | bytes 3145736 | tf_op jit(solution)/shard_map/ppermute | solution.py:327
  886.4 67.4 %collective-permute-start.45 = (bf16[2048,256]{1,0:T(8,128)(2,1)}, bf16[2048,256]{1,0:T(8,128)(2,1)S(1)}, u32[]{:S(2)}, u32[]{:S(2)}) collective-permute-start(bf16[2048,256]{1,0:T(8,128)(2,1)} %get-tuple-element.118), channel_id=1, source_target_pairs={{0,4},{1,5},{2,6},{3,7},{4,0},{5,1},{6,2},{7,3},{8,12},{9,13},{10,... | collective-permute-start | bytes 3145736 | tf_op jit(solution)/shard_map/ppermute | solution.py:327
  895.9 80.4 %collective-permute-start.60 = (bf16[2048,256]{1,0:T(8,128)(2,1)}, bf16[2048,256]{1,0:T(8,128)(2,1)S(1)}, u32[]{:S(2)}, u32[]{:S(2)}) collective-permute-start(bf16[2048,256]{1,0:T(8,128)(2,1)} %get-tuple-element.134), channel_id=1, source_target_pairs={{0,2},{1,3},{2,4},{3,5},{4,6},{5,7},{6,0},{7,1},{8,10},{9,11},{10,... | collective-permute-start | bytes 3145736 | tf_op jit(solution)/shard_map/ppermute | solution.py:327
  909.1 76.6 %collective-permute-start.61 = (bf16[2048,256]{1,0:T(8,128)(2,1)}, bf16[2048,256]{1,0:T(8,128)(2,1)S(1)}, u32[]{:S(2)}, u32[]{:S(2)}) collective-permute-start(bf16[2048,256]{1,0:T(8,128)(2,1)} %get-tuple-element.135), channel_id=1, source_target_pairs={{0,6},{1,7},{2,0},{3,1},{4,2},{5,3},{6,4},{7,5},{8,14},{9,15},{10,... | collective-permute-start | bytes 3145736 | tf_op jit(solution)/shard_map/ppermute | solution.py:327
  931.5 67.3 %collective-permute-start.62 = (bf16[2048,256]{1,0:T(8,128)(2,1)}, bf16[2048,256]{1,0:T(8,128)(2,1)S(1)}, u32[]{:S(2)}, u32[]{:S(2)}) collective-permute-start(bf16[2048,256]{1,0:T(8,128)(2,1)} %get-tuple-element.136), channel_id=1, source_target_pairs={{0,4},{1,5},{2,6},{3,7},{4,0},{5,1},{6,2},{7,3},{8,12},{9,13},{10,... | collective-permute-start | bytes 3145736 | tf_op jit(solution)/shard_map/ppermute | solution.py:327
  940.8 80.3 %collective-permute-start.77 = (bf16[2048,256]{1,0:T(8,128)(2,1)}, bf16[2048,256]{1,0:T(8,128)(2,1)S(1)}, u32[]{:S(2)}, u32[]{:S(2)}) collective-permute-start(bf16[2048,256]{1,0:T(8,128)(2,1)} %get-tuple-element.152), channel_id=1, source_target_pairs={{0,2},{1,3},{2,4},{3,5},{4,6},{5,7},{6,0},{7,1},{8,10},{9,11},{10,... | collective-permute-start | bytes 3145736 | tf_op jit(solution)/shard_map/ppermute | solution.py:327
  953.9 68.3 %collective-permute-start.78 = (bf16[2048,256]{1,0:T(8,128)(2,1)}, bf16[2048,256]{1,0:T(8,128)(2,1)S(1)}, u32[]{:S(2)}, u32[]{:S(2)}) collective-permute-start(bf16[2048,256]{1,0:T(8,128)(2,1)} %get-tuple-element.153), channel_id=1, source_target_pairs={{0,6},{1,7},{2,0},{3,1},{4,2},{5,3},{6,4},{7,5},{8,14},{9,15},{10,... | collective-permute-start | bytes 3145736 | tf_op jit(solution)/shard_map/ppermute | solution.py:327
  976.3 50.5 %collective-permute-start.79 = (bf16[1024,256]{1,0:T(8,128)(2,1)S(1)}, bf16[1024,256]{1,0:T(8,128)(2,1)S(1)}, u32[]{:S(2)}, u32[]{:S(2)}) collective-permute-start(bf16[1024,256]{1,0:T(8,128)(2,1)S(1)} %copy-done.18), channel_id=1, source_target_pairs={{0,4},{1,5},{2,6},{3,7},{4,0},{5,1},{6,2},{7,3},{8,12},{9,13},{10,... | collective-permute-start | bytes 1572872 | tf_op jit(solution)/shard_map/ppermute | solution.py:327
  (54 other events, 2017.7 us)

commit v4 on v3

--- a/solution.py
+++ b/solution.py
@@ -82,7 +82,7 @@
 
 def expand_pair(packed, odd, blk):
     rows = packed[0].shape[0]
-    tile = rows // 8
+    tile = rows // 4
     shape = (CHIPS, LANES, LANES)
     rel, k, n = (lax.broadcasted_iota(jnp.int32, shape, axis) for axis in range(3))
     same = k % blk == n % blk
@@ -294,20 +294,21 @@
 def core_stage(chip, own, mate, core_w, blk):
     total, width = own.shape
     rows = total // CHIPS
-    tile = rows // 8
+    steps = 4
+    tile = rows // steps
 
     def rel_spec(rel):
-        return pl.BlockSpec((tile, width), lambda i, c: (((c[0] + rel) % CHIPS) * 8 + i, 0))
+        return pl.BlockSpec((tile, width), lambda i, c: (((c[0] + rel) % CHIPS) * steps + i, 0))
 
     def w_spec(rel):
-        return pl.BlockSpec((1, tile, LANES), lambda i, c: (8, ((c[0] + rel) % CHIPS) * 8 + i, 0))
+        return pl.BlockSpec((1, tile, LANES), lambda i, c: (8, ((c[0] + rel) % CHIPS) * steps + i, 0))
 
     data = [rel_spec(r) for r in range(CHIPS)]
     return pl.pallas_call(
         functools.partial(core_kernel, blk),
         grid_spec=pltpu.PrefetchScalarGridSpec(
             num_scalar_prefetch=1,
-            grid=(8,),
+            grid=(steps,),
             in_specs=data + data + [w_spec(r) for r in range(CHIPS)],
             out_specs=[pl.BlockSpec((tile, width), lambda i, c: (i, 0))] * 4,
         ),

time: 1040 us -> 1030 us (level)
  waiting for transfers between devices: 450 us -> 509 us
  starting transfers between devices: 183 us -> 135 us
  Pallas kernels: 326 us -> 315 us
    ppermute x55, waiting for transfers between devices: 443 us -> 500 us  [to_chip(): return lax.ppermute(value, 'sp', pairs)]
    ppermute x55, starting transfers between devices: 170 us -> 122 us  [to_chip(): return lax.ppermute(value, 'sp', pairs)]
  transfers between devices with their start and end apart: 81 -> 81, of which waited for: 38 -> 39; matrix products, arithmetic and copies ran while one was open for 6% -> 6% of each run, Pallas kernels for 31% -> 30%
where the time goes in v4:
time: 1030 us
  waiting for transfers between devices  509 us (49%)
  Pallas kernels  315 us (31%)
  starting transfers between devices  135 us (13%)
  local copies, waits for them, and re-layouts  63.8 us (6%)
  other arithmetic  10.5 us (1%)
    ppermute x55, waiting for transfers between devices, to_chip(): return lax.ppermute(value, 'sp', pairs)  500 us
    pallas_call x4, Pallas kernels, middle(): pl.pallas_call(functools.partial(middle_kernel, blk), grid_spec=pltpu.Pre...  159 us
    ppermute x55, starting transfers between devices, to_chip(): return lax.ppermute(value, 'sp', pairs)  122 us
    pallas_call x8, Pallas kernels, chip_stages(): pl.pallas_call(functools.partial(chip_kernel, blk), grid=(rows // tile,),...  55.2 us
    pallas_call x2, Pallas kernels, spread(): pl.pallas_call(functools.partial(spread_kernel, first_map), grid=(5,), in...  52.5 us
    pallas_call x4, Pallas kernels, core_stage(): pl.pallas_call(functools.partial(core_kernel, blk), grid_spec=pltpu.Prefe...  26.4 us
    dynamic_slice x10, local copies, waits for them, and re-layouts, quarter(): return lax.dynamic_slice(array, (start, col), (group, wide))  24.5 us
    dynamic_update_slice x17, local copies, waits for them, and re-layouts, device_program(): result = lax.dynamic_update_slice(result, piece, at)  23.3 us
  transfers between devices with their start and end apart: 81, of which 39 were waited for; matrix products, arithmetic and copies ran while one was open for 6% of the time, Pallas kernels for 30%

profile of v4, /device:TPU:112, one launch (start us, length us, event | category | flops | bytes accessed | tf_op | source)
XLA Modules:
  0.0 1033.4 jit_solution(8561015307104788824)
XLA Ops:
  47.0 29.3 %collective-permute-done.3 = bf16[1024,128]{1,0:T(8,128)(2,1)} collective-permute-done((bf16[1024,128]{1,0:T(8,128)(2,1)}, bf16[1024,128]{1,0:T(8,128)(2,1)}, u32[]{:S(2)}, u32[]{:S(2)}) %collective-permute-start.3) | collective-permute-done | bytes 262176 | tf_op jit(solution)/shard_map/ppermute | solution.py:328
  101.0 11.0 %collective-permute-done.64.x2 = bf16[2048,256]{1,0:T(8,128)(2,1)} collective-permute-done((bf16[2048,256]{1,0:T(8,128)(2,1)S(1)}, bf16[2048,256]{1,0:T(8,128)(2,1)}, u32[]{:S(2)}, u32[]{:S(2)}) %collective-permute-start.64) | collective-permute-done | bytes 1048608 | tf_op jit(solution)/shard_map/ppermute | solution.py:328
  114.0 22.5 %collective-permute-done.46.x1 = bf16[2048,256]{1,0:T(8,128)(2,1)} collective-permute-done((bf16[2048,256]{1,0:T(8,128)(2,1)}, bf16[2048,256]{1,0:T(8,128)(2,1)}, u32[]{:S(2)}, u32[]{:S(2)}) %collective-permute-start.46) | collective-permute-done | bytes 1048608 | tf_op jit(solution)/shard_map/ppermute | solution.py:328
  143.9 13.2 %collective-permute-done.47.x2 = bf16[2048,256]{1,0:T(8,128)(2,1)} collective-permute-done((bf16[2048,256]{1,0:T(8,128)(2,1)S(1)}, bf16[2048,256]{1,0:T(8,128)(2,1)}, u32[]{:S(2)}, u32[]{:S(2)}) %collective-permute-start.47) | collective-permute-done | bytes 1048608 | tf_op jit(solution)/shard_map/ppermute | solution.py:328
  159.8 21.6 %collective-permute-done.29.x1 = bf16[2048,256]{1,0:T(8,128)(2,1)} collective-permute-done((bf16[2048,256]{1,0:T(8,128)(2,1)}, bf16[2048,256]{1,0:T(8,128)(2,1)}, u32[]{:S(2)}, u32[]{:S(2)}) %collective-permute-start.29) | collective-permute-done | bytes 1048608 | tf_op jit(solution)/shard_map/ppermute | solution.py:328
  188.2 6.9 chip_stages.14
  202.1 24.4 %collective-permute-done.x1 = bf16[2048,256]{1,0:T(8,128)(2,1)} collective-permute-done((bf16[2048,256]{1,0:T(8,128)(2,1)}, bf16[2048,256]{1,0:T(8,128)(2,1)}, u32[]{:S(2)}, u32[]{:S(2)}) %collective-permute-start) | collective-permute-done | bytes 1048608 | tf_op jit(solution)/shard_map/ppermute | solution.py:328
  226.5 6.9 chip_stages.12
  233.4 13.7 %collective-permute-done.1.x2 = bf16[2048,256]{1,0:T(8,128)(2,1)} collective-permute-done((bf16[2048,256]{1,0:T(8,128)(2,1)S(1)}, bf16[2048,256]{1,0:T(8,128)(2,1)}, u32[]{:S(2)}, u32[]{:S(2)}) %collective-permute-start.1) | collective-permute-done | bytes 1048608 | tf_op jit(solution)/shard_map/ppermute | solution.py:328
  251.6 19.7 %collective-permute-done.66.x1 = bf16[2048,256]{1,0:T(8,128)(2,1)S(1)} collective-permute-done((bf16[2048,256]{1,0:T(8,128)(2,1)}, bf16[2048,256]{1,0:T(8,128)(2,1)S(1)}, u32[]{:S(2)}, u32[]{:S(2)}) %collective-permute-start.66) | collective-permute-done | bytes 1048608 | tf_op jit(solution)/shard_map/ppermute | solution.py:328
  271.9 22.0 %collective-permute-start.51 = (bf16[2048,256]{1,0:T(8,128)(2,1)}, bf16[2048,256]{1,0:T(8,128)(2,1)}, u32[]{:S(2)}, u32[]{:S(2)}) collective-permute-start(bf16[2048,256]{1,0:T(8,128)(2,1)} %get-tuple-element.128), channel_id=1, source_target_pairs={{0,2},{1,3},{2,4},{3,5},{4,6},{5,7},{6,0},{7,1},{8,10},{9,11},{10,... | collective-permute-start | bytes 3145736 | tf_op jit(solution)/shard_map/ppermute | solution.py:328
  294.0 6.9 chip_stages.10
  303.6 12.7 %collective-permute-done.49.x1 = bf16[2048,256]{1,0:T(8,128)(2,1)S(1)} collective-permute-done((bf16[2048,256]{1,0:T(8,128)(2,1)}, bf16[2048,256]{1,0:T(8,128)(2,1)S(1)}, u32[]{:S(2)}, u32[]{:S(2)}) %collective-permute-start.49) | collective-permute-done | bytes 1048608 | tf_op jit(solution)/shard_map/ppermute | solution.py:328
  316.9 6.9 chip_stages.8
  323.8 15.0 %collective-permute-start.34 = (bf16[2048,256]{1,0:T(8,128)(2,1)}, bf16[2048,256]{1,0:T(8,128)(2,1)}, u32[]{:S(2)}, u32[]{:S(2)}) collective-permute-start(bf16[2048,256]{1,0:T(8,128)(2,1)} %get-tuple-element.110), channel_id=1, source_target_pairs={{0,2},{1,3},{2,4},{3,5},{4,6},{5,7},{6,0},{7,1},{8,10},{9,11},{10,... | collective-permute-start | bytes 3145736 | tf_op jit(solution)/shard_map/ppermute | solution.py:328
  343.4 18.0 %collective-permute-done.32.x1 = bf16[2048,256]{1,0:T(8,128)(2,1)} collective-permute-done((bf16[2048,256]{1,0:T(8,128)(2,1)}, bf16[2048,256]{1,0:T(8,128)(2,1)}, u32[]{:S(2)}, u32[]{:S(2)}) %collective-permute-start.32) | collective-permute-done | bytes 1048608 | tf_op jit(solution)/shard_map/ppermute | solution.py:328
  362.0 21.9 %collective-permute-start.11 = (bf16[2048,256]{1,0:T(8,128)(2,1)}, bf16[2048,256]{1,0:T(8,128)(2,1)}, u32[]{:S(2)}, u32[]{:S(2)}) collective-permute-start(bf16[2048,256]{1,0:T(8,128)(2,1)} %get-tuple-element.90), channel_id=1, source_target_pairs={{0,2},{1,3},{2,4},{3,5},{4,6},{5,7},{6,0},{7,1},{8,10},{9,11},{10,... | collective-permute-start | bytes 3145736 | tf_op jit(solution)/shard_map/ppermute | solution.py:328
  388.8 17.6 %collective-permute-done.9.x1 = bf16[2048,256]{1,0:T(8,128)(2,1)} collective-permute-done((bf16[2048,256]{1,0:T(8,128)(2,1)}, bf16[2048,256]{1,0:T(8,128)(2,1)}, u32[]{:S(2)}, u32[]{:S(2)}) %collective-permute-start.9) | collective-permute-done | bytes 1048608 | tf_op jit(solution)/shard_map/ppermute | solution.py:328
  406.9 10.3 collective-permute-done.11.x3
  421.2 26.3 %spread.3.second_w.refs_8_.refs_9_.refs_10_.refs_11_ = bf16[10,8192,128]{2,1,0:T(8,128)(2,1)} custom-call(bf16[11,2,32,32,256]{4,3,2,1,0:T(8,128)(2,1)} %bitcast.5, bf16[11,2,32,32,256]{4,3,2,1,0:T(8,128)(2,1)} %bitcast.6), custom_call_target="tpu_custom_call" | custom-call | flops 2500000000 | bytes 2500000 | tf_op jit(solution)/shard_map/spread/pallas_call | solution.py:146
  448.5 26.2 %spread.2.core_w.first_w = bf16[10,8192,128]{2,1,0:T(8,128)(2,1)} custom-call(bf16[11,2,32,32,256]{4,3,2,1,0:T(8,128)(2,1)} %bitcast.9, bf16[11,2,32,32,256]{4,3,2,1,0:T(8,128)(2,1)} %bitcast.10), custom_call_target="tpu_custom_call" | custom-call | flops 2500000000 | bytes 2500000 | tf_op jit(solution)/shard_map/spread/pallas_call | solution.py:146
  474.7 39.8 %middle.7.refs_0_.refs_1_.refs_2_.refs_3_ = bf16[8192,256]{1,0:T(8,128)(2,1)} custom-call(s32[1]{0:T(128)} %bitcast.chip_ref, bf16[2048,256]{1,0:T(8,128)(2,1)} %get-tuple-element.143.x0, bf16[2048,256]{1,0:T(8,128)(2,1)} %copy-done.2, bf16[2048,256]{1,0:T(8,128)(2,1)} %collective-permute-done.67.x2, bf16[2048,256]{1,0:T(8,128)(2,1)} %collective-permute-done.68.x3, ...), custom_call_target="tpu_custom_call" | custom-call | flops 3500000000 | bytes 3500000 | tf_op jit(solution)/shard_map/middle/pallas_call | solution.py:263
  514.6 39.6 %middle.5.refs_0_.refs_1_.refs_2_.refs_3_ = bf16[8192,256]{1,0:T(8,128)(2,1)} custom-call(s32[1]{0:T(128)} %bitcast.chip_ref, bf16[2048,256]{1,0:T(8,128)(2,1)} %get-tuple-element.107.x0, bf16[2048,256]{1,0:T(8,128)(2,1)} %collective-permute-done.32.x1, bf16[2048,256]{1,0:T(8,128)(2,1)} %collective-permute-done.33.x2, ...), custom_call_target="tpu_custom_call" | custom-call | flops 3500000000 | bytes 3500000 | tf_op jit(solution)/shard_map/middle/pallas_call | solution.py:263
  554.7 39.9 %middle.4.refs_0_.refs_1_.refs_2_.refs_3_ = bf16[8192,256]{1,0:T(8,128)(2,1)} custom-call(s32[1]{0:T(128)} %bitcast.chip_ref, bf16[2048,256]{1,0:T(8,128)(2,1)} %get-tuple-element.87.x0, bf16[2048,256]{1,0:T(8,128)(2,1)} %collective-permute-done.9.x1, bf16[2048,256]{1,0:T(8,128)(2,1)} %collective-permute-done.10.x2, ...), custom_call_target="tpu_custom_call" | custom-call | flops 3500000000 | bytes 3500000 | tf_op jit(solution)/shard_map/middle/pallas_call | solution.py:263
  595.6 39.7 %middle.6.refs_0_.refs_1_.refs_2_.refs_3_ = bf16[8192,256]{1,0:T(8,128)(2,1)} custom-call(s32[1]{0:T(128)} %bitcast.chip_ref, bf16[2048,256]{1,0:T(8,128)(2,1)} %get-tuple-element.125.x0, bf16[2048,256]{1,0:T(8,128)(2,1)} %copy-done, bf16[2048,256]{1,0:T(8,128)(2,1)} %copy-done.1, bf16[2048,256]{1,0:T(8,128)(2,1)} %collective-permute-done.51.x3, ...), custom_call_target="tpu_custom_call" | custom-call | flops 3500000000 | bytes 3500000 | tf_op jit(solution)/shard_map/middle/pallas_call | solution.py:263
  637.3 8.3 collective-permute-done.22
  649.2 7.5 collective-permute-done.24
  658.7 6.8 core_stage.7
  672.6 6.6 core_stage.5
  690.0 23.6 %collective-permute-done.74.x1 = bf16[2048,256]{1,0:T(8,128)(2,1)S(1)} collective-permute-done((bf16[2048,256]{1,0:T(8,128)(2,1)}, bf16[2048,256]{1,0:T(8,128)(2,1)S(1)}, u32[]{:S(2)}, u32[]{:S(2)}) %collective-permute-start.74) | collective-permute-done | bytes 1048608 | tf_op jit(solution)/shard_map/ppermute | solution.py:328
  721.0 16.1 %collective-permute-done.40.x1 = bf16[2048,256]{1,0:T(8,128)(2,1)} collective-permute-done((bf16[2048,256]{1,0:T(8,128)(2,1)}, bf16[2048,256]{1,0:T(8,128)(2,1)}, u32[]{:S(2)}, u32[]{:S(2)}) %collective-permute-start.40) | collective-permute-done | bytes 1048608 | tf_op jit(solution)/shard_map/ppermute | solution.py:328
  744.8 54.2 %collective-permute-done.17.x1 = bf16[2048,256]{1,0:T(8,128)(2,1)} collective-permute-done((bf16[2048,256]{1,0:T(8,128)(2,1)}, bf16[2048,256]{1,0:T(8,128)(2,1)}, u32[]{:S(2)}, u32[]{:S(2)}) %collective-permute-start.17) | collective-permute-done | bytes 1048608 | tf_op jit(solution)/shard_map/ppermute | solution.py:328
  811.1 6.9 chip_stages.9
  821.3 7.0 chip_stages.15
  828.3 6.9 chip_stages.11
  835.2 14.2 %collective-permute-done.57.x1 = bf16[2048,256]{1,0:T(8,128)(2,1)} collective-permute-done((bf16[2048,256]{1,0:T(8,128)(2,1)}, bf16[2048,256]{1,0:T(8,128)(2,1)}, u32[]{:S(2)}, u32[]{:S(2)}) %collective-permute-start.57) | collective-permute-done | bytes 1048608 | tf_op jit(solution)/shard_map/ppermute | solution.py:328
  862.0 6.9 chip_stages.13
  868.9 14.0 %collective-permute-done.26 = bf16[2048,256]{1,0:T(8,128)(2,1)S(1)} collective-permute-done((bf16[2048,256]{1,0:T(8,128)(2,1)}, bf16[2048,256]{1,0:T(8,128)(2,1)S(1)}, u32[]{:S(2)}, u32[]{:S(2)}) %collective-permute-start.26) | collective-permute-done | bytes 1048608 | tf_op jit(solution)/shard_map/ppermute | solution.py:328
  884.0 10.3 collective-permute-done.27
  895.3 10.2 collective-permute-done.28
  910.0 18.0 %collective-permute-done.43 = bf16[2048,256]{1,0:T(8,128)(2,1)} collective-permute-done((bf16[2048,256]{1,0:T(8,128)(2,1)}, bf16[2048,256]{1,0:T(8,128)(2,1)}, u32[]{:S(2)}, u32[]{:S(2)}) %collective-permute-start.43) | collective-permute-done | bytes 1048608 | tf_op jit(solution)/shard_map/ppermute | solution.py:328
  930.3 8.9 collective-permute-done.44
  941.5 8.9 collective-permute-done.45
  953.7 19.1 %collective-permute-done.60 = bf16[2048,256]{1,0:T(8,128)(2,1)S(1)} collective-permute-done((bf16[2048,256]{1,0:T(8,128)(2,1)}, bf16[2048,256]{1,0:T(8,128)(2,1)S(1)}, u32[]{:S(2)}, u32[]{:S(2)}) %collective-permute-start.60) | collective-permute-done | bytes 1048608 | tf_op jit(solution)/shard_map/ppermute | solution.py:328
  973.8 10.3 collective-permute-done.61
  985.2 10.2 collective-permute-done.62
  997.4 20.0 %collective-permute-done.77 = bf16[2048,256]{1,0:T(8,128)(2,1)S(1)} collective-permute-done((bf16[2048,256]{1,0:T(8,128)(2,1)}, bf16[2048,256]{1,0:T(8,128)(2,1)S(1)}, u32[]{:S(2)}, u32[]{:S(2)}) %collective-permute-start.77) | collective-permute-done | bytes 1048608 | tf_op jit(solution)/shard_map/ppermute | solution.py:328
  1019.5 7.5 collective-permute-done.79
  (223 shorter events, 219.0 us)
Async XLA Ops:
  39.6 54.2 %collective-permute-start.63 = (bf16[2048,256]{1,0:T(8,128)(2,1)}, bf16[2048,256]{1,0:T(8,128)(2,1)}, u32[]{:S(2)}, u32[]{:S(2)}) collective-permute-start(bf16[2048,256]{1,0:T(8,128)(2,1)} %get-tuple-element.140), channel_id=1, source_target_pairs={{0,6},{1,7},{2,0},{3,1},{4,2},{5,3},{6,4},{7,5},{8,14},{9,15},{10,... | collective-permute-start | bytes 3145736 | tf_op jit(solution)/shard_map/ppermute | solution.py:328
  45.8 52.2 %collective-permute-start.65 = (bf16[2048,256]{1,0:T(8,128)(2,1)}, bf16[2048,256]{1,0:T(8,128)(2,1)}, u32[]{:S(2)}, u32[]{:S(2)}) collective-permute-start(bf16[2048,256]{1,0:T(8,128)(2,1)} %get-tuple-element.142), channel_id=1, source_target_pairs={{0,2},{1,3},{2,4},{3,5},{4,6},{5,7},{6,0},{7,1},{8,10},{9,11},{10,... | collective-permute-start | bytes 3145736 | tf_op jit(solution)/shard_map/ppermute | solution.py:328
  93.8 63.3 %collective-permute-start.47 = (bf16[2048,256]{1,0:T(8,128)(2,1)S(1)}, bf16[2048,256]{1,0:T(8,128)(2,1)}, u32[]{:S(2)}, u32[]{:S(2)}) collective-permute-start(bf16[2048,256]{1,0:T(8,128)(2,1)S(1)} %constant_dynamic-slice_fusion.19), channel_id=1, source_target_pairs={{0,4},{1,5},{2,6},{3,7},{4,0},{5,1},{6,2},{7,3},{8,12},{9,13},{10,... | collective-permute-start | bytes 3145736 | tf_op jit(solution)/shard_map/ppermute | solution.py:328
  98.0 83.4 %collective-permute-start.29 = (bf16[2048,256]{1,0:T(8,128)(2,1)}, bf16[2048,256]{1,0:T(8,128)(2,1)}, u32[]{:S(2)}, u32[]{:S(2)}) collective-permute-start(bf16[2048,256]{1,0:T(8,128)(2,1)} %get-tuple-element.104), channel_id=1, source_target_pairs={{0,6},{1,7},{2,0},{3,1},{4,2},{5,3},{6,4},{7,5},{8,14},{9,15},{10,... | collective-permute-start | bytes 3145736 | tf_op jit(solution)/shard_map/ppermute | solution.py:328
  112.1 83.0 %collective-permute-start.31 = (bf16[2048,256]{1,0:T(8,128)(2,1)}, bf16[2048,256]{1,0:T(8,128)(2,1)S(1)}, u32[]{:S(2)}, u32[]{:S(2)}) collective-permute-start(bf16[2048,256]{1,0:T(8,128)(2,1)} %get-tuple-element.106), channel_id=1, source_target_pairs={{0,2},{1,3},{2,4},{3,5},{4,6},{5,7},{6,0},{7,1},{8,10},{9,11},{10,... | collective-permute-start | bytes 3145736 | tf_op jit(solution)/shard_map/ppermute | solution.py:328
  136.5 65.6 %collective-permute-start.30 = (bf16[2048,256]{1,0:T(8,128)(2,1)}, bf16[2048,256]{1,0:T(8,128)(2,1)}, u32[]{:S(2)}, u32[]{:S(2)}) collective-permute-start(bf16[2048,256]{1,0:T(8,128)(2,1)} %constant_dynamic-slice_fusion.23), channel_id=1, source_target_pairs={{0,4},{1,5},{2,6},{3,7},{4,0},{5,1},{6,2},{7,3},{8,12},{9,13},{10,... | collective-permute-start | bytes 3145736 | tf_op jit(solution)/shard_map/ppermute | solution.py:328
  141.8 84.6 %collective-permute-start = (bf16[2048,256]{1,0:T(8,128)(2,1)}, bf16[2048,256]{1,0:T(8,128)(2,1)}, u32[]{:S(2)}, u32[]{:S(2)}) collective-permute-start(bf16[2048,256]{1,0:T(8,128)(2,1)} %get-tuple-element.82), channel_id=1, source_target_pairs={{0,6},{1,7},{2,0},{3,1},{4,2},{5,3},{6,4},{7,5},{8,14},{9,15},{10,... | collective-permute-start | bytes 3145736 | tf_op jit(solution)/shard_map/ppermute | solution.py:328
  157.1 69.4 %collective-permute-start.2 = (bf16[2048,256]{1,0:T(8,128)(2,1)}, bf16[2048,256]{1,0:T(8,128)(2,1)}, u32[]{:S(2)}, u32[]{:S(2)}) collective-permute-start(bf16[2048,256]{1,0:T(8,128)(2,1)} %get-tuple-element.84), channel_id=1, source_target_pairs={{0,2},{1,3},{2,4},{3,5},{4,6},{5,7},{6,0},{7,1},{8,10},{9,11},{10,... | collective-permute-start | bytes 3145736 | tf_op jit(solution)/shard_map/ppermute | solution.py:328
  181.5 65.6 %collective-permute-start.1 = (bf16[2048,256]{1,0:T(8,128)(2,1)S(1)}, bf16[2048,256]{1,0:T(8,128)(2,1)}, u32[]{:S(2)}, u32[]{:S(2)}) collective-permute-start(bf16[2048,256]{1,0:T(8,128)(2,1)S(1)} %constant_dynamic-slice_fusion.11), channel_id=1, source_target_pairs={{0,4},{1,5},{2,6},{3,7},{4,0},{5,1},{6,2},{7,3},{8,12},{9,13},{10,... | collective-permute-start | bytes 3145736 | tf_op jit(solution)/shard_map/ppermute | solution.py:328
  196.2 75.2 %collective-permute-start.66 = (bf16[2048,256]{1,0:T(8,128)(2,1)}, bf16[2048,256]{1,0:T(8,128)(2,1)S(1)}, u32[]{:S(2)}, u32[]{:S(2)}) collective-permute-start(bf16[2048,256]{1,0:T(8,128)(2,1)} %get-tuple-element.144), channel_id=1, source_target_pairs={{0,6},{1,7},{2,0},{3,1},{4,2},{5,3},{6,4},{7,5},{8,14},{9,15},{10,... | collective-permute-start | bytes 3145736 | tf_op jit(solution)/shard_map/ppermute | solution.py:328
  202.1 69.9 %collective-permute-start.67 = (bf16[2048,256]{1,0:T(8,128)(2,1)}, bf16[2048,256]{1,0:T(8,128)(2,1)}, u32[]{:S(2)}, u32[]{:S(2)}) collective-permute-start(bf16[2048,256]{1,0:T(8,128)(2,1)} %get-tuple-element.145), channel_id=1, source_target_pairs={{0,4},{1,5},{2,6},{3,7},{4,0},{5,1},{6,2},{7,3},{8,12},{9,13},{10,... | collective-permute-start | bytes 3145736 | tf_op jit(solution)/shard_map/ppermute | solution.py:328
  226.4 67.5 %collective-permute-start.68 = (bf16[2048,256]{1,0:T(8,128)(2,1)}, bf16[2048,256]{1,0:T(8,128)(2,1)}, u32[]{:S(2)}, u32[]{:S(2)}) collective-permute-start(bf16[2048,256]{1,0:T(8,128)(2,1)} %get-tuple-element.146), channel_id=1, source_target_pairs={{0,2},{1,3},{2,4},{3,5},{4,6},{5,7},{6,0},{7,1},{8,10},{9,11},{10,... | collective-permute-start | bytes 3145736 | tf_op jit(solution)/shard_map/ppermute | solution.py:328
  226.5 74.4 %collective-permute-start.69 = (bf16[2048,256]{1,0:T(8,128)(2,1)}, bf16[2048,256]{1,0:T(8,128)(2,1)}, u32[]{:S(2)}, u32[]{:S(2)}) collective-permute-start(bf16[2048,256]{1,0:T(8,128)(2,1)} %get-tuple-element.143.x0), channel_id=1, source_target_pairs={{0,1},{1,0},{2,3},{3,2},{4,5},{5,4},{6,7},{7,6},{8,9},{9,8},{10,11... | collective-permute-start | bytes 3145736 | tf_op jit(solution)/shard_map/ppermute | solution.py:331
  247.1 69.2 %collective-permute-start.49 = (bf16[2048,256]{1,0:T(8,128)(2,1)}, bf16[2048,256]{1,0:T(8,128)(2,1)S(1)}, u32[]{:S(2)}, u32[]{:S(2)}) collective-permute-start(bf16[2048,256]{1,0:T(8,128)(2,1)} %get-tuple-element.126), channel_id=1, source_target_pairs={{0,6},{1,7},{2,0},{3,1},{4,2},{5,3},{6,4},{7,5},{8,14},{9,15},{10,... | collective-permute-start | bytes 3145736 | tf_op jit(solution)/shard_map/ppermute | solution.py:328
  271.3 52.5 %collective-permute-start.50 = (bf16[2048,256]{1,0:T(8,128)(2,1)}, bf16[2048,256]{1,0:T(8,128)(2,1)S(1)}, u32[]{:S(2)}, u32[]{:S(2)}) collective-permute-start(bf16[2048,256]{1,0:T(8,128)(2,1)} %get-tuple-element.127), channel_id=1, source_target_pairs={{0,4},{1,5},{2,6},{3,7},{4,0},{5,1},{6,2},{7,3},{8,12},{9,13},{10,... | collective-permute-start | bytes 3145736 | tf_op jit(solution)/shard_map/ppermute | solution.py:328
  271.9 71.4 %collective-permute-start.51 = (bf16[2048,256]{1,0:T(8,128)(2,1)}, bf16[2048,256]{1,0:T(8,128)(2,1)}, u32[]{:S(2)}, u32[]{:S(2)}) collective-permute-start(bf16[2048,256]{1,0:T(8,128)(2,1)} %get-tuple-element.128), channel_id=1, source_target_pairs={{0,2},{1,3},{2,4},{3,5},{4,6},{5,7},{6,0},{7,1},{8,10},{9,11},{10,... | collective-permute-start | bytes 3145736 | tf_op jit(solution)/shard_map/ppermute | solution.py:328
  300.8 60.6 %collective-permute-start.32 = (bf16[2048,256]{1,0:T(8,128)(2,1)}, bf16[2048,256]{1,0:T(8,128)(2,1)}, u32[]{:S(2)}, u32[]{:S(2)}) collective-permute-start(bf16[2048,256]{1,0:T(8,128)(2,1)} %get-tuple-element.108), channel_id=1, source_target_pairs={{0,6},{1,7},{2,0},{3,1},{4,2},{5,3},{6,4},{7,5},{8,14},{9,15},{10,... | collective-permute-start | bytes 3145736 | tf_op jit(solution)/shard_map/ppermute | solution.py:328
  323.8 64.5 %collective-permute-start.34 = (bf16[2048,256]{1,0:T(8,128)(2,1)}, bf16[2048,256]{1,0:T(8,128)(2,1)}, u32[]{:S(2)}, u32[]{:S(2)}) collective-permute-start(bf16[2048,256]{1,0:T(8,128)(2,1)} %get-tuple-element.110), channel_id=1, source_target_pairs={{0,2},{1,3},{2,4},{3,5},{4,6},{5,7},{6,0},{7,1},{8,10},{9,11},{10,... | collective-permute-start | bytes 3145736 | tf_op jit(solution)/shard_map/ppermute | solution.py:328
  343.4 63.0 %collective-permute-start.9 = (bf16[2048,256]{1,0:T(8,128)(2,1)}, bf16[2048,256]{1,0:T(8,128)(2,1)}, u32[]{:S(2)}, u32[]{:S(2)}) collective-permute-start(bf16[2048,256]{1,0:T(8,128)(2,1)} %get-tuple-element.88), channel_id=1, source_target_pairs={{0,6},{1,7},{2,0},{3,1},{4,2},{5,3},{6,4},{7,5},{8,14},{9,15},{10,... | collective-permute-start | bytes 3145736 | tf_op jit(solution)/shard_map/ppermute | solution.py:328
  362.0 55.2 %collective-permute-start.11 = (bf16[2048,256]{1,0:T(8,128)(2,1)}, bf16[2048,256]{1,0:T(8,128)(2,1)}, u32[]{:S(2)}, u32[]{:S(2)}) collective-permute-start(bf16[2048,256]{1,0:T(8,128)(2,1)} %get-tuple-element.90), channel_id=1, source_target_pairs={{0,2},{1,3},{2,4},{3,5},{4,6},{5,7},{6,0},{7,1},{8,10},{9,11},{10,... | collective-permute-start | bytes 3145736 | tf_op jit(solution)/shard_map/ppermute | solution.py:328
  420.7 93.8 %collective-permute-start.14 = (bf16[2048,256]{1,0:T(8,128)(2,1)}, bf16[2048,256]{1,0:T(8,128)(2,1)}, u32[]{:S(2)}, u32[]{:S(2)}) collective-permute-start(bf16[2048,256]{1,0:T(8,128)(2,1)} %collective-permute-done.10.x2), channel_id=1, source_target_pairs={{0,1},{1,0},{2,3},{3,2},{4,5},{5,4},{6,7},{7,6},{8,9},{9,8},{10,11... | collective-permute-start | bytes 3145736 | tf_op jit(solution)/shard_map/ppermute | solution.py:331
  421.1 133.1 %collective-permute-start.15 = (bf16[2048,256]{1,0:T(8,128)(2,1)}, bf16[2048,256]{1,0:T(8,128)(2,1)}, u32[]{:S(2)}, u32[]{:S(2)}) collective-permute-start(bf16[2048,256]{1,0:T(8,128)(2,1)} %collective-permute-done.11.x3), channel_id=1, source_target_pairs={{0,1},{1,0},{2,3},{3,2},{4,5},{5,4},{6,7},{7,6},{8,9},{9,8},{10,11... | collective-permute-start | bytes 3145736 | tf_op jit(solution)/shard_map/ppermute | solution.py:331
  447.5 147.1 %collective-permute-start.53 = (bf16[2048,256]{1,0:T(8,128)(2,1)S(1)}, bf16[2048,256]{1,0:T(8,128)(2,1)S(1)}, u32[]{:S(2)}, u32[]{:S(2)}) collective-permute-start(bf16[2048,256]{1,0:T(8,128)(2,1)S(1)} %collective-permute-done.49.x1), channel_id=1, source_target_pairs={{0,1},{1,0},{2,3},{3,2},{4,5},{5,4},{6,7},{7,6},{8,9},{9,8},{10,11... | collective-permute-start | bytes 3145736 | tf_op jit(solution)/shard_map/ppermute | solution.py:331
  448.0 146.9 %collective-permute-start.54 = (bf16[2048,256]{1,0:T(8,128)(2,1)S(1)}, bf16[2048,256]{1,0:T(8,128)(2,1)}, u32[]{:S(2)}, u32[]{:S(2)}) collective-permute-start(bf16[2048,256]{1,0:T(8,128)(2,1)S(1)} %collective-permute-done.50.x2), channel_id=1, source_target_pairs={{0,1},{1,0},{2,3},{3,2},{4,5},{5,4},{6,7},{7,6},{8,9},{9,8},{10,11... | collective-permute-start | bytes 3145736 | tf_op jit(solution)/shard_map/ppermute | solution.py:331
  448.1 146.7 %collective-permute-start.55 = (bf16[2048,256]{1,0:T(8,128)(2,1)}, bf16[2048,256]{1,0:T(8,128)(2,1)}, u32[]{:S(2)}, u32[]{:S(2)}) collective-permute-start(bf16[2048,256]{1,0:T(8,128)(2,1)} %collective-permute-done.51.x3), channel_id=1, source_target_pairs={{0,1},{1,0},{2,3},{3,2},{4,5},{5,4},{6,7},{7,6},{8,9},{9,8},{10,11... | collective-permute-start | bytes 3145736 | tf_op jit(solution)/shard_map/ppermute | solution.py:331
  514.4 144.1 %collective-permute-start.73 = (bf16[8192,256]{1,0:T(8,128)(2,1)}, bf16[8192,256]{1,0:T(8,128)(2,1)}, u32[]{:S(2)}, u32[]{:S(2)}) collective-permute-start(bf16[8192,256]{1,0:T(8,128)(2,1)} %middle.7.refs_0_.refs_1_.refs_2_.refs_3_), channel_id=1, source_target_pairs={{0,1},{1,0},{2,3},{3,2},{4,5},{5,4},{6,7},{7,6},{8,9},{9,8},{10,11... | collective-permute-start | bytes 12582920 | tf_op jit(solution)/shard_map/ppermute | solution.py:331
  554.2 116.5 %collective-permute-start.39 = (bf16[8192,256]{1,0:T(8,128)(2,1)}, bf16[8192,256]{1,0:T(8,128)(2,1)}, u32[]{:S(2)}, u32[]{:S(2)}) collective-permute-start(bf16[8192,256]{1,0:T(8,128)(2,1)} %middle.5.refs_0_.refs_1_.refs_2_.refs_3_), channel_id=1, source_target_pairs={{0,1},{1,0},{2,3},{3,2},{4,5},{5,4},{6,7},{7,6},{8,9},{9,8},{10,11... | collective-permute-start | bytes 12582920 | tf_op jit(solution)/shard_map/ppermute | solution.py:331
  594.6 84.5 %collective-permute-start.16 = (bf16[8192,256]{1,0:T(8,128)(2,1)}, bf16[8192,256]{1,0:T(8,128)(2,1)}, u32[]{:S(2)}, u32[]{:S(2)}) collective-permute-start(bf16[8192,256]{1,0:T(8,128)(2,1)} %middle.4.refs_0_.refs_1_.refs_2_.refs_3_), channel_id=1, source_target_pairs={{0,1},{1,0},{2,3},{3,2},{4,5},{5,4},{6,7},{7,6},{8,9},{9,8},{10,11... | collective-permute-start | bytes 12582920 | tf_op jit(solution)/shard_map/ppermute | solution.py:331
  635.3 51.9 %collective-permute-start.56 = (bf16[8192,256]{1,0:T(8,128)(2,1)}, bf16[8192,256]{1,0:T(8,128)(2,1)}, u32[]{:S(2)}, u32[]{:S(2)}) collective-permute-start(bf16[8192,256]{1,0:T(8,128)(2,1)} %middle.6.refs_0_.refs_1_.refs_2_.refs_3_), channel_id=1, source_target_pairs={{0,1},{1,0},{2,3},{3,2},{4,5},{5,4},{6,7},{7,6},{8,9},{9,8},{10,11... | collective-permute-start | bytes 12582920 | tf_op jit(solution)/shard_map/ppermute | solution.py:331
  679.2 58.0 %collective-permute-start.40 = (bf16[2048,256]{1,0:T(8,128)(2,1)}, bf16[2048,256]{1,0:T(8,128)(2,1)}, u32[]{:S(2)}, u32[]{:S(2)}) collective-permute-start(bf16[2048,256]{1,0:T(8,128)(2,1)} %get-tuple-element.112), channel_id=1, source_target_pairs={{0,6},{1,7},{2,0},{3,1},{4,2},{5,3},{6,4},{7,5},{8,14},{9,15},{10,... | collective-permute-start | bytes 3145736 | tf_op jit(solution)/shard_map/ppermute | solution.py:328
  687.2 111.7 %collective-permute-start.17 = (bf16[2048,256]{1,0:T(8,128)(2,1)}, bf16[2048,256]{1,0:T(8,128)(2,1)}, u32[]{:S(2)}, u32[]{:S(2)}) collective-permute-start(bf16[2048,256]{1,0:T(8,128)(2,1)} %get-tuple-element.92), channel_id=1, source_target_pairs={{0,6},{1,7},{2,0},{3,1},{4,2},{5,3},{6,4},{7,5},{8,14},{9,15},{10,... | collective-permute-start | bytes 3145736 | tf_op jit(solution)/shard_map/ppermute | solution.py:328
  713.6 104.3 %collective-permute-start.41 = (bf16[2048,256]{1,0:T(8,128)(2,1)}, bf16[2048,256]{1,0:T(8,128)(2,1)}, u32[]{:S(2)}, u32[]{:S(2)}) collective-permute-start(bf16[2048,256]{1,0:T(8,128)(2,1)} %get-tuple-element.113), channel_id=1, source_target_pairs={{0,4},{1,5},{2,6},{3,7},{4,0},{5,1},{6,2},{7,3},{8,12},{9,13},{10,... | collective-permute-start | bytes 3145736 | tf_op jit(solution)/shard_map/ppermute | solution.py:328
  713.7 96.5 %collective-permute-start.18 = (bf16[2048,256]{1,0:T(8,128)(2,1)}, bf16[2048,256]{1,0:T(8,128)(2,1)}, u32[]{:S(2)}, u32[]{:S(2)}) collective-permute-start(bf16[2048,256]{1,0:T(8,128)(2,1)} %get-tuple-element.93), channel_id=1, source_target_pairs={{0,4},{1,5},{2,6},{3,7},{4,0},{5,1},{6,2},{7,3},{8,12},{9,13},{10,... | collective-permute-start | bytes 3145736 | tf_op jit(solution)/shard_map/ppermute | solution.py:328
  719.8 90.4 %collective-permute-start.19 = (bf16[2048,256]{1,0:T(8,128)(2,1)}, bf16[2048,256]{1,0:T(8,128)(2,1)}, u32[]{:S(2)}, u32[]{:S(2)}) collective-permute-start(bf16[2048,256]{1,0:T(8,128)(2,1)} %get-tuple-element.94), channel_id=1, source_target_pairs={{0,2},{1,3},{2,4},{3,5},{4,6},{5,7},{6,0},{7,1},{8,10},{9,11},{10,... | collective-permute-start | bytes 3145736 | tf_op jit(solution)/shard_map/ppermute | solution.py:328
  737.2 83.5 %collective-permute-start.42 = (bf16[2048,256]{1,0:T(8,128)(2,1)}, bf16[2048,256]{1,0:T(8,128)(2,1)}, u32[]{:S(2)}, u32[]{:S(2)}) collective-permute-start(bf16[2048,256]{1,0:T(8,128)(2,1)} %get-tuple-element.114), channel_id=1, source_target_pairs={{0,2},{1,3},{2,4},{3,5},{4,6},{5,7},{6,0},{7,1},{8,10},{9,11},{10,... | collective-permute-start | bytes 3145736 | tf_op jit(solution)/shard_map/ppermute | solution.py:328
  810.2 51.8 %collective-permute-start.59 = (bf16[2048,256]{1,0:T(8,128)(2,1)}, bf16[2048,256]{1,0:T(8,128)(2,1)}, u32[]{:S(2)}, u32[]{:S(2)}) collective-permute-start(bf16[2048,256]{1,0:T(8,128)(2,1)} %get-tuple-element.132), channel_id=1, source_target_pairs={{0,2},{1,3},{2,4},{3,5},{4,6},{5,7},{6,0},{7,1},{8,10},{9,11},{10,... | collective-permute-start | bytes 3145736 | tf_op jit(solution)/shard_map/ppermute | solution.py:328
  818.0 65.0 %collective-permute-start.26 = (bf16[2048,256]{1,0:T(8,128)(2,1)}, bf16[2048,256]{1,0:T(8,128)(2,1)S(1)}, u32[]{:S(2)}, u32[]{:S(2)}) collective-permute-start(bf16[2048,256]{1,0:T(8,128)(2,1)} %get-tuple-element.98), channel_id=1, source_target_pairs={{0,2},{1,3},{2,4},{3,5},{4,6},{5,7},{6,0},{7,1},{8,10},{9,11},{10,... | collective-permute-start | bytes 3145736 | tf_op jit(solution)/shard_map/ppermute | solution.py:328
  820.7 73.6 %collective-permute-start.27 = (bf16[2048,256]{1,0:T(8,128)(2,1)}, bf16[2048,256]{1,0:T(8,128)(2,1)S(1)}, u32[]{:S(2)}, u32[]{:S(2)}) collective-permute-start(bf16[2048,256]{1,0:T(8,128)(2,1)} %get-tuple-element.99), channel_id=1, source_target_pairs={{0,6},{1,7},{2,0},{3,1},{4,2},{5,3},{6,4},{7,5},{8,14},{9,15},{10,... | collective-permute-start | bytes 3145736 | tf_op jit(solution)/shard_map/ppermute | solution.py:328
  849.3 56.2 %collective-permute-start.28 = (bf16[2048,256]{1,0:T(8,128)(2,1)}, bf16[2048,256]{1,0:T(8,128)(2,1)}, u32[]{:S(2)}, u32[]{:S(2)}) collective-permute-start(bf16[2048,256]{1,0:T(8,128)(2,1)} %get-tuple-element.100), channel_id=1, source_target_pairs={{0,4},{1,5},{2,6},{3,7},{4,0},{5,1},{6,2},{7,3},{8,12},{9,13},{10,... | collective-permute-start | bytes 3145736 | tf_op jit(solution)/shard_map/ppermute | solution.py:328
  857.3 70.6 %collective-permute-start.43 = (bf16[2048,256]{1,0:T(8,128)(2,1)}, bf16[2048,256]{1,0:T(8,128)(2,1)}, u32[]{:S(2)}, u32[]{:S(2)}) collective-permute-start(bf16[2048,256]{1,0:T(8,128)(2,1)} %get-tuple-element.116), channel_id=1, source_target_pairs={{0,2},{1,3},{2,4},{3,5},{4,6},{5,7},{6,0},{7,1},{8,10},{9,11},{10,... | collective-permute-start | bytes 3145736 | tf_op jit(solution)/shard_map/ppermute | solution.py:328
  862.0 77.2 %collective-permute-start.44 = (bf16[2048,256]{1,0:T(8,128)(2,1)}, bf16[2048,256]{1,0:T(8,128)(2,1)}, u32[]{:S(2)}, u32[]{:S(2)}) collective-permute-start(bf16[2048,256]{1,0:T(8,128)(2,1)} %get-tuple-element.117), channel_id=1, source_target_pairs={{0,6},{1,7},{2,0},{3,1},{4,2},{5,3},{6,4},{7,5},{8,14},{9,15},{10,... | collective-permute-start | bytes 3145736 | tf_op jit(solution)/shard_map/ppermute | solution.py:328
  882.9 67.4 %collective-permute-start.45 = (bf16[2048,256]{1,0:T(8,128)(2,1)}, bf16[2048,256]{1,0:T(8,128)(2,1)S(1)}, u32[]{:S(2)}, u32[]{:S(2)}) collective-permute-start(bf16[2048,256]{1,0:T(8,128)(2,1)} %get-tuple-element.118), channel_id=1, source_target_pairs={{0,4},{1,5},{2,6},{3,7},{4,0},{5,1},{6,2},{7,3},{8,12},{9,13},{10,... | collective-permute-start | bytes 3145736 | tf_op jit(solution)/shard_map/ppermute | solution.py:328
  894.2 78.5 %collective-permute-start.60 = (bf16[2048,256]{1,0:T(8,128)(2,1)}, bf16[2048,256]{1,0:T(8,128)(2,1)S(1)}, u32[]{:S(2)}, u32[]{:S(2)}) collective-permute-start(bf16[2048,256]{1,0:T(8,128)(2,1)} %get-tuple-element.134), channel_id=1, source_target_pairs={{0,2},{1,3},{2,4},{3,5},{4,6},{5,7},{6,0},{7,1},{8,10},{9,11},{10,... | collective-permute-start | bytes 3145736 | tf_op jit(solution)/shard_map/ppermute | solution.py:328
  905.5 78.6 %collective-permute-start.61 = (bf16[2048,256]{1,0:T(8,128)(2,1)}, bf16[2048,256]{1,0:T(8,128)(2,1)S(1)}, u32[]{:S(2)}, u32[]{:S(2)}) collective-permute-start(bf16[2048,256]{1,0:T(8,128)(2,1)} %get-tuple-element.135), channel_id=1, source_target_pairs={{0,6},{1,7},{2,0},{3,1},{4,2},{5,3},{6,4},{7,5},{8,14},{9,15},{10,... | collective-permute-start | bytes 3145736 | tf_op jit(solution)/shard_map/ppermute | solution.py:328
  928.0 67.4 %collective-permute-start.62 = (bf16[2048,256]{1,0:T(8,128)(2,1)}, bf16[2048,256]{1,0:T(8,128)(2,1)S(1)}, u32[]{:S(2)}, u32[]{:S(2)}) collective-permute-start(bf16[2048,256]{1,0:T(8,128)(2,1)} %get-tuple-element.136), channel_id=1, source_target_pairs={{0,4},{1,5},{2,6},{3,7},{4,0},{5,1},{6,2},{7,3},{8,12},{9,13},{10,... | collective-permute-start | bytes 3145736 | tf_op jit(solution)/shard_map/ppermute | solution.py:328
  939.2 78.2 %collective-permute-start.77 = (bf16[2048,256]{1,0:T(8,128)(2,1)}, bf16[2048,256]{1,0:T(8,128)(2,1)S(1)}, u32[]{:S(2)}, u32[]{:S(2)}) collective-permute-start(bf16[2048,256]{1,0:T(8,128)(2,1)} %get-tuple-element.152), channel_id=1, source_target_pairs={{0,2},{1,3},{2,4},{3,5},{4,6},{5,7},{6,0},{7,1},{8,10},{9,11},{10,... | collective-permute-start | bytes 3145736 | tf_op jit(solution)/shard_map/ppermute | solution.py:328
  950.4 68.1 %collective-permute-start.78 = (bf16[2048,256]{1,0:T(8,128)(2,1)}, bf16[2048,256]{1,0:T(8,128)(2,1)S(1)}, u32[]{:S(2)}, u32[]{:S(2)}) collective-permute-start(bf16[2048,256]{1,0:T(8,128)(2,1)} %get-tuple-element.153), channel_id=1, source_target_pairs={{0,6},{1,7},{2,0},{3,1},{4,2},{5,3},{6,4},{7,5},{8,14},{9,15},{10,... | collective-permute-start | bytes 3145736 | tf_op jit(solution)/shard_map/ppermute | solution.py:328
  972.8 54.2 %collective-permute-start.79 = (bf16[1024,256]{1,0:T(8,128)(2,1)S(1)}, bf16[1024,256]{1,0:T(8,128)(2,1)S(1)}, u32[]{:S(2)}, u32[]{:S(2)}) collective-permute-start(bf16[1024,256]{1,0:T(8,128)(2,1)S(1)} %copy-done.18), channel_id=1, source_target_pairs={{0,4},{1,5},{2,6},{3,7},{4,0},{5,1},{6,2},{7,3},{8,12},{9,13},{10,... | collective-permute-start | bytes 1572872 | tf_op jit(solution)/shard_map/ppermute | solution.py:328
  (54 other events, 2015.9 us)
